TPU v7x, 256 devices: a 4x2x16 block of a 4x16x16 slice. The times are simulated.
256 devices in a mesh: groups: 2 (over y), row: 16 (over z), col: 4 (over x), sub: 2 (over core).
Axes of the slice: x: 4, y: 2, z: 16, core: 2. Of those that a mesh axis runs over, the one named last changes fastest.
The devices are a block of a 4x16x16 slice.
Arguments:
- saved_alignment: bfloat16 [64, 1024, 256], P(('col', 'sub'), ('groups', 'row')), parts along dimension 1, may hold values from -6 to 6
- homolog_existence: int32 [64, 1024], P(('col', 'sub'), ('groups', 'row')), parts along dimension 1, may hold values 0 or 1
- amino_existence: int32 [1024], P(('groups', 'row')), parts along dimension 0, may hold values 0 or 1
- couple_delta_adjoint: bfloat16 [1024, 512, 128], P(('groups', 'row'), ('col', 'sub')), parts along dimension 0, may hold values from -1.5 to 1.5
- feedforward_adjoint: bfloat16 [64, 1024, 256], P(('col', 'sub'), ('groups', 'row')), parts along dimension 1, may hold values from -1.5 to 1.5
- feedforward_scale: float32 [256], replicated, may hold values from 0.1 to 1.9
- expansion_matrix: bfloat16 [256, 1024], replicated, may hold values from -0.375 to 0.375
- contraction_matrix: bfloat16 [1024, 256], replicated, may hold values from -0.1875 to 0.1875
- product_scale_vector: float32 [256], replicated, may hold values from 0.1 to 1.9
- twin_operand_matrix: bfloat16 [256, 64], replicated, may hold values from -0.375 to 0.375
- couple_projection_matrix: bfloat16 [1024, 128], replicated, may hold values from -0.1875 to 0.1875
Outputs:
- alignment_start_adjoint: bfloat16 [64, 1024, 256], P(('col', 'sub'), ('groups', 'row')), parts along dimension 1
- grad_out_weight: float32 [2048, 128], P('groups'), parts along dimension 0
- grad_factor_weight: float32 [512, 64], P('groups'), parts along dimension 0
- grad_w_in: float32 [512, 1024], P('groups'), parts along dimension 0
- grad_w_mid: float32 [2048, 256], P('groups'), parts along dimension 0
- feedforward_scale_adjoint: float32 [512], P('groups'), parts along dimension 0
- product_scale_adjoint: float32 [512], P('groups'), parts along dimension 0
There are 2 independent parts, one for each index of `groups`. A program takes and returns all parts, laid end to end along the dimension named above; an argument that names none is the same for every part. Nothing has to cross between parts.
All inputs are finite; a program needn't handle non-finite values. No bound on the sum of `homolog_existence` or of `amino_existence` on one device may be relied on, other than what follows from the above.
Results may differ from a plain program's by a relative error of at most 0.015.
Values may be sent and summed in bfloat16 or wider, within the bound.
No kernel may reach another device: no remote copies, remote signals or barrier semaphores. Data moves between devices by JAX's collectives and lax.ppermute only.
A program may use at most 64 MiB of HBM per device.

v0:
```python
import math

import jax
import jax.numpy as jnp
from jax import lax
from jax.sharding import PartitionSpec as P

epsilon = 1e-05


def in_one_piece(arrays, axis, dim, along):
    ends, at = ([], 0)
    for a in arrays[:-1]:
        at += a.shape[along]
        ends.append(at)
    both = jnp.concatenate(arrays, axis=along)
    return tuple(jnp.split(lax.all_gather(both, axis, axis=dim, tiled=True), ends, axis=along))


def joined_along(parts, dim):
    parts = jnp.moveaxis(parts, 0, dim)
    lengths = parts.shape
    return parts.reshape(*lengths[:dim], lengths[dim] * lengths[dim + 1], *lengths[dim + 2 :])


def one_gather(arrays, axis, dims):
    vector = jnp.concatenate([a.reshape(-1) for a in arrays])
    lines, at, done = (lax.all_gather(vector, axis), 0, [])
    for a, dim in zip(arrays, dims):
        parts = lines[:, at : at + a.size].reshape(-1, *a.shape)
        done.append(joined_along(parts, dim))
        at += a.size
    return tuple(done)


def split_up(shard, dim, devices):
    lengths = shard.shape
    parts = shard.reshape(*lengths[:dim], devices, lengths[dim] // devices, *lengths[dim + 1 :])
    return jnp.moveaxis(parts, dim, 0)


def sent_and_summed(shard, axis, dim):
    parts = split_up(shard, dim, lax.axis_size(axis))
    arrived = lax.all_to_all(parts, axis, split_axis=0, concat_axis=0, tiled=True)
    return arrived.astype(jnp.float32).sum(axis=0)


def layer_normalize(values):
    centre = jnp.mean(values, axis=-1, keepdims=True)
    centred = values - centre
    variance = jnp.mean(centred * centred, axis=-1, keepdims=True)
    inv_std = lax.rsqrt(variance + epsilon)
    return (centred * inv_std, inv_std)


def standardizer_adjoint(grad_hat, normed, inv_std):
    first_mean = jnp.mean(grad_hat, axis=-1, keepdims=True)
    second_mean = jnp.mean(grad_hat * normed, axis=-1, keepdims=True)
    return inv_std * (grad_hat - first_mean - normed * second_mean)


def exact_gelu(values):
    return jax.nn.gelu(values, approximate=False)


def contract_rows(first_arr, second_arr):
    return lax.dot_general(
        first_arr, second_arr, (((0,), (0,)), ((), ())), preferred_element_type=jnp.float32
    )


def contract_last(first_arr, second_arr):
    return lax.dot_general(
        first_arr, second_arr, (((1,), (1,)), ((), ())), preferred_element_type=jnp.float32
    )


def per_device(
    saved_alignment,
    homolog_existence,
    amino_existence,
    couple_delta_adjoint,
    feedforward_adjoint,
    feedforward_scale,
    expansion_matrix,
    contraction_matrix,
    product_scale_vector,
    twin_operand_matrix,
    couple_projection_matrix,
):
    homolog_split_total, amino_split_total, lane_breadth = saved_alignment.shape
    factor = twin_operand_matrix.shape[1] // 2
    pair_width = couple_projection_matrix.shape[1]
    existing_record_lines = homolog_split_total * amino_split_total
    shard_count = lax.axis_size(("col", "sub"))
    row_devices = lax.axis_size("row")
    total_res = amino_split_total * row_devices
    col_res = total_res // shard_count
    all_seqs = homolog_split_total * shard_count
    embedding_numbers = saved_alignment.astype(jnp.float32).reshape(
        existing_record_lines, lane_breadth
    )
    transition_standardized, transition_inv_deviation = layer_normalize(embedding_numbers)
    normalized_input = (transition_standardized * feedforward_scale).astype(jnp.bfloat16)
    hidden_pre = jnp.dot(normalized_input, expansion_matrix, preferred_element_type=jnp.float32)
    gelu_value, gelu_back = jax.vjp(exact_gelu, hidden_pre)
    hidden = gelu_value.astype(jnp.bfloat16)
    mixed_values = embedding_numbers + jnp.dot(
        hidden, contraction_matrix, preferred_element_type=jnp.float32
    )
    product_zscored, product_reciprocal_spread = layer_normalize(mixed_values)
    normalized_output = (product_zscored * product_scale_vector).astype(jnp.bfloat16)
    projected = jnp.dot(normalized_output, twin_operand_matrix, preferred_element_type=jnp.float32)
    keep_mask = (homolog_existence * amino_existence[None, :]).astype(jnp.float32)
    keep_col = keep_mask.reshape(existing_record_lines, 1)
    left_factor = (
        (projected[:, :factor] * keep_col)
        .astype(jnp.bfloat16)
        .reshape(homolog_split_total, amino_split_total * factor)
    )
    right_factor = (
        (projected[:, factor:] * keep_col)
        .astype(jnp.bfloat16)
        .reshape(homolog_split_total, amino_split_total * factor)
    )
    keep_half = keep_mask.astype(jnp.bfloat16)
    left_all, keep_rows = in_one_piece((left_factor, keep_half), ("col", "sub"), 0, 1)
    right_spread, keep_spread = one_gather((right_factor, keep_half), "row", (1, 1))
    right_flat, keep_cols = (
        lax.all_to_all(right_spread, ("col", "sub"), split_axis=1, concat_axis=0, tiled=True),
        lax.all_to_all(keep_spread, ("col", "sub"), split_axis=1, concat_axis=0, tiled=True),
    )
    right_cols = right_flat.reshape(all_seqs, col_res, factor)
    left_rows = left_all.reshape(all_seqs, amino_split_total, factor)
    pair_count = contract_rows(keep_rows, keep_cols)
    inverse = 1.0 / jnp.maximum(pair_count, 1.0)
    block_rows = math.gcd(amino_split_total, 16)
    result_adjoint = jnp.zeros((factor * factor, pair_width), jnp.float32)
    grad_right = jnp.zeros((all_seqs, col_res, factor), jnp.float32)
    left_parts = []
    for row_start in range(0, amino_split_total, block_rows):
        left_block = left_rows[:, row_start : row_start + block_rows, :]
        inv_block = inverse[row_start : row_start + block_rows]
        cot_block = couple_delta_adjoint[row_start : row_start + block_rows]
        outer_sum = jnp.einsum(
            "sip,sjq->ijpq", left_block, right_cols, preferred_element_type=jnp.float32
        )
        outer_half = (outer_sum * inv_block[:, :, None, None]).astype(jnp.bfloat16)
        outer_half = outer_half.reshape(block_rows, col_res, factor * factor)
        result_adjoint = result_adjoint + jnp.einsum(
            "ijk,ijl->kl", outer_half, cot_block, preferred_element_type=jnp.float32
        )
        pair_back = jnp.einsum(
            "ijl,kl->ijk", cot_block, couple_projection_matrix, preferred_element_type=jnp.float32
        )
        back_half = (pair_back * inv_block[:, :, None]).astype(jnp.bfloat16)
        back_half = back_half.reshape(block_rows, col_res, factor, factor)
        left_parts.append(
            jnp.einsum("ijpq,sjq->sip", back_half, right_cols, preferred_element_type=jnp.float32)
        )
        grad_right = grad_right + jnp.einsum(
            "ijpq,sip->sjq", back_half, left_block, preferred_element_type=jnp.float32
        )
    grad_left = jnp.concatenate(left_parts, axis=1).reshape(all_seqs, amino_split_total * factor)
    left_own = sent_and_summed(grad_left.astype(jnp.bfloat16), ("col", "sub"), 0)
    right_back = lax.all_to_all(
        grad_right.reshape(all_seqs, col_res * factor).astype(jnp.bfloat16),
        ("col", "sub"),
        split_axis=0,
        concat_axis=1,
        tiled=True,
    )
    right_own = sent_and_summed(right_back, "row", 1)
    grad_proj = jnp.concatenate(
        [
            left_own.reshape(existing_record_lines, factor),
            right_own.reshape(existing_record_lines, factor),
        ],
        axis=1,
    )
    grad_proj = (grad_proj * keep_col).astype(jnp.bfloat16)
    operand_adjoint = contract_rows(normalized_output, grad_proj)
    rescaled_result_adjoint = contract_last(grad_proj, twin_operand_matrix)
    product_scale_adjoint = jnp.sum(rescaled_result_adjoint * product_zscored, axis=0)
    combined_adjoint = feedforward_adjoint.astype(jnp.float32).reshape(
        existing_record_lines, lane_breadth
    ) + standardizer_adjoint(
        rescaled_result_adjoint * product_scale_vector, product_zscored, product_reciprocal_spread
    )
    grad_mixed_half = combined_adjoint.astype(jnp.bfloat16)
    hidden_adjoint = contract_rows(hidden, grad_mixed_half)
    grad_hidden = contract_last(grad_mixed_half, contraction_matrix)
    grad_pre = gelu_back(grad_hidden)[0].astype(jnp.bfloat16)
    expansion_adjoint = contract_rows(normalized_input, grad_pre)
    normed_input_gradient = contract_last(grad_pre, expansion_matrix)
    feedforward_scale_adjoint = jnp.sum(normed_input_gradient * transition_standardized, axis=0)
    alignment_start_adjoint = combined_adjoint + standardizer_adjoint(
        normed_input_gradient * feedforward_scale, transition_standardized, transition_inv_deviation
    )
    weight_grads = lax.psum(
        (
            result_adjoint,
            operand_adjoint,
            expansion_adjoint,
            hidden_adjoint,
            feedforward_scale_adjoint,
            product_scale_adjoint,
        ),
        ("row", "col", "sub"),
    )
    return (
        alignment_start_adjoint.astype(jnp.bfloat16).reshape(
            homolog_split_total, amino_split_total, lane_breadth
        ),
        weight_grads[0],
        weight_grads[1],
        weight_grads[2],
        weight_grads[3],
        weight_grads[4],
        weight_grads[5],
    )


def solution(mesh):
    return jax.shard_map(
        per_device,
        mesh=mesh,
        in_specs=(
            P(("col", "sub"), ("groups", "row"), None),
            P(("col", "sub"), ("groups", "row")),
            P(("groups", "row")),
            P(("groups", "row"), ("col", "sub"), None),
            P(("col", "sub"), ("groups", "row"), None),
            P(),
            P(),
            P(),
            P(),
            P(),
            P(),
        ),
        out_specs=(
            P(("col", "sub"), ("groups", "row"), None),
            P("groups", None),
            P("groups", None),
            P("groups", None),
            P("groups", None),
            P("groups"),
            P("groups"),
        ),
        check_vma=False,
    )
```

profile of v0, /device:TPU:33, one launch (start us, length us, event | category | flops | bytes accessed | tf_op | source)
XLA Modules:
  0.0 527.1 jit_solution(18394093957308587515)
XLA Ops:
  11.5 3.4 multiply_convert_fusion.2
  17.4 45.3 %all-gather.1 = bf16[16,1,8448]{2,1,0:T(2,128)(2,1)S(1)} all-gather(bf16[1,1,8448]{2,1,0:T(2,128)(2,1)S(1)} %reshape.176), channel_id=2, replica_groups=mesh['groups'=2,'row'=16,'col'=4,'sub'=2] {'row'}, dimensions={0}, use_global_device_ids=true | all-gather | bytes 287232 | tf_op jit(solution)/shard_map/all_gather | solution.py:28
  63.6 12.2 %all-to-all-start.1 = ((bf16[8,2,256]{2,1,0:T(2,128)(2,1)}), bf16[8,2,256]{2,1,0:T(2,128)(2,1)S(1)}, u32[]{:S(2)}, u32[]{:S(2)}) async-start(bf16[8,2,256]{2,1,0:T(2,128)(2,1)} %reshape.192), calls=%async_computation.1 | async-start | bytes 16384 | tf_op jit(solution)/shard_map/all_to_all | solution.py:131
  76.1 13.7 %all_gather.11 = bf16[64,1056]{1,0:T(8,128)(2,1)S(1)} all-gather(bf16[8,1056]{1,0:T(8,128)(2,1)S(1)} %pad_maximum_fusion.2), channel_id=1, replica_groups=mesh['groups'=2,'row'=16,'col'=4,'sub'=2] {'col','sub'}, dimensions={0}, use_global_device_ids=true | all-gather | bytes 152064 | tf_op jit(solution)/shard_map/all_gather | solution.py:17
  90.9 4.1 all-to-all-start
  95.3 1.7 multiply_convert_fusion
  97.1 3.2 copy.56
  100.3 1.7 multiply_convert_fusion.1
  102.0 3.2 copy.53
  105.2 3.8 fusion.10
  109.0 1.5 fusion.19
  111.2 1.8 convert_element_type.80
  113.1 5.0 all-to-all-start.3
  118.1 1.9 reshape.161
  120.9 3.6 fusion.29
  124.6 1.3 fusion.32
  128.9 4.8 all-to-all-start.2
  133.7 3.2 fusion.1
  139.0 4.0 all-to-all-start.4
  145.4 2.7 copy.67
  148.2 2.7 copy.70
  151.9 1.8 fusion.22
  153.8 2.7 all-to-all-done.4
  158.2 1.3 fusion.50
  159.6 2.1 add_convert_fusion
  161.7 1.3 fusion.67
  163.6 252.7 %all-reduce = (f32[256]{0:T(256)}, f32[256]{0:T(256)}) all-reduce(f32[256]{0:T(256)S(1)} %get-tuple-element.9, f32[256]{0:T(256)S(1)} %get-tuple-element.7), channel_id=1, replica_groups=mesh['groups'=2,'row'=16,'col'=4,'sub'=2] {'row','col','sub'}, use_global_device_ids=true, to_apply=%region_15.0 | all-reduce | flops 512 | bytes 4096 | tf_op jit(solution)/shard_map/psum | solution.py:200
  417.1 95.3 %all-reduce.4.cloned.1.call-done = (f32[1024,128]{1,0:T(8,128)}, f32[256,64]{0,1:T(8,128)}, f32[256,1024]{1,0:T(8,128)}, f32[1024,256]{1,0:T(8,128)}) async-done(((f32[1024,128]{1,0:T(8,128)}, f32[256,64]{0,1:T(8,128)}, f32[256,1024]{1,0:T(8,128)}, f32[1024,256]{1,0:T(8,128)}), (f32[1024,128]{1,0:T(8,128)}, f32[256,64]{0,1:T(8,128)}, f32[256,1024]{1,0:T(8,128)}, ...) | async-done | bytes 2686992 | tf_op jit(solution)/shard_map/psum | solution.py:200
  512.4 1.9 copy.122
  514.2 1.5 copy.123
  515.7 2.3 copy.124
  518.0 2.3 copy.125
  (122 shorter events, 22.6 us)
Async XLA Ops:
  7.2 4.3 copy-start
  8.4 6.6 %copy-start.17 = (f32[256]{0:T(256)}, f32[256]{0:T(256)S(1)}, u32[]{:S(2)}) copy-start(f32[256]{0:T(256)S(1)} %div.30) | copy-start | bytes 3076
  9.5 5.4 %copy-start.19 = (f32[256]{0:T(256)}, f32[256]{0:T(256)S(1)}, u32[]{:S(2)}) copy-start(f32[256]{0:T(256)S(1)} %rsqrt.20) | copy-start | bytes 3076
  10.3 6.7 %copy-start.21 = (f32[256]{0:T(256)}, f32[256]{0:T(256)S(1)}, u32[]{:S(2)}) copy-start(f32[256]{0:T(256)S(1)} %mul.200) | copy-start | bytes 3076
  11.5 4.3 copy-start.4
  11.5 4.3 copy-start.8
  11.5 5.3 copy-start.23
  11.5 5.4 %copy-start.10 = (bf16[256,64]{0,1:T(8,128)(2,1)S(1)}, bf16[256,64]{0,1:T(8,128)(2,1)}, u32[]{:S(2)}) copy-start(bf16[256,64]{0,1:T(8,128)(2,1)} %param.20) | copy-start | bytes 98308
  15.0 0.8 copy-start.5
  16.2 0.6 copy-start.13
  16.8 59.3 %copy-start.15 = (f32[256]{0:T(256)}, f32[256]{0:T(256)S(1)}, u32[]{:S(2)}) copy-start(f32[256]{0:T(256)S(1)} %add_rsqrt_fusion.1) | copy-start | bytes 3076
  63.6 27.3 %all-to-all-start.1 = ((bf16[8,2,256]{2,1,0:T(2,128)(2,1)}), bf16[8,2,256]{2,1,0:T(2,128)(2,1)S(1)}, u32[]{:S(2)}, u32[]{:S(2)}) async-start(bf16[8,2,256]{2,1,0:T(2,128)(2,1)} %reshape.192), calls=%async_computation.1 | async-start | bytes 16384 | tf_op jit(solution)/shard_map/all_to_all | solution.py:131
  90.9 22.1 %all-to-all-start = ((bf16[8,8,2048]{2,0,1:T(8,128)(2,1)}), bf16[8,8,2048]{2,0,1:T(8,128)(2,1)}, u32[]{:S(2)}, u32[]{:S(2)}) async-start(bf16[8,8,2048]{2,0,1:T(8,128)(2,1)} %copy.49), calls=%async_computation | async-start | bytes 524288 | tf_op jit(solution)/shard_map/all_to_all | solution.py:130
  105.2 3.8 copy-start.1
  113.1 15.9 %all-to-all-start.3 = ((bf16[8,8,2048]{2,1,0:T(8,128)(2,1)}), bf16[8,8,2048]{2,1,0:T(8,128)(2,1)S(1)}, u32[]{:S(2)}, u32[]{:S(2)}) async-start(bf16[8,8,2048]{2,1,0:T(8,128)(2,1)} %convert_element_type.80), calls=%async_computation.3 | async-start | bytes 524288 | tf_op jit(solution)/shard_map/all_to_all | solution.py:166
  120.9 3.7 copy-start.2
  128.9 10.1 %all-to-all-start.2 = ((bf16[8,8,1024]{2,1,0:T(8,128)(2,1)}), bf16[8,8,1024]{2,1,0:T(8,128)(2,1)S(1)}, u32[]{:S(2)}, u32[]{:S(2)}) async-start(bf16[8,8,1024]{2,1,0:T(8,128)(2,1)} %convert_element_type.77), calls=%async_computation.2 | async-start | bytes 262144 | tf_op jit(solution)/shard_map/all_to_all | solution.py:44
  139.0 17.5 %all-to-all-start.4 = ((bf16[16,8,1024]{2,1,0:T(8,128)(2,1)}), bf16[16,8,1024]{2,1,0:T(8,128)(2,1)S(1)}, u32[]{:S(2)}, u32[]{:S(2)}) async-start(bf16[16,8,1024]{2,1,0:T(8,128)(2,1)} %copy.65), calls=%async_computation.4 | async-start | bytes 524288 | tf_op jit(solution)/shard_map/all_to_all | solution.py:44
  143.0 369.4 %all-reduce.4.cloned.1.call-start = ((), (), s32[]{:S(2)}) async-start(), calls=%async_computation.5 | async-start | bytes 5373952 | tf_op jit(solution)/shard_map/psum | solution.py:200
  143.3 2.2 copy-start.3
  148.1 2.7 copy-start.7
  151.8 4.8 copy-start.22
  151.8 5.8 %copy-start.11 = (bf16[256,64]{0,1:T(8,128)(2,1)S(1)}, bf16[256,64]{0,1:T(8,128)(2,1)}, u32[]{:S(2)}) copy-start(bf16[256,64]{0,1:T(8,128)(2,1)} %param.20) | copy-start | bytes 98308
  151.8 5.8 %copy-start.14 = (f32[256]{0:T(256)S(1)}, f32[256]{0:T(256)}, u32[]{:S(2)}) copy-start(f32[256]{0:T(256)} %copy-done.13) | copy-start | bytes 3076
  151.8 5.8 %copy-start.16 = (f32[256]{0:T(256)S(1)}, f32[256]{0:T(256)}, u32[]{:S(2)}) copy-start(f32[256]{0:T(256)} %copy-done.15) | copy-start | bytes 3076
  151.9 5.8 %copy-start.24 = (f32[256]{0:T(256)S(1)}, f32[256]{0:T(256)}, u32[]{:S(2)}) copy-start(f32[256]{0:T(256)} %param.19) | copy-start | bytes 3076
  151.9 6.1 %copy-start.12 = (bf16[8,32,256]{2,1,0:T(8,128)(2,1)S(1)}, bf16[8,32,256]{2,1,0:T(8,128)(2,1)}, u32[]{:S(2)}) copy-start(bf16[8,32,256]{2,1,0:T(8,128)(2,1)} %param.15) | copy-start | bytes 393220
  151.9 6.3 %copy-start.6 = (bf16[256,1024]{1,0:T(8,128)(2,1)S(1)}, bf16[256,1024]{1,0:T(8,128)(2,1)}, u32[]{:S(2)}) copy-start(bf16[256,1024]{1,0:T(8,128)(2,1)} %copy-done.5) | copy-start | bytes 1572868
  151.9 7.7 %copy-start.9 = (bf16[1024,256]{1,0:T(8,128)(2,1)S(1)}, bf16[1024,256]{1,0:T(8,128)(2,1)}, u32[]{:S(2)}) copy-start(bf16[1024,256]{1,0:T(8,128)(2,1)} %param.18) | copy-start | bytes 1572868
  159.5 3.5 copy-start.18
  159.5 3.5 copy-start.20
  159.5 3.5 copy-start.25
Sparse Core Ops, SparseCore 0:
  163.2 349.1 all-reduce.3
where the time goes:
time: 528 us; the launch traced here: 527 us
  blocking collectives  312 us (59%)
  waiting for transfers between devices  99 us (19%)
  local copies, waits for them, and re-layouts  34.5 us (7%)
  matrix products  31.3 us (6%)
  starting transfers between devices  30.4 us (6%)
  between operations  14.6 us (3%)
  other arithmetic  5.63 us (1%)
    psum x1, blocking collectives, per_device(): lax.psum((result_adjoint, operand_adjoint, expansion_adjoint, hidden_adjo...  253 us
    psum x1, waiting for transfers between devices, per_device(): lax.psum((result_adjoint, operand_adjoint, expansion_adjoint, hidden_adjo...  95.3 us
    all_gather x1, blocking collectives, one_gather(): lines, at, done = (lax.all_gather(vector, axis), 0, [])  45.3 us
    all_gather x1, blocking collectives, in_one_piece(): lax.all_gather(both, axis, axis=dim, tiled=True)  13.7 us
    all_to_all x1, starting transfers between devices, per_device(): lax.all_to_all(keep_spread, ('col', 'sub'), split_axis=1, concat_axis=0,...  12.2 us
    unnamed x60, local copies, waits for them, and re-layouts  11 us
  transfers between devices with their start and end apart: 6, of which 3 were waited for; matrix products, arithmetic and copies ran while one was open for 9% of the time, Pallas kernels for 0%

commit v1 on v0

v1 whole, which is shorter than its diff:
```python
import math

import jax
import jax.numpy as jnp
from jax import lax
from jax.experimental import pallas as pl
from jax.experimental.pallas import tpu as pltpu
from jax.sharding import PartitionSpec as P

epsilon = 1e-05
lanes = 128
f32 = jnp.float32
bf16 = jnp.bfloat16
INTERPRET = False


def layer_normalize(values):
    centre = jnp.mean(values, axis=-1, keepdims=True)
    centred = values - centre
    variance = jnp.mean(centred * centred, axis=-1, keepdims=True)
    inv_std = lax.rsqrt(variance + epsilon)
    return (centred * inv_std, inv_std)


def standardizer_adjoint(grad_hat, normed, inv_std):
    first_mean = jnp.mean(grad_hat, axis=-1, keepdims=True)
    second_mean = jnp.mean(grad_hat * normed, axis=-1, keepdims=True)
    return inv_std * (grad_hat - first_mean - normed * second_mean)


def plain(a, b):
    return lax.dot_general(a, b, (((1,), (0,)), ((), ())), preferred_element_type=f32)


def last_last(a, b):
    return lax.dot_general(a, b, (((1,), (1,)), ((), ())), preferred_element_type=f32)


def first_first(a, b):
    return lax.dot_general(a, b, (((0,), (0,)), ((), ())), preferred_element_type=f32)


def turn(values, shift):
    shift = shift % lanes
    return values if shift == 0 else pltpu.roll(values, shift, 1)


def lane_index(shape):
    return lax.broadcasted_iota(jnp.int32, shape, 1)


def keep_column(keep, seqs, res):
    rows = seqs * res
    wide = jnp.broadcast_to(keep[:, None, :], (seqs, res, lanes)).reshape(rows, lanes)
    residue = lax.broadcasted_iota(jnp.int32, (rows, lanes), 0) % res
    own = lane_index((rows, lanes)) == residue
    return jnp.sum(jnp.where(own, wide, 0.0), axis=1, keepdims=True)


def forward_kernel(
    x_ref, keep_ref, scale_in_ref, w_in_ref, w_mid_ref, scale_out_ref, twin_ref,
    right_ref, left_ref, normed_in_ref, hidden_ref, slope_ref, hat_in_ref, hat_out_ref,
    normed_out_ref, spread_ref, left_rows, right_rows,
):
    seqs = keep_ref.shape[0]
    rows = x_ref.shape[0]
    res = rows // seqs
    factor = twin_ref.shape[0] // 2
    group = lanes // factor
    x = x_ref[...].astype(f32)
    hat_in, inv_in = layer_normalize(x)
    hat_in_ref[...] = hat_in
    normed_in = (hat_in * scale_in_ref[...]).astype(bf16)
    normed_in_ref[...] = normed_in
    pre = plain(normed_in, w_in_ref[...])
    share = 0.5 * (1.0 + lax.erf(pre * math.sqrt(0.5)))
    hidden = (pre * share).astype(bf16)
    hidden_ref[...] = hidden
    slope_ref[...] = share + pre * (jnp.exp(-0.5 * pre * pre) * (1.0 / math.sqrt(2.0 * math.pi)))
    mixed = x + plain(hidden, w_mid_ref[...])
    hat_out, inv_out = layer_normalize(mixed)
    hat_out_ref[...] = hat_out
    lane = lane_index((rows, lanes))
    spread_ref[...] = jnp.where(lane == 0, inv_in, inv_out)
    normed_out = (hat_out * scale_out_ref[...]).astype(bf16)
    normed_out_ref[...] = normed_out
    keep = keep_ref[...]
    twin = twin_ref[...]
    projected = last_last(
        normed_out, jnp.concatenate([twin, jnp.zeros((lanes - 2 * factor, twin.shape[1]), bf16)], axis=0)
    )
    left_rows[...] = jnp.where(lane < factor, projected * keep_column(keep, seqs, res), 0.0)
    turned = last_last(twin[factor:], normed_out)
    per = lanes // res
    for s in range(seqs):
        tile = turned[:, (s // per) * lanes : (s // per + 1) * lanes]
        right_rows[s * factor : (s + 1) * factor, :] = turn(tile, -(s % per) * res)
    for t in range(res // group):
        tile = left_rows[pl.ds(t * group, seqs, stride=res), :]
        for m in range(1, group):
            tile = tile + turn(left_rows[pl.ds(t * group + m, seqs, stride=res), :], m * factor)
        left_ref[:, t * lanes : (t + 1) * lanes] = tile.astype(bf16)
    left_ref[:, res * factor :] = keep.astype(bf16)
    pieces = []
    for t in range(factor // per):
        tile = right_rows[pl.ds(t * per, seqs, stride=factor), :] * keep
        for m in range(1, per):
            piece = right_rows[pl.ds(t * per + m, seqs, stride=factor), :] * keep
            tile = tile + turn(piece, m * res)
        pieces.append(tile)
    record = jnp.concatenate(pieces + [keep], axis=1).astype(bf16)
    for c in range(right_ref.shape[0]):
        right_ref[c] = record


def pair_kernel(
    rec_ref, cot_ref, proj_ref, back_ref, grad_ref,
    left_all, right_all, outer_all, adjoint_all, pulled_all, proj_rows, proj_all,
):
    shards, parts, seqs, _ = rec_ref.shape
    blocks = parts - 1
    all_seqs = shards * seqs
    res = cot_ref.shape[0]
    cols = cot_ref.shape[1]
    wide = back_ref.shape[3]
    factor = wide // res
    pairs = lanes // cols
    sets = factor // pairs
    half = cols // blocks
    lane = lane_index((all_seqs, lanes))

    def gathered(part, t):
        return rec_ref[:, part, :, t * lanes : (t + 1) * lanes].astype(f32).reshape(all_seqs, lanes)

    for t in range(wide // lanes):
        left_all[:, t * lanes : (t + 1) * lanes] = gathered(blocks, t).astype(bf16)
        a, b = gathered(0, t), gathered(1, t)
        first = jnp.where(
            lane < 32, a, jnp.where(lane < 64, turn(b, 32), jnp.where(lane < 96, turn(a, 32), turn(b, 64)))
        )
        second = jnp.where(
            lane < 32, turn(a, 64), jnp.where(lane < 64, turn(b, 96), jnp.where(lane < 96, turn(a, 96), b))
        )
        right_all[:, 2 * t * lanes : (2 * t + 1) * lanes] = first.astype(bf16)
        right_all[:, (2 * t + 1) * lanes : (2 * t + 2) * lanes] = second.astype(bf16)
    last = wide // lanes
    keep_rows = gathered(blocks, last).astype(bf16)
    keep_cols = (gathered(0, last) + turn(gathered(1, last), half)).astype(bf16)
    count = first_first(keep_cols, keep_rows)[:cols]
    inverse = 1.0 / jnp.maximum(count, 1.0)
    nothing = jnp.zeros((cols, lanes), bf16)
    for i in range(res):
        scaled = (cot_ref[i].astype(f32) * inverse[:, i : i + 1]).astype(bf16)
        at = i * lanes
        for k in range(pairs):
            for m in range(pairs):
                adjoint_all[at + k * cols : at + (k + 1) * cols, m * lanes : (m + 1) * lanes] = (
                    scaled if k == m else nothing
                )
    proj_rows[...] = proj_ref[...].astype(f32)
    for n in range(sets):
        for k in range(pairs):
            proj_all[n * factor : (n + 1) * factor, k * lanes : (k + 1) * lanes] = proj_rows[
                pl.ds(n * pairs + k, factor, stride=factor), :
            ].astype(bf16)
    step = 256 // factor
    for c in range(res // step):
        outer = first_first(left_all[:, c * step * factor : (c + 1) * step * factor], right_all[...])
        for i in range(step):
            at = (c * step + i) * lanes
            for n in range(sets):
                outer_all[n * factor : (n + 1) * factor, at : at + lanes] = outer[
                    i * factor : (i + 1) * factor, n * lanes : (n + 1) * lanes
                ].astype(bf16)
        pulled = last_last(proj_all[...], adjoint_all[c * step * lanes : (c + 1) * step * lanes, :])
        for i in range(step):
            at = (c * step + i) * factor
            for n in range(sets):
                pulled_all[at : at + factor, n * lanes : (n + 1) * lanes] = pulled[
                    n * factor : (n + 1) * factor, i * lanes : (i + 1) * lanes
                ].astype(bf16)
    grad_ref[...] = plain(outer_all[...], adjoint_all[...])
    grad_left = last_last(right_all[...], pulled_all[...])
    grad_right = plain(left_all[...], pulled_all[...])

    def put(part, t, values):
        back_ref[:, part, :, t * lanes : (t + 1) * lanes] = values.reshape(shards, seqs, lanes).astype(bf16)

    for t in range(wide // lanes):
        put(blocks, t, grad_left[:, t * lanes : (t + 1) * lanes])
        a = grad_right[:, 2 * t * lanes : (2 * t + 1) * lanes]
        b = grad_right[:, (2 * t + 1) * lanes : (2 * t + 2) * lanes]
        put(0, t, jnp.where(
            lane < 32, a, jnp.where(lane < 64, turn(a, 96), jnp.where(lane < 96, turn(b, 64), turn(b, 32)))
        ))
        put(1, t, jnp.where(
            lane < 32, turn(a, 96), jnp.where(lane < 64, turn(a, 64), jnp.where(lane < 96, turn(b, 32), b))
        ))


def chunk_rows(rows, features, hidden, factor, pair_width, chunks):
    sizes = (
        features * hidden // chunks // lanes,
        hidden * features // chunks // lanes,
        factor * factor * pair_width // chunks // lanes,
        2 * factor * features // chunks // lanes,
    )
    starts = [0]
    for size in sizes:
        starts.append(starts[-1] + size)
    return starts


def backward_kernel(
    core_ref, left_ref, right_ref, keep_ref, cot_ref, scale_in_ref, w_in_ref, w_mid_ref, scale_out_ref,
    twin_ref, grad_ref, normed_in_ref, hidden_ref, slope_ref, hat_in_ref, hat_out_ref, normed_out_ref,
    spread_ref, out_ref, own_ref, send_ref, left_rows, right_rows, chunks_ref,
):
    seqs = keep_ref.shape[0]
    rows, features = cot_ref.shape
    res = rows // seqs
    factor = twin_ref.shape[0] // 2
    group = lanes // factor
    per = lanes // res
    cols = own_ref.shape[0]
    chunks = 2 * cols
    units = hidden_ref.shape[1]
    pair_width = lanes
    starts = chunk_rows(rows, features, units, factor, pair_width, chunks)
    keep = keep_ref[...]
    lane_small = lane_index((seqs, lanes))
    last = left_ref.shape[1] - 1
    for t in range(res // group):
        tile = jnp.sum(left_ref[:, last, :, t * lanes : (t + 1) * lanes].astype(f32), axis=0)
        for m in range(group):
            piece = jnp.where(lane_small < factor, turn(tile, -m * factor), 0.0)
            left_rows[pl.ds(t * group + m, seqs, stride=res), :] = piece
    for t in range(factor // per):
        tile = jnp.sum(right_ref[:, :, t * lanes : (t + 1) * lanes].astype(f32), axis=0)
        for m in range(per):
            right_rows[pl.ds(t * per + m, seqs, stride=factor), :] = turn(tile, -m * res) * keep
    tiles = []
    for h in range(rows // lanes):
        tile = right_rows[h * per * factor : (h * per + 1) * factor, :]
        for m in range(1, per):
            at = (h * per + m) * factor
            tile = tile + turn(right_rows[at : at + factor, :], m * res)
        tiles.append(tile)
    turned = jnp.concatenate(tiles, axis=1)
    turned = jnp.concatenate(
        [jnp.zeros((factor, rows), f32), turned, jnp.zeros((lanes - 2 * factor, rows), f32)], axis=0
    )
    grad_proj = (left_rows[...] * keep_column(keep, seqs, res) + jnp.transpose(turned)).astype(bf16)
    twin = twin_ref[...]
    twin = jnp.concatenate([twin, jnp.zeros((lanes - 2 * factor, features), bf16)], axis=0)
    operand_adjoint = first_first(grad_proj, normed_out_ref[...])
    rescaled = plain(grad_proj, twin)
    hat_out = hat_out_ref[...]
    product_adjoint = jnp.sum(rescaled * hat_out, axis=0, keepdims=True)
    inv_in = spread_ref[:, 0:1]
    inv_out = spread_ref[:, 1:2]
    combined = cot_ref[...].astype(f32) + standardizer_adjoint(
        rescaled * scale_out_ref[...], hat_out, inv_out
    )
    mixed_half = combined.astype(bf16)
    grad_hidden = last_last(mixed_half, w_mid_ref[...])
    grad_pre = (slope_ref[...] * grad_hidden).astype(bf16)
    grad_in = last_last(grad_pre, w_in_ref[...])
    hat_in = hat_in_ref[...]
    scale_adjoint = jnp.sum(grad_in * hat_in, axis=0, keepdims=True)
    out_ref[...] = (
        combined + standardizer_adjoint(grad_in * scale_in_ref[...], hat_in, inv_in)
    ).astype(bf16)
    hidden_adjoint = first_first(hidden_ref[...], mixed_half)
    expansion_adjoint = first_first(normed_in_ref[...], grad_pre)
    split = features // lanes

    def put(k, at, values):
        chunks_ref[k // cols, k % cols, at : at + values.shape[0], :] = values.astype(bf16)

    unit_step = units // chunks
    for k in range(chunks):
        put(k, starts[0], expansion_adjoint[:, k * unit_step : (k + 1) * unit_step])
        for m in range(split):
            put(k, starts[1] + m * unit_step,
                hidden_adjoint[k * unit_step : (k + 1) * unit_step, m * lanes : (m + 1) * lanes])
        height = grad_ref.shape[0] // chunks
        for m in range(grad_ref.shape[1] // lanes):
            put(k, starts[2] + m * height, grad_ref[k * height : (k + 1) * height, m * lanes : (m + 1) * lanes])
        height = 2 * factor // chunks
        tail = [
            operand_adjoint[k * height : (k + 1) * height, m * lanes : (m + 1) * lanes] for m in range(split)
        ]
        row = lax.broadcasted_iota(jnp.int32, (8, lanes), 0)
        extra = jnp.zeros((8, lanes), f32)
        if k == 0:
            for n, vector in enumerate((scale_adjoint, product_adjoint)):
                for m in range(split):
                    extra = jnp.where(row == n * split + m, vector[:, m * lanes : (m + 1) * lanes], extra)
        rest = chunks_ref.shape[2] - starts[4] - 8
        block = jnp.concatenate(tail + [extra, jnp.zeros((rest, lanes), f32)], axis=0)
        put(k, starts[3], block)
    core = core_ref[0]
    own_ref[...] = chunks_ref[core]
    send_ref[...] = chunks_ref[1 - core]


def final_kernel(
    core_ref, half_ref, other_ref, grad_ref, twin_ref, w_in_ref, w_mid_ref, scale_ref, product_ref
):
    cols = half_ref.shape[0]
    chunks = 2 * cols
    features, units = w_in_ref.shape
    factor = twin_ref.shape[0] // 2
    starts = chunk_rows(0, features, units, factor, lanes, chunks)
    split = features // lanes
    unit_step = units // chunks
    core = core_ref[0]
    height = factor * factor // 2 // chunks
    for k in range(chunks):
        mine = core == k // cols

        def read(at, size):
            return jnp.where(
                mine,
                half_ref[k % cols, at : at + size, :].astype(f32),
                other_ref[k % cols, at : at + size, :].astype(f32),
            )

        w_in_ref[:, k * unit_step : (k + 1) * unit_step] = read(starts[0], features)
        for m in range(split):
            w_mid_ref[k * unit_step : (k + 1) * unit_step, m * lanes : (m + 1) * lanes] = read(
                starts[1] + m * unit_step, unit_step
            )
        for m in range(2):
            block = read(starts[2] + m * height, height)
            for n in range(height // factor):
                q = 2 * (k * (height // factor) + n) + m
                grad_ref[pl.ds(q, factor, stride=factor), :] = block[n * factor : (n + 1) * factor]
        tall = 2 * factor // chunks
        block = read(starts[3], starts[4] - starts[3])
        for m in range(split):
            twin_ref[k * tall : (k + 1) * tall, m * lanes : (m + 1) * lanes] = block[m * tall : (m + 1) * tall]
        if k == 0:
            extra = read(starts[4], 8)
            for n, ref in enumerate((scale_ref, product_ref)):
                for m in range(split):
                    ref[:, m * lanes : (m + 1) * lanes] = extra[n * split + m : n * split + m + 1]


def call(kernel, outs, scratch, *args, scalars=0):
    specs = [pl.BlockSpec(memory_space=pltpu.SMEM)] * scalars
    specs += [pl.BlockSpec(memory_space=pltpu.VMEM)] * (len(args) - scalars)
    return pl.pallas_call(
        kernel,
        out_shape=[jax.ShapeDtypeStruct(s, d) for s, d in outs],
        in_specs=specs,
        out_specs=[pl.BlockSpec(memory_space=pltpu.VMEM)] * len(outs),
        scratch_shapes=[pltpu.VMEM(s, d) for s, d in scratch],
        interpret=INTERPRET,
    )(*args)


def exchanged(parts, axis):
    return lax.all_to_all(parts, axis, split_axis=0, concat_axis=0, tiled=True)


def copies(own, axis):
    return exchanged(jnp.broadcast_to(own, (lax.axis_size(axis),) + own.shape), axis)


def per_device(
    saved_alignment,
    homolog_existence,
    amino_existence,
    couple_delta_adjoint,
    feedforward_adjoint,
    feedforward_scale,
    expansion_matrix,
    contraction_matrix,
    product_scale_vector,
    twin_operand_matrix,
    couple_projection_matrix,
):
    seqs, res, features = saved_alignment.shape
    units = expansion_matrix.shape[1]
    factor = twin_operand_matrix.shape[1] // 2
    pair_width = couple_projection_matrix.shape[1]
    rows = seqs * res
    row_devices, cols, cores = (lax.axis_size(a) for a in ("row", "col", "sub"))
    shards = cols * cores
    blocks = row_devices // shards
    col_res = couple_delta_adjoint.shape[1]
    all_seqs = seqs * shards
    wide = res * factor
    assert (factor, res, blocks, cores, pair_width) == (32, 32, 2, 2, lanes)
    assert col_res == blocks * res and features == 2 * lanes and units == shards * lanes
    x = saved_alignment.reshape(rows, features)
    keep = jnp.pad(
        (homolog_existence * amino_existence[None, :]).astype(f32), ((0, 0), (0, lanes - res))
    )
    scale_in = feedforward_scale.reshape(1, features)
    scale_out = product_scale_vector.reshape(1, features)
    twin = twin_operand_matrix.T
    record = wide + lanes
    (right, left, normed_in, hidden, slope, hat_in, hat_out, normed_out, spread) = call(
        forward_kernel,
        [
            ((row_devices, seqs, record), bf16),
            ((seqs, record), bf16),
            ((rows, features), bf16),
            ((rows, units), bf16),
            ((rows, units), f32),
            ((rows, features), f32),
            ((rows, features), f32),
            ((rows, features), bf16),
            ((rows, lanes), f32),
        ],
        [((rows, lanes), f32), ((seqs * factor, lanes), f32)],
        x, keep, scale_in, expansion_matrix, contraction_matrix, scale_out, twin,
    )
    right = exchanged(right, "row").reshape(shards, blocks, seqs, record)
    left = jnp.broadcast_to(left, (shards, 1, seqs, record))
    records = exchanged(jnp.concatenate([right, left], axis=1), ("col", "sub"))
    pairs = lanes // col_res
    sets = factor // pairs
    back, result_adjoint = call(
        pair_kernel,
        [((shards, blocks + 1, seqs, wide), bf16), ((sets * factor, pairs * lanes), f32)],
        [
            ((all_seqs, wide), bf16),
            ((all_seqs, col_res * factor), bf16),
            ((sets * factor, res * lanes), bf16),
            ((res * lanes, pairs * lanes), bf16),
            ((res * factor, sets * lanes), bf16),
            ((factor * factor, lanes), f32),
            ((sets * factor, pairs * lanes), bf16),
        ],
        records, couple_delta_adjoint, couple_projection_matrix,
    )
    back = exchanged(back, ("col", "sub"))
    right_back = exchanged(back[:, :blocks].reshape(row_devices, seqs, wide), "row")
    core = lax.axis_index("sub").reshape(1)
    starts = chunk_rows(rows, features, units, factor, pair_width, shards)
    lines = -(-(starts[4] + 8) // (2 * row_devices)) * 2 * row_devices
    start_adjoint, own, send = call(
        backward_kernel,
        [
            ((rows, features), bf16),
            ((cols, lines, lanes), bf16),
            ((cols, lines, lanes), bf16),
        ],
        [
            ((rows, lanes), f32),
            ((seqs * factor, lanes), f32),
            ((cores, cols, lines, lanes), bf16),
        ],
        core, back, right_back, keep, feedforward_adjoint.reshape(rows, features), scale_in,
        expansion_matrix, contraction_matrix, scale_out, twin, result_adjoint, normed_in, hidden, slope,
        hat_in, hat_out, normed_out, spread,
        scalars=1,
    )
    swap = [(0, 1), (1, 0)]
    half = (own.astype(f32) + lax.ppermute(send, "sub", swap).astype(f32)).astype(bf16)
    half = exchanged(half, "col").astype(f32).sum(axis=0).astype(bf16)
    half = exchanged(half.reshape(row_devices, -1, 2, lanes), "row").astype(f32).sum(axis=0).astype(bf16)
    half = copies(half, "row").reshape(lines, lanes)
    half = copies(half, "col")
    other = lax.ppermute(half, "sub", swap)
    grads = call(
        final_kernel,
        [
            ((factor * factor, pair_width), f32),
            ((2 * factor, features), f32),
            ((features, units), f32),
            ((units, features), f32),
            ((1, features), f32),
            ((1, features), f32),
        ],
        [],
        core, half, other,
        scalars=1,
    )
    return (
        start_adjoint.reshape(seqs, res, features),
        grads[0],
        grads[1].T,
        grads[2],
        grads[3],
        grads[4].reshape(features),
        grads[5].reshape(features),
    )


def solution(mesh):
    return jax.shard_map(
        per_device,
        mesh=mesh,
        in_specs=(
            P(("col", "sub"), ("groups", "row"), None),
            P(("col", "sub"), ("groups", "row")),
            P(("groups", "row")),
            P(("groups", "row"), ("col", "sub"), None),
            P(("col", "sub"), ("groups", "row"), None),
            P(),
            P(),
            P(),
            P(),
            P(),
            P(),
        ),
        out_specs=(
            P(("col", "sub"), ("groups", "row"), None),
            P("groups", None),
            P("groups", None),
            P("groups", None),
            P("groups", None),
            P("groups"),
            P("groups"),
        ),
        check_vma=False,
    )
```

time: 528 us -> 193 us (0.37)
  blocking collectives: 312 us -> 130 us
  waiting for transfers between devices: 99 us -> 16.6 us
  matrix products: 31.3 us -> 0 us
  local copies, waits for them, and re-layouts: 34.5 us -> 3.87 us
  Pallas kernels: 0 us -> 20.1 us
  between operations: 14.6 us -> 0.68 us
  starting transfers between devices: 30.4 us -> 18.4 us
    psum x1 -> x0, blocking collectives: 253 us -> none  [per_device(): lax.psum((result_adjoint, operand_adjoint, expansion_adjoint, hidden_adjo...]
    all_to_all x0 -> x7, blocking collectives: none -> 130 us  [exchanged(): return lax.all_to_all(parts, axis, split_axis=0, concat_axis=0, tiled=True)]
    psum x1 -> x0, waiting for transfers between devices: 95.3 us -> none  [per_device(): lax.psum((result_adjoint, operand_adjoint, expansion_adjoint, hidden_adjo...]
    all_gather x2 -> x0, blocking collectives: 58.9 us -> none  [the longest x1 45.3 us: one_gather(): lines, at, done = (lax.all_gather(vector, axis), 0, [])]
    dot_general x20 -> x0, matrix products: 31.3 us -> none  [the longest x2 5.26 us: per_device(): jnp.einsum('ijpq,sip->sjq', back_half, left_block, preferred_element_type...]
    all_to_all x5 -> x1, starting transfers between devices: 30.1 us -> 6.05 us  [exchanged(): return lax.all_to_all(parts, axis, split_axis=0, concat_axis=0, tiled=True)]
    pallas_call x0 -> x4, Pallas kernels: none -> 20.1 us  [call(): pl.pallas_call(kernel, out_shape=[jax.ShapeDtypeStruct(s, d) for s, d in...]
    convert_element_type x9 -> x0, local copies, waits for them, and re-layouts: 15.8 us -> none  [the longest x2 6.37 us: per_device(): back_half = (pair_back * inv_block[:, :, None]).astype(jnp.bfloat16)]
  transfers between devices with their start and end apart: 6 -> 3, of which waited for: 3 -> 3; matrix products, arithmetic and copies ran while one was open for 9% -> 0% of each run, Pallas kernels for 0% -> 0%
where the time goes in v1:
time: 193 us; the launch traced here: 192 us
  blocking collectives  130 us (67%)
  Pallas kernels  20.1 us (10%)
  starting transfers between devices  18.4 us (10%)
  waiting for transfers between devices  16.6 us (9%)
  local copies, waits for them, and re-layouts  3.87 us (2%)
  other arithmetic  2.31 us (1%)
    all_to_all x7, blocking collectives, exchanged(): return lax.all_to_all(parts, axis, split_axis=0, concat_axis=0, tiled=True)  130 us
    pallas_call x4, Pallas kernels, call(): pl.pallas_call(kernel, out_shape=[jax.ShapeDtypeStruct(s, d) for s, d in...  20.1 us
    all_to_all x1, waiting for transfers between devices, exchanged(): return lax.all_to_all(parts, axis, split_axis=0, concat_axis=0, tiled=True)  12.9 us
    ppermute x1, starting transfers between devices, per_device(): lax.ppermute(send, 'sub', swap).astype(f32)  6.47 us
    all_to_all x1, starting transfers between devices, exchanged(): return lax.all_to_all(parts, axis, split_axis=0, concat_axis=0, tiled=True)  6.05 us
    ppermute x1, starting transfers between devices, per_device(): other = lax.ppermute(half, 'sub', swap)  5.92 us
  transfers between devices with their start and end apart: 3, of which 3 were waited for; matrix products, arithmetic and copies ran while one was open for 0% of the time, Pallas kernels for 0%

profile of v1, /device:TPU:33, one launch (start us, length us, event | category | flops | bytes accessed | tf_op | source)
XLA Modules:
  0.0 191.9 jit_solution(2397121592637325118)
XLA Ops:
  0.6 0.7 multiply_convert_fusion
  1.3 0.6 pad.4.keep_ref
  1.9 3.8 %shard_map.162 = (bf16[16,8,1152]{2,1,0:T(8,128)(2,1)}, bf16[8,1152]{1,0:T(8,128)(2,1)}, bf16[256,256]{1,0:T(8,128)(2,1)}, bf16[256,1024]{1,0:T(8,128)(2,1)}, f3...) custom-call(bf16[256,256]{1,0:T(8,128)(2,1)} %bitcast.19, ...), custom_call_target="tpu_custom_call" | custom-call | tf_op jit(solution)/shard_map/pallas_call | solution.py:354
  5.7 38.6 %all_to_all.40 = bf16[16,8,1152]{2,1,0:T(8,128)(2,1)S(1)} all-to-all(bf16[16,8,1152]{2,1,0:T(8,128)(2,1)} %get-tuple-element.27), channel_id=1, replica_groups=mesh['groups'=2,'row'=16,'col'=4,'sub'=2] {'row'}, dimensions={0} | all-to-all | bytes 589824 | tf_op jit(solution)/shard_map/all_to_all | solution.py:365
  44.3 0.7 broadcast_in_dim.10
  45.1 19.2 %all_to_all.41.rec_ref = bf16[8,3,8,1152]{3,2,1,0:T(8,128)(2,1)} all-to-all(bf16[8,3,8,1152]{3,2,1,0:T(8,128)(2,1)S(1)} %pad_maximum_fusion), channel_id=1, replica_groups=mesh['groups'=2,'row'=16,'col'=4,'sub'=2] {'col','sub'}, dimensions={0} | all-to-all | bytes 884736 | tf_op jit(solution)/shard_map/all_to_all | solution.py:365
  64.2 8.3 %shard_map.163 = (bf16[8,3,8,1024]{3,2,1,0:T(8,128)(2,1)}, f32[512,256]{1,0:T(8,128)}) custom-call(bf16[8,3,8,1152]{3,2,1,0:T(8,128)(2,1)} %all_to_all.41.rec_ref, bf16[32,64,128]{2,1,0:T(8,128)(2,1)} %cot_ref.1, bf16[1024,128]{1,0:T(8,128)(2,1)} %proj_ref.1), custom_call_target="tpu_custom_call" | custom-call | tf_op jit(solution)/shard_map/pallas_call | solution.py:354
  72.6 12.4 %all_to_all.42.left_ref = bf16[8,3,8,1024]{3,2,1,0:T(8,128)(2,1)S(1)} all-to-all(bf16[8,3,8,1024]{3,2,1,0:T(8,128)(2,1)} %get-tuple-element.29), channel_id=1, replica_groups=mesh['groups'=2,'row'=16,'col'=4,'sub'=2] {'col','sub'}, dimensions={0} | all-to-all | bytes 786432 | tf_op jit(solution)/shard_map/all_to_all | solution.py:365
  85.0 0.0 copy-start
  85.0 0.8 slice.4
  85.7 6.0 %all-to-all-start.3 = ((bf16[16,8,1024]{2,1,0:T(8,128)(2,1)}), bf16[16,8,1024]{2,1,0:T(8,128)(2,1)S(1)}, u32[]{:S(2)}, u32[]{:S(2)}) async-start(bf16[16,8,1024]{2,1,0:T(8,128)(2,1)} %bitcast.6), calls=%async_computation.3 | async-start | bytes 524288 | tf_op jit(solution)/shard_map/all_to_all | solution.py:365
  91.8 12.9 %all-to-all-done.3.right_ref = bf16[16,8,1024]{2,1,0:T(8,128)(2,1)S(1)} async-done(((bf16[16,8,1024]{2,1,0:T(8,128)(2,1)}), bf16[16,8,1024]{2,1,0:T(8,128)(2,1)S(1)}, u32[]{:S(2)}, u32[]{:S(2)}) %all-to-all-start.3) | async-done | bytes 262176 | tf_op jit(solution)/shard_map/all_to_all | solution.py:365
  104.7 0.0 copy-start.2
  104.7 0.0 copy-done
  104.7 0.7 copy-done.2
  105.4 4.8 %shard_map.164 = (bf16[256,256]{1,0:T(8,128)(2,1)}, bf16[4,672,128]{2,1,0:T(8,128)(2,1)}, bf16[4,672,128]{2,1,0:T(8,128)(2,1)}) custom-call(s32[1]{0:T(128)} %bitcast.core_ref, bf16[8,3,8,1024]{3,2,1,0:T(8,128)(2,1)} %copy-done, bf16[16,8,1024]{2,1,0:T(8,128)(2,1)} %copy-done.2, f32[8,128]{1,0:T(8,128)} %pad.4.keep_ref, bf16[256,256]{1,0:T(8,128)(2,1)} %bitcast.20, ...), custom_call_target="tpu_custom_call" | custom-call | tf_op jit(solution)/shard_map/pallas_call | solution.py:354
  110.2 6.5 %collective-permute-start = (bf16[4,672,128]{2,1,0:T(8,128)(2,1)}, bf16[4,672,128]{2,1,0:T(8,128)(2,1)S(1)}, u32[]{:S(2)}, u32[]{:S(2)}) collective-permute-start(bf16[4,672,128]{2,1,0:T(8,128)(2,1)} %get-tuple-element.40), channel_id=1, source_target_pairs={{0,1},{1,0},{2,3},{3,2},{4,5},{5,4},{6,7},{7,6},{8,9},{9,8},{10,11... | collective-permute-start | bytes 2064392 | tf_op jit(solution)/shard_map/ppermute | solution.py:464
  116.7 2.0 %collective-permute-done = bf16[4,672,128]{2,1,0:T(8,128)(2,1)S(1)} collective-permute-done((bf16[4,672,128]{2,1,0:T(8,128)(2,1)}, bf16[4,672,128]{2,1,0:T(8,128)(2,1)S(1)}, u32[]{:S(2)}, u32[]{:S(2)}) %collective-permute-start) | collective-permute-done | bytes 688160 | tf_op jit(solution)/shard_map/ppermute | solution.py:464
  118.7 1.3 add_convert_fusion
  120.0 13.3 %all_to_all.43 = bf16[4,672,128]{2,1,0:T(8,128)(2,1)S(1)} all-to-all(bf16[4,672,128]{2,1,0:T(8,128)(2,1)S(1)} %add_convert_fusion), channel_id=1, replica_groups=mesh['groups'=2,'row'=16,'col'=4,'sub'=2] {'col'}, dimensions={0} | all-to-all | bytes 1376256 | tf_op jit(solution)/shard_map/all_to_all | solution.py:365
  133.2 0.1 reduce_sum.24
  133.4 17.2 %all_to_all.44 = bf16[16,21,2,128]{3,2,1,0:T(2,128)(2,1)S(1)} all-to-all(bf16[16,21,2,128]{3,2,1,0:T(2,128)(2,1)S(1)} %bitcast.15), channel_id=1, replica_groups=mesh['groups'=2,'row'=16,'col'=4,'sub'=2] {'row'}, dimensions={0} | all-to-all | bytes 344064 | tf_op jit(solution)/shard_map/all_to_all | solution.py:365
  150.6 0.2 reduce_sum.25
  150.8 0.1 broadcast_in_dim.11
  150.9 19.0 %all_to_all.45 = bf16[16,21,2,128]{3,2,1,0:T(2,128)(2,1)S(1)} all-to-all(bf16[16,21,2,128]{3,2,1,0:T(2,128)(2,1)S(1)} %broadcast_in_dim.11), channel_id=1, replica_groups=mesh['groups'=2,'row'=16,'col'=4,'sub'=2] {'row'}, dimensions={0} | all-to-all | bytes 344064 | tf_op jit(solution)/shard_map/all_to_all | solution.py:365
  169.8 0.1 broadcast_in_dim.12
  169.9 10.2 %all_to_all.46.half_ref = bf16[4,672,128]{2,1,0:T(8,128)(2,1)S(1)} all-to-all(bf16[4,672,128]{2,1,0:T(8,128)(2,1)S(1)} %broadcast_in_dim.12), channel_id=1, replica_groups=mesh['groups'=2,'row'=16,'col'=4,'sub'=2] {'col'}, dimensions={0} | all-to-all | bytes 1376256 | tf_op jit(solution)/shard_map/all_to_all | solution.py:365
  180.2 5.9 %collective-permute-start.1 = (bf16[4,672,128]{2,1,0:T(8,128)(2,1)S(1)}, bf16[4,672,128]{2,1,0:T(8,128)(2,1)S(1)}, u32[]{:S(2)}, u32[]{:S(2)}) collective-permute-start(bf16[4,672,128]{2,1,0:T(8,128)(2,1)S(1)} %all_to_all.46.half_ref), channel_id=1, source_target_pairs={{0,1},{1,0},{2,3},{3,2},{4,5},{5,4},{6,7},{7,6},{8,9},{9,8},{10,11... | collective-permute-start | bytes 2064392 | tf_op jit(solution)/shard_map/ppermute | solution.py:469
  186.1 1.8 collective-permute-done.1.other_ref
  187.9 0.0 copy-done.1
  187.9 0.9 copy-done.3
  188.7 3.1 %shard_map.165 = (f32[1024,128]{1,0:T(8,128)}, f32[64,256]{1,0:T(8,128)}, f32[256,1024]{1,0:T(8,128)}, f32[1024,256]{1,0:T(8,128)}, f32[1,256]{1,0:T(1,128)}, /*index=5*/f32[1,256]{1,0:T(1,128)}) custom-call(s32[1]{0:T(128)} %bitcast.core_ref, bf16[4,672,128]{2,1,0:T(8,128)(2,1)} %copy-done.1, bf16[4,672,128]{2,1,0:T(8,128)(2,1)} %copy-done.3), custom_call_target="tpu_custom_call" | custom-call | tf_op jit(solution)/shard_map/pallas_call | solution.py:354
  (3 shorter events, 0.1 us)
Async XLA Ops:
  85.0 19.7 %copy-start = (bf16[8,3,8,1024]{3,2,1,0:T(8,128)(2,1)}, bf16[8,3,8,1024]{3,2,1,0:T(8,128)(2,1)S(1)}, u32[]{:S(2)}) copy-start(bf16[8,3,8,1024]{3,2,1,0:T(8,128)(2,1)S(1)} %all_to_all.42.left_ref) | copy-start | bytes 1179652
  85.7 18.9 %all-to-all-start.3 = ((bf16[16,8,1024]{2,1,0:T(8,128)(2,1)}), bf16[16,8,1024]{2,1,0:T(8,128)(2,1)S(1)}, u32[]{:S(2)}, u32[]{:S(2)}) async-start(bf16[16,8,1024]{2,1,0:T(8,128)(2,1)} %bitcast.6), calls=%async_computation.3 | async-start | bytes 524288 | tf_op jit(solution)/shard_map/all_to_all | solution.py:365
  104.7 0.7 copy-start.2
  110.2 8.5 %collective-permute-start = (bf16[4,672,128]{2,1,0:T(8,128)(2,1)}, bf16[4,672,128]{2,1,0:T(8,128)(2,1)S(1)}, u32[]{:S(2)}, u32[]{:S(2)}) collective-permute-start(bf16[4,672,128]{2,1,0:T(8,128)(2,1)} %get-tuple-element.40), channel_id=1, source_target_pairs={{0,1},{1,0},{2,3},{3,2},{4,5},{5,4},{6,7},{7,6},{8,9},{9,8},{10,11... | collective-permute-start | bytes 2064392 | tf_op jit(solution)/shard_map/ppermute | solution.py:464
  180.2 7.7 %copy-start.1 = (bf16[4,672,128]{2,1,0:T(8,128)(2,1)}, bf16[4,672,128]{2,1,0:T(8,128)(2,1)S(1)}, u32[]{:S(2)}) copy-start(bf16[4,672,128]{2,1,0:T(8,128)(2,1)S(1)} %all_to_all.46.half_ref) | copy-start | bytes 2064388
  180.2 7.7 %collective-permute-start.1 = (bf16[4,672,128]{2,1,0:T(8,128)(2,1)S(1)}, bf16[4,672,128]{2,1,0:T(8,128)(2,1)S(1)}, u32[]{:S(2)}, u32[]{:S(2)}) collective-permute-start(bf16[4,672,128]{2,1,0:T(8,128)(2,1)S(1)} %all_to_all.46.half_ref), channel_id=1, source_target_pairs={{0,1},{1,0},{2,3},{3,2},{4,5},{5,4},{6,7},{7,6},{8,9},{9,8},{10,11... | collective-permute-start | bytes 2064392 | tf_op jit(solution)/shard_map/ppermute | solution.py:469
  187.9 0.9 copy-start.3

commit v2 on v1

--- a/solution.py
+++ b/solution.py
@@ -114,27 +114,33 @@
 
 
 def pair_kernel(
-    rec_ref, cot_ref, proj_ref, back_ref, grad_ref,
+    parity_ref, rec_ref, other_ref, cot_ref, proj_ref, own_ref, send_ref, back_ref, grad_ref,
     left_all, right_all, outer_all, adjoint_all, pulled_all, proj_rows, proj_all,
 ):
-    shards, parts, seqs, _ = rec_ref.shape
-    blocks = parts - 1
+    shards, _, seqs, _ = rec_ref.shape
+    blocks = 2
+    even = parity_ref[0] == 0
     all_seqs = shards * seqs
     res = cot_ref.shape[0]
     cols = cot_ref.shape[1]
-    wide = back_ref.shape[3]
+    wide = back_ref.shape[2]
     factor = wide // res
     pairs = lanes // cols
     sets = factor // pairs
     half = cols // blocks
     lane = lane_index((all_seqs, lanes))
 
-    def gathered(part, t):
-        return rec_ref[:, part, :, t * lanes : (t + 1) * lanes].astype(f32).reshape(all_seqs, lanes)
+    def left_tile(t):
+        return rec_ref[:, 1, :, t * lanes : (t + 1) * lanes].astype(f32).reshape(all_seqs, lanes)
+
+    def right_tiles(t):
+        own = rec_ref[:, 0, :, t * lanes : (t + 1) * lanes].astype(f32).reshape(all_seqs, lanes)
+        other = other_ref[:, :, t * lanes : (t + 1) * lanes].astype(f32).reshape(all_seqs, lanes)
+        return jnp.where(even, own, other), jnp.where(even, other, own)
 
     for t in range(wide // lanes):
-        left_all[:, t * lanes : (t + 1) * lanes] = gathered(blocks, t).astype(bf16)
-        a, b = gathered(0, t), gathered(1, t)
+        left_all[:, t * lanes : (t + 1) * lanes] = left_tile(t).astype(bf16)
+        a, b = right_tiles(t)
         first = jnp.where(
             lane < 32, a, jnp.where(lane < 64, turn(b, 32), jnp.where(lane < 96, turn(a, 32), turn(b, 64)))
         )
@@ -144,8 +150,9 @@
         right_all[:, 2 * t * lanes : (2 * t + 1) * lanes] = first.astype(bf16)
         right_all[:, (2 * t + 1) * lanes : (2 * t + 2) * lanes] = second.astype(bf16)
     last = wide // lanes
-    keep_rows = gathered(blocks, last).astype(bf16)
-    keep_cols = (gathered(0, last) + turn(gathered(1, last), half)).astype(bf16)
+    keep_rows = left_tile(last).astype(bf16)
+    a, b = right_tiles(last)
+    keep_cols = (a + turn(b, half)).astype(bf16)
     count = first_first(keep_cols, keep_rows)[:cols]
     inverse = 1.0 / jnp.maximum(count, 1.0)
     nothing = jnp.zeros((cols, lanes), bf16)
@@ -183,19 +190,21 @@
     grad_left = last_last(right_all[...], pulled_all[...])
     grad_right = plain(left_all[...], pulled_all[...])
 
-    def put(part, t, values):
-        back_ref[:, part, :, t * lanes : (t + 1) * lanes] = values.reshape(shards, seqs, lanes).astype(bf16)
+    def put(ref, t, values):
+        ref[:, :, t * lanes : (t + 1) * lanes] = values.reshape(shards, seqs, lanes).astype(bf16)
 
     for t in range(wide // lanes):
-        put(blocks, t, grad_left[:, t * lanes : (t + 1) * lanes])
+        put(back_ref, t, grad_left[:, t * lanes : (t + 1) * lanes])
         a = grad_right[:, 2 * t * lanes : (2 * t + 1) * lanes]
         b = grad_right[:, (2 * t + 1) * lanes : (2 * t + 2) * lanes]
-        put(0, t, jnp.where(
+        first = jnp.where(
             lane < 32, a, jnp.where(lane < 64, turn(a, 96), jnp.where(lane < 96, turn(b, 64), turn(b, 32)))
-        ))
-        put(1, t, jnp.where(
+        )
+        second = jnp.where(
             lane < 32, turn(a, 96), jnp.where(lane < 64, turn(a, 64), jnp.where(lane < 96, turn(b, 32), b))
-        ))
+        )
+        put(own_ref, t, jnp.where(even, first, second))
+        put(send_ref, t, jnp.where(even, second, first))
 
 
 def chunk_rows(rows, features, hidden, factor, pair_width, chunks):
@@ -361,12 +370,14 @@
     )(*args)
 
 
-def exchanged(parts, axis):
-    return lax.all_to_all(parts, axis, split_axis=0, concat_axis=0, tiled=True)
-
-
-def copies(own, axis):
-    return exchanged(jnp.broadcast_to(own, (lax.axis_size(axis),) + own.shape), axis)
+def exchanged(parts, axis, groups=None):
+    return lax.all_to_all(
+        parts, axis, split_axis=0, concat_axis=0, axis_index_groups=groups, tiled=True
+    )
+
+
+def copies(own, axis, groups):
+    return exchanged(jnp.broadcast_to(own, (len(groups[0]),) + own.shape), axis, groups)
 
 
 def per_device(
@@ -406,7 +417,7 @@
     (right, left, normed_in, hidden, slope, hat_in, hat_out, normed_out, spread) = call(
         forward_kernel,
         [
-            ((row_devices, seqs, record), bf16),
+            ((row_devices // 2, seqs, record), bf16),
             ((seqs, record), bf16),
             ((rows, features), bf16),
             ((rows, units), bf16),
@@ -419,14 +430,24 @@
         [((rows, lanes), f32), ((seqs * factor, lanes), f32)],
         x, keep, scale_in, expansion_matrix, contraction_matrix, scale_out, twin,
     )
-    right = exchanged(right, "row").reshape(shards, blocks, seqs, record)
-    left = jnp.broadcast_to(left, (shards, 1, seqs, record))
-    records = exchanged(jnp.concatenate([right, left], axis=1), ("col", "sub"))
+    alike = [list(range(b, row_devices, 2)) for b in range(2)]
+    swap_rows = [(i, i ^ 1) for i in range(row_devices)]
+    parity = (lax.axis_index("row") % 2).reshape(1)
+    right = exchanged(right, "row", alike)
+    records = exchanged(
+        jnp.stack([right, jnp.broadcast_to(left, (shards, seqs, record))], axis=1), ("col", "sub")
+    )
+    other = lax.ppermute(records[:, 0], "row", swap_rows)
     pairs = lanes // col_res
     sets = factor // pairs
-    back, result_adjoint = call(
+    own, send, left, result_adjoint = call(
         pair_kernel,
-        [((shards, blocks + 1, seqs, wide), bf16), ((sets * factor, pairs * lanes), f32)],
+        [
+            ((shards, seqs, wide), bf16),
+            ((shards, seqs, wide), bf16),
+            ((shards, seqs, wide), bf16),
+            ((sets * factor, pairs * lanes), f32),
+        ],
         [
             ((all_seqs, wide), bf16),
             ((all_seqs, col_res * factor), bf16),
@@ -436,10 +457,12 @@
             ((factor * factor, lanes), f32),
             ((sets * factor, pairs * lanes), bf16),
         ],
-        records, couple_delta_adjoint, couple_projection_matrix,
-    )
-    back = exchanged(back, ("col", "sub"))
-    right_back = exchanged(back[:, :blocks].reshape(row_devices, seqs, wide), "row")
+        parity, records, other, couple_delta_adjoint, couple_projection_matrix,
+        scalars=1,
+    )
+    own = (own.astype(f32) + lax.ppermute(send, "row", swap_rows).astype(f32)).astype(bf16)
+    back = exchanged(jnp.stack([own, left], axis=1), ("col", "sub"))
+    right_back = exchanged(back[:, 0], "row", alike)
     core = lax.axis_index("sub").reshape(1)
     starts = chunk_rows(rows, features, units, factor, pair_width, shards)
     lines = -(-(starts[4] + 8) // (2 * row_devices)) * 2 * row_devices
@@ -462,10 +485,15 @@
     )
     swap = [(0, 1), (1, 0)]
     half = (own.astype(f32) + lax.ppermute(send, "sub", swap).astype(f32)).astype(bf16)
-    half = exchanged(half, "col").astype(f32).sum(axis=0).astype(bf16)
-    half = exchanged(half.reshape(row_devices, -1, 2, lanes), "row").astype(f32).sum(axis=0).astype(bf16)
-    half = copies(half, "row").reshape(lines, lanes)
-    half = copies(half, "col")
+    near = [
+        [(2 * m + b) * cols + c for c in range(cols) for b in range(2)] for m in range(row_devices // 2)
+    ]
+    half = exchanged(half.reshape(2 * cols, lines // 2, lanes), ("row", "col"), near)
+    half = half.astype(f32).sum(axis=0).astype(bf16)
+    half = exchanged(half.reshape(row_devices // 2, -1, 2, lanes), "row", alike)
+    half = half.astype(f32).sum(axis=0).astype(bf16)
+    half = copies(half, "row", alike).reshape(lines // 2, lanes)
+    half = copies(half, ("row", "col"), near).reshape(cols, lines, lanes)
     other = lax.ppermute(half, "sub", swap)
     grads = call(
         final_kernel,

time: 193 us -> 188 us (0.974)
  blocking collectives: 130 us -> 120 us
  waiting for transfers between devices: 16.6 us -> 25.6 us
  starting transfers between devices: 18.4 us -> 12.5 us
    all_to_all x7, blocking collectives: 130 us -> 120 us  [exchanged(): lax.all_to_all(parts, axis, split_axis=0, concat_axis=0, axis_index_group...]
    ppermute x0 -> x2, waiting for transfers between devices: none -> 8.81 us  [the longest x1 4.8 us: per_device(): other = lax.ppermute(records[:, 0], 'row', swap_rows)]
    ppermute x1, starting transfers between devices: 6.47 us -> 3.05 us  [per_device(): lax.ppermute(send, 'sub', swap).astype(f32)]
    all_to_all x1, starting transfers between devices: 6.05 us -> 3.58 us  [exchanged(): lax.all_to_all(parts, axis, split_axis=0, concat_axis=0, axis_index_group...]
  transfers between devices with their start and end apart: 3 -> 5, of which waited for: 3 -> 5; matrix products, arithmetic and copies ran while one was open for 0% -> 0% of each run, Pallas kernels for 0% -> 0%
where the time goes in v2:
time: 188 us; the launch traced here: 187 us
  blocking collectives  120 us (64%)
  waiting for transfers between devices  25.6 us (14%)
  Pallas kernels  20 us (11%)
  starting transfers between devices  12.5 us (7%)
  local copies, waits for them, and re-layouts  4.42 us (2%)
  other arithmetic  4.06 us (2%)
    all_to_all x7, blocking collectives, exchanged(): lax.all_to_all(parts, axis, split_axis=0, concat_axis=0, axis_index_group...  120 us
    pallas_call x4, Pallas kernels, call(): pl.pallas_call(kernel, out_shape=[jax.ShapeDtypeStruct(s, d) for s, d in...  20 us
    all_to_all x1, waiting for transfers between devices, exchanged(): lax.all_to_all(parts, axis, split_axis=0, concat_axis=0, axis_index_group...  13 us
    ppermute x1, starting transfers between devices, per_device(): other = lax.ppermute(half, 'sub', swap)  5.68 us
    ppermute x1, waiting for transfers between devices, per_device(): other = lax.ppermute(records[:, 0], 'row', swap_rows)  4.8 us
    ppermute x1, waiting for transfers between devices, per_device(): lax.ppermute(send, 'row', swap_rows).astype(f32)  4.01 us
  transfers between devices with their start and end apart: 5, of which 5 were waited for; matrix products, arithmetic and copies ran while one was open for 0% of the time, Pallas kernels for 0%

profile of v2, /device:TPU:33, one launch (start us, length us, event | category | flops | bytes accessed | tf_op | source)
XLA Modules:
  0.0 187.0 jit_solution(5628313300599730343)
XLA Ops:
  0.6 0.7 multiply_convert_fusion
  1.3 0.6 pad.4.keep_ref
  1.9 3.7 %shard_map.162 = (bf16[8,8,1152]{2,1,0:T(8,128)(2,1)}, bf16[8,1152]{1,0:T(8,128)(2,1)}, bf16[256,256]{1,0:T(8,128)(2,1)}, bf16[256,1024]{1,0:T(8,128)(2,1)}, f32...) custom-call(bf16[256,256]{1,0:T(8,128)(2,1)} %bitcast.35, ...), custom_call_target="tpu_custom_call" | custom-call | tf_op jit(solution)/shard_map/pallas_call | solution.py:363
  5.7 38.4 %all_to_all.40 = bf16[8,8,1152]{2,1,0:T(8,128)(2,1)S(1)} all-to-all(bf16[8,8,1152]{2,1,0:T(8,128)(2,1)} %get-tuple-element.29), channel_id=1, replica_groups={{0,16,32,48,64,80,96,112},{8,24,40,56,72,88,104,120},{1,17,33,49,65,81,..., dimensions={0} | all-to-all | bytes 294912 | tf_op jit(solution)/shard_map/all_to_all | solution.py:374
  44.1 0.7 stack_broadcast_in_dim.3
  44.9 15.2 %all_to_all.41.rec_ref = bf16[8,2,8,1152]{3,2,1,0:T(8,128)(2,1)S(1)} all-to-all(bf16[8,2,8,1152]{3,2,1,0:T(8,128)(2,1)S(1)} %copy.28), channel_id=1, replica_groups=mesh['groups'=2,'row'=16,'col'=4,'sub'=2] {'col','sub'}, dimensions={0} | all-to-all | bytes 589824 | tf_op jit(solution)/shard_map/all_to_all | solution.py:374
  60.1 0.1 collective-permute-start
  60.3 4.8 %collective-permute-done.other_ref = bf16[8,8,1152]{2,1,0:T(8,128)(2,1)S(1)} collective-permute-done((bf16[8,8,1152]{2,1,0:T(8,128)(2,1)S(1)}, bf16[8,8,1152]{2,1,0:T(8,128)(2,1)S(1)}, u32[]{:S(2)}, u32[]{:S(2)}) %collective-permute-start) | collective-permute-done | bytes 147488 | tf_op jit(solution)/shard_map/ppermute | solution.py:440
  65.1 0.6 copy-done.5
  65.7 8.4 %shard_map.163 = (bf16[8,8,1024]{2,1,0:T(8,128)(2,1)}, bf16[8,8,1024]{2,1,0:T(8,128)(2,1)}, bf16[8,8,1024]{2,1,0:T(8,128)(2,1)}, f32[512,256]{1,0:T(8,128)}) custom-call(s32[1]{0:T(128)} %bitcast.1.parity_ref, bf16[8,2,8,1152]{3,2,1,0:T(8,128)(2,1)} %copy-done.1, bf16[8,8,1152]{2,1,0:T(8,128)(2,1)} %copy-done.5, bf16[32,64,128]{2,1,0:T(8,128)(2,1)} %cot_ref.1, ...), custom_call_target="tpu_custom_call" | custom-call | tf_op jit(solution)/shard_map/pallas_call | solution.py:363
  74.1 4.0 %collective-permute-done.1 = bf16[8,8,1024]{2,1,0:T(8,128)(2,1)S(1)} collective-permute-done((bf16[8,8,1024]{2,1,0:T(8,128)(2,1)}, bf16[8,8,1024]{2,1,0:T(8,128)(2,1)S(1)}, u32[]{:S(2)}, u32[]{:S(2)}) %collective-permute-start.1) | collective-permute-done | bytes 131104 | tf_op jit(solution)/shard_map/ppermute | solution.py:463
  78.1 0.9 fusion
  79.1 0.9 pad_maximum_fusion.1
  80.0 11.5 %all_to_all.42.left_ref = bf16[8,2,8,1024]{3,2,1,0:T(8,128)(2,1)S(1)} all-to-all(bf16[8,2,8,1024]{3,2,1,0:T(8,128)(2,1)S(1)} %copy.30), channel_id=1, replica_groups=mesh['groups'=2,'row'=16,'col'=4,'sub'=2] {'col','sub'}, dimensions={0} | all-to-all | bytes 524288 | tf_op jit(solution)/shard_map/all_to_all | solution.py:374
  91.6 0.7 slice_bitcast_fusion.1
  92.3 3.6 %all-to-all-start.3 = ((bf16[8,8,1024]{2,1,0:T(8,128)(2,1)}), bf16[8,8,1024]{2,1,0:T(8,128)(2,1)S(1)}, u32[]{:S(2)}, u32[]{:S(2)}) async-start(bf16[8,8,1024]{2,1,0:T(8,128)(2,1)} %slice_bitcast_fusion.1), calls=%async_computation.3 | async-start | bytes 262144 | tf_op jit(solution)/shard_map/all_to_all | solution.py:374
  95.9 13.0 %all-to-all-done.3.right_ref = bf16[8,8,1024]{2,1,0:T(8,128)(2,1)S(1)} async-done(((bf16[8,8,1024]{2,1,0:T(8,128)(2,1)}), bf16[8,8,1024]{2,1,0:T(8,128)(2,1)S(1)}, u32[]{:S(2)}, u32[]{:S(2)}) %all-to-all-start.3) | async-done | bytes 131104 | tf_op jit(solution)/shard_map/all_to_all | solution.py:374
  108.9 0.6 copy-done.4
  109.5 4.7 %shard_map.164 = (bf16[256,256]{1,0:T(8,128)(2,1)}, bf16[4,672,128]{2,1,0:T(8,128)(2,1)}, bf16[4,672,128]{2,1,0:T(8,128)(2,1)}) custom-call(s32[1]{0:T(128)} %bitcast.core_ref, bf16[8,2,8,1024]{3,2,1,0:T(8,128)(2,1)} %copy-done.2, bf16[8,8,1024]{2,1,0:T(8,128)(2,1)} %copy-done.4, f32[8,128]{1,0:T(8,128)} %pad.4.keep_ref, bf16[256,256]{1,0:T(8,128)(2,1)} %bitcast.36, ...), custom_call_target="tpu_custom_call" | custom-call | tf_op jit(solution)/shard_map/pallas_call | solution.py:363
  114.3 3.1 %collective-permute-start.2 = (bf16[4,672,128]{2,1,0:T(8,128)(2,1)}, bf16[4,672,128]{2,1,0:T(8,128)(2,1)S(1)}, u32[]{:S(2)}, u32[]{:S(2)}) collective-permute-start(bf16[4,672,128]{2,1,0:T(8,128)(2,1)} %get-tuple-element.44), channel_id=1, source_target_pairs={{0,1},{1,0},{2,3},{3,2},{4,5},{5,4},{6,7},{7,6},{8,9},{9,8},{10,11... | collective-permute-start | bytes 2064392 | tf_op jit(solution)/shard_map/ppermute | solution.py:487
  117.3 2.0 %collective-permute-done.2 = bf16[4,672,128]{2,1,0:T(8,128)(2,1)S(1)} collective-permute-done((bf16[4,672,128]{2,1,0:T(8,128)(2,1)}, bf16[4,672,128]{2,1,0:T(8,128)(2,1)S(1)}, u32[]{:S(2)}, u32[]{:S(2)}) %collective-permute-start.2) | collective-permute-done | bytes 688160 | tf_op jit(solution)/shard_map/ppermute | solution.py:487
  119.3 1.3 add_convert_fusion
  120.6 13.8 %all_to_all.43 = bf16[8,336,128]{2,1,0:T(8,128)(2,1)S(1)} all-to-all(bf16[8,336,128]{2,1,0:T(8,128)(2,1)S(1)} %bitcast.29), channel_id=1, replica_groups={{0,8,2,10,4,12,6,14},{16,24,18,26,20,28,22,30},{32,40,34,42,36,44,38,46..., dimensions={0} | all-to-all | bytes 1376256 | tf_op jit(solution)/shard_map/all_to_all | solution.py:374
  134.4 0.1 reduce_sum.24
  134.5 15.0 %all_to_all.44 = bf16[8,21,2,128]{3,2,1,0:T(2,128)(2,1)S(1)} all-to-all(bf16[8,21,2,128]{3,2,1,0:T(2,128)(2,1)S(1)} %bitcast.32), channel_id=1, replica_groups={{0,16,32,48,64,80,96,112},{8,24,40,56,72,88,104,120},{1,17,33,49,65,81,..., dimensions={0} | all-to-all | bytes 172032 | tf_op jit(solution)/shard_map/all_to_all | solution.py:374
  149.6 14.9 %all_to_all.45 = bf16[8,21,2,128]{3,2,1,0:T(2,128)(2,1)S(1)} all-to-all(bf16[8,21,2,128]{3,2,1,0:T(2,128)(2,1)S(1)} %broadcast_in_dim.7), channel_id=1, replica_groups={{0,16,32,48,64,80,96,112},{8,24,40,56,72,88,104,120},{1,17,33,49,65,81,..., dimensions={0} | all-to-all | bytes 172032 | tf_op jit(solution)/shard_map/all_to_all | solution.py:374
  164.5 0.1 broadcast_in_dim.8
  164.5 11.0 %all_to_all.46 = bf16[8,336,128]{2,1,0:T(8,128)(2,1)S(1)} all-to-all(bf16[8,336,128]{2,1,0:T(8,128)(2,1)S(1)} %broadcast_in_dim.8), channel_id=1, replica_groups={{0,8,2,10,4,12,6,14},{16,24,18,26,20,28,22,30},{32,40,34,42,36,44,38,46..., dimensions={0} | all-to-all | bytes 1376256 | tf_op jit(solution)/shard_map/all_to_all | solution.py:374
  175.5 5.7 %collective-permute-start.3 = (bf16[4,672,128]{2,1,0:T(8,128)(2,1)S(1)}, bf16[4,672,128]{2,1,0:T(8,128)(2,1)S(1)}, u32[]{:S(2)}, u32[]{:S(2)}) collective-permute-start(bf16[4,672,128]{2,1,0:T(8,128)(2,1)S(1)} %bitcast.27), channel_id=1, source_target_pairs={{0,1},{1,0},{2,3},{3,2},{4,5},{5,4},{6,7},{7,6},{8,9},{9,8},{10,11... | collective-permute-start | bytes 2064392 | tf_op jit(solution)/shard_map/ppermute | solution.py:497
  181.2 1.8 collective-permute-done.3.other_ref
  183.0 0.9 copy-done.3
  183.8 3.1 %shard_map.165 = (f32[1024,128]{1,0:T(8,128)}, f32[64,256]{1,0:T(8,128)}, f32[256,1024]{1,0:T(8,128)}, f32[1024,256]{1,0:T(8,128)}, f32[1,256]{1,0:T(1,128)}, /*index=5*/f32[1,256]{1,0:T(1,128)}) custom-call(s32[1]{0:T(128)} %bitcast.core_ref, bf16[4,672,128]{2,1,0:T(8,128)(2,1)} %bitcast.28, bf16[4,672,128]{2,1,0:T(8,128)(2,1)} %copy-done.3), custom_call_target="tpu_custom_call" | custom-call | tf_op jit(solution)/shard_map/pallas_call | solution.py:363
  (16 shorter events, 0.3 us)
Async XLA Ops:
  60.1 5.0 %copy-start.1 = (bf16[8,2,8,1152]{3,2,1,0:T(8,128)(2,1)}, bf16[8,2,8,1152]{3,2,1,0:T(8,128)(2,1)S(1)}, u32[]{:S(2)}) copy-start(bf16[8,2,8,1152]{3,2,1,0:T(8,128)(2,1)S(1)} %all_to_all.41.rec_ref) | copy-start | bytes 884740
  60.1 5.0 %collective-permute-start = (bf16[8,8,1152]{2,1,0:T(8,128)(2,1)S(1)}, bf16[8,8,1152]{2,1,0:T(8,128)(2,1)S(1)}, u32[]{:S(2)}, u32[]{:S(2)}) collective-permute-start(bf16[8,8,1152]{2,1,0:T(8,128)(2,1)S(1)} %slice_bitcast_fusion), channel_id=1, source_target_pairs={{0,8},{8,0},{16,24},{24,16},{32,40},{40,32},{48,56},{56,48},{64,72... | collective-permute-start | bytes 442376 | tf_op jit(solution)/shard_map/ppermute | solution.py:440
  65.1 0.7 copy-start.5
  74.1 4.0 %collective-permute-start.1 = (bf16[8,8,1024]{2,1,0:T(8,128)(2,1)}, bf16[8,8,1024]{2,1,0:T(8,128)(2,1)S(1)}, u32[]{:S(2)}, u32[]{:S(2)}) collective-permute-start(bf16[8,8,1024]{2,1,0:T(8,128)(2,1)} %get-tuple-element.32), channel_id=1, source_target_pairs={{0,8},{8,0},{16,24},{24,16},{32,40},{40,32},{48,56},{56,48},{64,72... | collective-permute-start | bytes 393224 | tf_op jit(solution)/shard_map/ppermute | solution.py:463
  91.6 17.3 %copy-start.2 = (bf16[8,2,8,1024]{3,2,1,0:T(8,128)(2,1)}, bf16[8,2,8,1024]{3,2,1,0:T(8,128)(2,1)S(1)}, u32[]{:S(2)}) copy-start(bf16[8,2,8,1024]{3,2,1,0:T(8,128)(2,1)S(1)} %all_to_all.42.left_ref) | copy-start | bytes 786436
  92.3 16.6 %all-to-all-start.3 = ((bf16[8,8,1024]{2,1,0:T(8,128)(2,1)}), bf16[8,8,1024]{2,1,0:T(8,128)(2,1)S(1)}, u32[]{:S(2)}, u32[]{:S(2)}) async-start(bf16[8,8,1024]{2,1,0:T(8,128)(2,1)} %slice_bitcast_fusion.1), calls=%async_computation.3 | async-start | bytes 262144 | tf_op jit(solution)/shard_map/all_to_all | solution.py:374
  108.9 0.6 copy-start.4
  114.3 5.0 %collective-permute-start.2 = (bf16[4,672,128]{2,1,0:T(8,128)(2,1)}, bf16[4,672,128]{2,1,0:T(8,128)(2,1)S(1)}, u32[]{:S(2)}, u32[]{:S(2)}) collective-permute-start(bf16[4,672,128]{2,1,0:T(8,128)(2,1)} %get-tuple-element.44), channel_id=1, source_target_pairs={{0,1},{1,0},{2,3},{3,2},{4,5},{5,4},{6,7},{7,6},{8,9},{9,8},{10,11... | collective-permute-start | bytes 2064392 | tf_op jit(solution)/shard_map/ppermute | solution.py:487
  175.5 7.5 %copy-start = (bf16[8,336,128]{2,1,0:T(8,128)(2,1)}, bf16[8,336,128]{2,1,0:T(8,128)(2,1)S(1)}, u32[]{:S(2)}) copy-start(bf16[8,336,128]{2,1,0:T(8,128)(2,1)S(1)} %all_to_all.46) | copy-start | bytes 2064388
  175.5 7.4 %collective-permute-start.3 = (bf16[4,672,128]{2,1,0:T(8,128)(2,1)S(1)}, bf16[4,672,128]{2,1,0:T(8,128)(2,1)S(1)}, u32[]{:S(2)}, u32[]{:S(2)}) collective-permute-start(bf16[4,672,128]{2,1,0:T(8,128)(2,1)S(1)} %bitcast.27), channel_id=1, source_target_pairs={{0,1},{1,0},{2,3},{3,2},{4,5},{5,4},{6,7},{7,6},{8,9},{9,8},{10,11... | collective-permute-start | bytes 2064392 | tf_op jit(solution)/shard_map/ppermute | solution.py:497
  183.0 0.9 copy-start.3

commit v3 on v2

--- a/solution.py
+++ b/solution.py
@@ -58,13 +58,14 @@
 
 
 def forward_kernel(
-    x_ref, keep_ref, scale_in_ref, w_in_ref, w_mid_ref, scale_out_ref, twin_ref,
-    right_ref, left_ref, normed_in_ref, hidden_ref, slope_ref, hat_in_ref, hat_out_ref,
+    x_ref, present_ref, residue_ref, scale_in_ref, w_in_ref, w_mid_ref, scale_out_ref, twin_ref,
+    keep_ref, right_ref, left_ref, normed_in_ref, hidden_ref, slope_ref, hat_in_ref, hat_out_ref,
     normed_out_ref, spread_ref, left_rows, right_rows,
 ):
-    seqs = keep_ref.shape[0]
+    seqs, res = present_ref.shape
     rows = x_ref.shape[0]
-    res = rows // seqs
+    keep_ref[...] = jnp.zeros((seqs, lanes), f32)
+    keep_ref[:, :res] = (present_ref[...] * residue_ref[...]).astype(f32)
     factor = twin_ref.shape[0] // 2
     group = lanes // factor
     x = x_ref[...].astype(f32)
@@ -95,12 +96,15 @@
     for s in range(seqs):
         tile = turned[:, (s // per) * lanes : (s // per + 1) * lanes]
         right_rows[s * factor : (s + 1) * factor, :] = turn(tile, -(s % per) * res)
+    left_pieces = []
     for t in range(res // group):
         tile = left_rows[pl.ds(t * group, seqs, stride=res), :]
         for m in range(1, group):
             tile = tile + turn(left_rows[pl.ds(t * group + m, seqs, stride=res), :], m * factor)
-        left_ref[:, t * lanes : (t + 1) * lanes] = tile.astype(bf16)
-    left_ref[:, res * factor :] = keep.astype(bf16)
+        left_pieces.append(tile)
+    left_record = jnp.concatenate(left_pieces + [keep], axis=1).astype(bf16)
+    for c in range(left_ref.shape[0]):
+        left_ref[c] = left_record
     pieces = []
     for t in range(factor // per):
         tile = right_rows[pl.ds(t * per, seqs, stride=factor), :] * keep
@@ -115,9 +119,11 @@
 
 def pair_kernel(
     parity_ref, rec_ref, other_ref, cot_ref, proj_ref, own_ref, send_ref, back_ref, grad_ref,
-    left_all, right_all, outer_all, adjoint_all, pulled_all, proj_rows, proj_all,
+    left_all, right_all, outer_all, adjoint_all, pulled_all, proj_rows, proj_all, other_all, sem,
 ):
-    shards, _, seqs, _ = rec_ref.shape
+    shards, seqs, record = other_ref.shape
+    start = pltpu.make_async_copy(other_ref, other_all, sem)
+    start.start()
     blocks = 2
     even = parity_ref[0] == 0
     all_seqs = shards * seqs
@@ -131,15 +137,24 @@
     lane = lane_index((all_seqs, lanes))
 
     def left_tile(t):
-        return rec_ref[:, 1, :, t * lanes : (t + 1) * lanes].astype(f32).reshape(all_seqs, lanes)
+        at = record + t * lanes
+        return rec_ref[:, :, at : at + lanes].astype(f32).reshape(all_seqs, lanes)
 
     def right_tiles(t):
-        own = rec_ref[:, 0, :, t * lanes : (t + 1) * lanes].astype(f32).reshape(all_seqs, lanes)
-        other = other_ref[:, :, t * lanes : (t + 1) * lanes].astype(f32).reshape(all_seqs, lanes)
+        own = rec_ref[:, :, t * lanes : (t + 1) * lanes].astype(f32).reshape(all_seqs, lanes)
+        other = other_all[:, :, t * lanes : (t + 1) * lanes].astype(f32).reshape(all_seqs, lanes)
         return jnp.where(even, own, other), jnp.where(even, other, own)
 
+    proj_rows[...] = proj_ref[...].astype(f32)
+    for n in range(sets):
+        for k in range(pairs):
+            proj_all[n * factor : (n + 1) * factor, k * lanes : (k + 1) * lanes] = proj_rows[
+                pl.ds(n * pairs + k, factor, stride=factor), :
+            ].astype(bf16)
     for t in range(wide // lanes):
         left_all[:, t * lanes : (t + 1) * lanes] = left_tile(t).astype(bf16)
+    start.wait()
+    for t in range(wide // lanes):
         a, b = right_tiles(t)
         first = jnp.where(
             lane < 32, a, jnp.where(lane < 64, turn(b, 32), jnp.where(lane < 96, turn(a, 32), turn(b, 64)))
@@ -164,12 +179,6 @@
                 adjoint_all[at + k * cols : at + (k + 1) * cols, m * lanes : (m + 1) * lanes] = (
                     scaled if k == m else nothing
                 )
-    proj_rows[...] = proj_ref[...].astype(f32)
-    for n in range(sets):
-        for k in range(pairs):
-            proj_all[n * factor : (n + 1) * factor, k * lanes : (k + 1) * lanes] = proj_rows[
-                pl.ds(n * pairs + k, factor, stride=factor), :
-            ].astype(bf16)
     step = 256 // factor
     for c in range(res // step):
         outer = first_first(left_all[:, c * step * factor : (c + 1) * step * factor], right_all[...])
@@ -223,8 +232,10 @@
 def backward_kernel(
     core_ref, left_ref, right_ref, keep_ref, cot_ref, scale_in_ref, w_in_ref, w_mid_ref, scale_out_ref,
     twin_ref, grad_ref, normed_in_ref, hidden_ref, slope_ref, hat_in_ref, hat_out_ref, normed_out_ref,
-    spread_ref, out_ref, own_ref, send_ref, left_rows, right_rows, chunks_ref,
+    spread_ref, out_ref, own_ref, send_ref, left_rows, right_rows, chunks_ref, right_all, sem,
 ):
+    start = pltpu.make_async_copy(right_ref, right_all, sem)
+    start.start()
     seqs = keep_ref.shape[0]
     rows, features = cot_ref.shape
     res = rows // seqs
@@ -238,14 +249,15 @@
     starts = chunk_rows(rows, features, units, factor, pair_width, chunks)
     keep = keep_ref[...]
     lane_small = lane_index((seqs, lanes))
-    last = left_ref.shape[1] - 1
+    half = res * factor
     for t in range(res // group):
-        tile = jnp.sum(left_ref[:, last, :, t * lanes : (t + 1) * lanes].astype(f32), axis=0)
+        tile = jnp.sum(left_ref[:, :, half + t * lanes : half + (t + 1) * lanes].astype(f32), axis=0)
         for m in range(group):
             piece = jnp.where(lane_small < factor, turn(tile, -m * factor), 0.0)
             left_rows[pl.ds(t * group + m, seqs, stride=res), :] = piece
+    start.wait()
     for t in range(factor // per):
-        tile = jnp.sum(right_ref[:, :, t * lanes : (t + 1) * lanes].astype(f32), axis=0)
+        tile = jnp.sum(right_all[:, :, t * lanes : (t + 1) * lanes].astype(f32), axis=0)
         for m in range(per):
             right_rows[pl.ds(t * per + m, seqs, stride=factor), :] = turn(tile, -m * res) * keep
     tiles = []
@@ -315,8 +327,12 @@
 
 
 def final_kernel(
-    core_ref, half_ref, other_ref, grad_ref, twin_ref, w_in_ref, w_mid_ref, scale_ref, product_ref
+    core_ref, half_ref, other_ref, grad_ref, twin_ref, w_in_ref, w_mid_ref, scale_ref, product_ref,
+    other_all, sem,
 ):
+    start = pltpu.make_async_copy(other_ref, other_all, sem)
+    start.start()
+    start.wait()
     cols = half_ref.shape[0]
     chunks = 2 * cols
     features, units = w_in_ref.shape
@@ -333,7 +349,7 @@
             return jnp.where(
                 mine,
                 half_ref[k % cols, at : at + size, :].astype(f32),
-                other_ref[k % cols, at : at + size, :].astype(f32),
+                other_all[k % cols, at : at + size, :].astype(f32),
             )
 
         w_in_ref[:, k * unit_step : (k + 1) * unit_step] = read(starts[0], features)
@@ -357,15 +373,15 @@
                     ref[:, m * lanes : (m + 1) * lanes] = extra[n * split + m : n * split + m + 1]
 
 
-def call(kernel, outs, scratch, *args, scalars=0):
-    specs = [pl.BlockSpec(memory_space=pltpu.SMEM)] * scalars
-    specs += [pl.BlockSpec(memory_space=pltpu.VMEM)] * (len(args) - scalars)
+def call(kernel, outs, scratch, *args, scalars=0, loose=()):
+    spaces = [pltpu.SMEM if n < scalars else pl.ANY if n in loose else pltpu.VMEM for n in range(len(args))]
+    specs = [pl.BlockSpec(memory_space=space) for space in spaces]
     return pl.pallas_call(
         kernel,
         out_shape=[jax.ShapeDtypeStruct(s, d) for s, d in outs],
         in_specs=specs,
         out_specs=[pl.BlockSpec(memory_space=pltpu.VMEM)] * len(outs),
-        scratch_shapes=[pltpu.VMEM(s, d) for s, d in scratch],
+        scratch_shapes=[pltpu.SemaphoreType.DMA if s is None else pltpu.VMEM(*s) for s in scratch],
         interpret=INTERPRET,
     )(*args)
 
@@ -407,18 +423,16 @@
     assert (factor, res, blocks, cores, pair_width) == (32, 32, 2, 2, lanes)
     assert col_res == blocks * res and features == 2 * lanes and units == shards * lanes
     x = saved_alignment.reshape(rows, features)
-    keep = jnp.pad(
-        (homolog_existence * amino_existence[None, :]).astype(f32), ((0, 0), (0, lanes - res))
-    )
     scale_in = feedforward_scale.reshape(1, features)
     scale_out = product_scale_vector.reshape(1, features)
     twin = twin_operand_matrix.T
     record = wide + lanes
-    (right, left, normed_in, hidden, slope, hat_in, hat_out, normed_out, spread) = call(
+    (keep, right, left, normed_in, hidden, slope, hat_in, hat_out, normed_out, spread) = call(
         forward_kernel,
         [
+            ((seqs, lanes), f32),
             ((row_devices // 2, seqs, record), bf16),
-            ((seqs, record), bf16),
+            ((shards, seqs, record), bf16),
             ((rows, features), bf16),
             ((rows, units), bf16),
             ((rows, units), f32),
@@ -428,16 +442,17 @@
             ((rows, lanes), f32),
         ],
         [((rows, lanes), f32), ((seqs * factor, lanes), f32)],
-        x, keep, scale_in, expansion_matrix, contraction_matrix, scale_out, twin,
+        x, homolog_existence, amino_existence.reshape(1, res), scale_in, expansion_matrix,
+        contraction_matrix, scale_out, twin,
     )
     alike = [list(range(b, row_devices, 2)) for b in range(2)]
     swap_rows = [(i, i ^ 1) for i in range(row_devices)]
     parity = (lax.axis_index("row") % 2).reshape(1)
     right = exchanged(right, "row", alike)
     records = exchanged(
-        jnp.stack([right, jnp.broadcast_to(left, (shards, seqs, record))], axis=1), ("col", "sub")
-    )
-    other = lax.ppermute(records[:, 0], "row", swap_rows)
+        jnp.concatenate([right, left], axis=2), ("col", "sub")
+    )
+    other = lax.ppermute(records[:, :, :record], "row", swap_rows)
     pairs = lanes // col_res
     sets = factor // pairs
     own, send, left, result_adjoint = call(
@@ -456,13 +471,15 @@
             ((res * factor, sets * lanes), bf16),
             ((factor * factor, lanes), f32),
             ((sets * factor, pairs * lanes), bf16),
+            ((shards, seqs, record), bf16),
+            None,
         ],
         parity, records, other, couple_delta_adjoint, couple_projection_matrix,
-        scalars=1,
+        scalars=1, loose=(2,),
     )
     own = (own.astype(f32) + lax.ppermute(send, "row", swap_rows).astype(f32)).astype(bf16)
-    back = exchanged(jnp.stack([own, left], axis=1), ("col", "sub"))
-    right_back = exchanged(back[:, 0], "row", alike)
+    back = exchanged(jnp.concatenate([own, left], axis=2), ("col", "sub"))
+    right_back = exchanged(back[:, :, :wide], "row", alike)
     core = lax.axis_index("sub").reshape(1)
     starts = chunk_rows(rows, features, units, factor, pair_width, shards)
     lines = -(-(starts[4] + 8) // (2 * row_devices)) * 2 * row_devices
@@ -477,11 +494,13 @@
             ((rows, lanes), f32),
             ((seqs * factor, lanes), f32),
             ((cores, cols, lines, lanes), bf16),
+            ((shards, seqs, wide), bf16),
+            None,
         ],
         core, back, right_back, keep, feedforward_adjoint.reshape(rows, features), scale_in,
         expansion_matrix, contraction_matrix, scale_out, twin, result_adjoint, normed_in, hidden, slope,
         hat_in, hat_out, normed_out, spread,
-        scalars=1,
+        scalars=1, loose=(2,),
     )
     swap = [(0, 1), (1, 0)]
     half = (own.astype(f32) + lax.ppermute(send, "sub", swap).astype(f32)).astype(bf16)
@@ -505,9 +524,9 @@
             ((1, features), f32),
             ((1, features), f32),
         ],
-        [],
+        [((cols, lines, lanes), bf16), None],
         core, half, other,
-        scalars=1,
+        scalars=1, loose=(2,),
     )
     return (
         start_adjoint.reshape(seqs, res, features),

time: 188 us -> 189 us (level)
    another operation x3 -> x0, other arithmetic: 1.91 us -> none  [the longest x2 1.87 us: per_device(): back = exchanged(jnp.stack([own, left], axis=1), ('col', 'sub'))]
where the time goes in v3:
time: 189 us; the launch traced here: 188 us
  blocking collectives  120 us (63%)
  waiting for transfers between devices  25.5 us (13%)
  Pallas kernels  21.8 us (12%)
  starting transfers between devices  12.7 us (7%)
  other arithmetic  4.26 us (2%)
  local copies, waits for them, and re-layouts  3.04 us (2%)
    all_to_all x7, blocking collectives, exchanged(): lax.all_to_all(parts, axis, split_axis=0, concat_axis=0, axis_index_group...  120 us
    pallas_call x4, Pallas kernels, call(): pl.pallas_call(kernel, out_shape=[jax.ShapeDtypeStruct(s, d) for s, d in...  21.8 us
    all_to_all x1, waiting for transfers between devices, exchanged(): lax.all_to_all(parts, axis, split_axis=0, concat_axis=0, axis_index_group...  13 us
    ppermute x1, starting transfers between devices, per_device(): other = lax.ppermute(half, 'sub', swap)  5.68 us
    ppermute x1, waiting for transfers between devices, per_device(): other = lax.ppermute(records[:, :, :record], 'row', swap_rows)  4.8 us
    ppermute x1, waiting for transfers between devices, per_device(): lax.ppermute(send, 'row', swap_rows).astype(f32)  4 us
  transfers between devices with their start and end apart: 5, of which 5 were waited for; matrix products, arithmetic and copies ran while one was open for 0% of the time, Pallas kernels for 0%

profile of v3, /device:TPU:33, one launch (start us, length us, event | category | flops | bytes accessed | tf_op | source)
XLA Modules:
  0.0 187.8 jit_solution(4542999774104217167)
XLA Ops:
  0.6 3.6 %shard_map.162 = (f32[8,128]{1,0:T(8,128)}, bf16[8,8,1152]{2,1,0:T(8,128)(2,1)}, bf16[8,8,1152]{2,1,0:T(8,128)(2,1)}, bf16[256,256]{1,0:T(8,128)(2,1)}, bf16[256...) custom-call(bf16[256,256]{1,0:T(8,128)(2,1)} %bitcast.23, ...), custom_call_target="tpu_custom_call" | custom-call | tf_op jit(solution)/shard_map/pallas_call | solution.py:379
  4.2 38.4 %all_to_all.40 = bf16[8,8,1152]{2,1,0:T(8,128)(2,1)S(1)} all-to-all(bf16[8,8,1152]{2,1,0:T(8,128)(2,1)} %get-tuple-element.30), channel_id=1, replica_groups={{0,16,32,48,64,80,96,112},{8,24,40,56,72,88,104,120},{1,17,33,49,65,81,..., dimensions={0} | all-to-all | bytes 294912 | tf_op jit(solution)/shard_map/all_to_all | solution.py:390
  42.6 0.9 pad_maximum_fusion
  43.6 15.2 %all_to_all.41.rec_ref = bf16[8,8,2304]{2,1,0:T(8,128)(2,1)S(1)} all-to-all(bf16[8,8,2304]{2,1,0:T(8,128)(2,1)S(1)} %pad_maximum_fusion), channel_id=1, replica_groups=mesh['groups'=2,'row'=16,'col'=4,'sub'=2] {'col','sub'}, dimensions={0} | all-to-all | bytes 589824 | tf_op jit(solution)/shard_map/all_to_all | solution.py:390
  58.8 0.1 collective-permute-start
  58.9 4.8 %collective-permute-done.other_ref = bf16[8,8,1152]{2,1,0:T(8,128)(2,1)S(1)} collective-permute-done((bf16[8,8,1152]{2,1,0:T(8,128)(2,1)S(1)}, bf16[8,8,1152]{2,1,0:T(8,128)(2,1)S(1)}, u32[]{:S(2)}, u32[]{:S(2)}) %collective-permute-start) | collective-permute-done | bytes 147488 | tf_op jit(solution)/shard_map/ppermute | solution.py:455
  63.7 0.6 copy-done.5
  64.4 8.6 %shard_map.163 = (bf16[8,8,1024]{2,1,0:T(8,128)(2,1)}, bf16[8,8,1024]{2,1,0:T(8,128)(2,1)}, bf16[8,8,1024]{2,1,0:T(8,128)(2,1)}, f32[512,256]{1,0:T(8,128)}) custom-call(s32[1]{0:T(128)} %bitcast.1.parity_ref, bf16[8,8,2304]{2,1,0:T(8,128)(2,1)} %copy-done.1, bf16[8,8,1152]{2,1,0:T(8,128)(2,1)} %copy-done.5, bf16[32,64,128]{2,1,0:T(8,128)(2,1)} %cot_ref.1, ...), custom_call_target="tpu_custom_call" | custom-call | tf_op jit(solution)/shard_map/pallas_call | solution.py:379
  73.0 0.1 collective-permute-start.1
  73.1 4.0 %collective-permute-done.1 = bf16[8,8,1024]{2,1,0:T(8,128)(2,1)S(1)} collective-permute-done((bf16[8,8,1024]{2,1,0:T(8,128)(2,1)}, bf16[8,8,1024]{2,1,0:T(8,128)(2,1)S(1)}, u32[]{:S(2)}, u32[]{:S(2)}) %collective-permute-start.1) | collective-permute-done | bytes 131104 | tf_op jit(solution)/shard_map/ppermute | solution.py:480
  77.1 0.9 add_convert_fusion.1
  78.1 0.9 pad_maximum_fusion.1
  79.0 11.5 %all_to_all.42.left_ref = bf16[8,8,2048]{2,1,0:T(8,128)(2,1)S(1)} all-to-all(bf16[8,8,2048]{2,1,0:T(8,128)(2,1)S(1)} %pad_maximum_fusion.1), channel_id=1, replica_groups=mesh['groups'=2,'row'=16,'col'=4,'sub'=2] {'col','sub'}, dimensions={0} | all-to-all | bytes 524288 | tf_op jit(solution)/shard_map/all_to_all | solution.py:390
  90.5 0.7 slice.9
  91.2 3.6 %all-to-all-start.3 = ((bf16[8,8,1024]{2,1,0:T(8,128)(2,1)}), bf16[8,8,1024]{2,1,0:T(8,128)(2,1)S(1)}, u32[]{:S(2)}, u32[]{:S(2)}) async-start(bf16[8,8,1024]{2,1,0:T(8,128)(2,1)} %slice.9), calls=%async_computation.3 | async-start | bytes 262144 | tf_op jit(solution)/shard_map/all_to_all | solution.py:390
  94.8 13.0 %all-to-all-done.3.right_ref = bf16[8,8,1024]{2,1,0:T(8,128)(2,1)S(1)} async-done(((bf16[8,8,1024]{2,1,0:T(8,128)(2,1)}), bf16[8,8,1024]{2,1,0:T(8,128)(2,1)S(1)}, u32[]{:S(2)}, u32[]{:S(2)}) %all-to-all-start.3) | async-done | bytes 131104 | tf_op jit(solution)/shard_map/all_to_all | solution.py:390
  107.8 0.6 copy-done.4
  108.5 5.6 %shard_map.164 = (bf16[256,256]{1,0:T(8,128)(2,1)}, bf16[4,672,128]{2,1,0:T(8,128)(2,1)}, bf16[4,672,128]{2,1,0:T(8,128)(2,1)}) custom-call(s32[1]{0:T(128)} %bitcast.core_ref, bf16[8,8,2048]{2,1,0:T(8,128)(2,1)} %copy-done.2, bf16[8,8,1024]{2,1,0:T(8,128)(2,1)} %copy-done.4, f32[8,128]{1,0:T(8,128)} %get-tuple-element.35.keep_ref, ...), custom_call_target="tpu_custom_call" | custom-call | tf_op jit(solution)/shard_map/pallas_call | solution.py:379
  114.1 3.2 %collective-permute-start.2 = (bf16[4,672,128]{2,1,0:T(8,128)(2,1)}, bf16[4,672,128]{2,1,0:T(8,128)(2,1)S(1)}, u32[]{:S(2)}, u32[]{:S(2)}) collective-permute-start(bf16[4,672,128]{2,1,0:T(8,128)(2,1)} %get-tuple-element.46), channel_id=1, source_target_pairs={{0,1},{1,0},{2,3},{3,2},{4,5},{5,4},{6,7},{7,6},{8,9},{9,8},{10,11... | collective-permute-start | bytes 2064392 | tf_op jit(solution)/shard_map/ppermute | solution.py:506
  117.2 2.0 %collective-permute-done.2 = bf16[4,672,128]{2,1,0:T(8,128)(2,1)S(1)} collective-permute-done((bf16[4,672,128]{2,1,0:T(8,128)(2,1)}, bf16[4,672,128]{2,1,0:T(8,128)(2,1)S(1)}, u32[]{:S(2)}, u32[]{:S(2)}) %collective-permute-start.2) | collective-permute-done | bytes 688160 | tf_op jit(solution)/shard_map/ppermute | solution.py:506
  119.2 1.3 add_convert_fusion
  120.5 13.8 %all_to_all.43 = bf16[8,336,128]{2,1,0:T(8,128)(2,1)S(1)} all-to-all(bf16[8,336,128]{2,1,0:T(8,128)(2,1)S(1)} %bitcast.18), channel_id=1, replica_groups={{0,8,2,10,4,12,6,14},{16,24,18,26,20,28,22,30},{32,40,34,42,36,44,38,46..., dimensions={0} | all-to-all | bytes 1376256 | tf_op jit(solution)/shard_map/all_to_all | solution.py:390
  134.3 0.1 reduce_sum.24
  134.4 15.0 %all_to_all.44 = bf16[8,21,2,128]{3,2,1,0:T(2,128)(2,1)S(1)} all-to-all(bf16[8,21,2,128]{3,2,1,0:T(2,128)(2,1)S(1)} %bitcast.20), channel_id=1, replica_groups={{0,16,32,48,64,80,96,112},{8,24,40,56,72,88,104,120},{1,17,33,49,65,81,..., dimensions={0} | all-to-all | bytes 172032 | tf_op jit(solution)/shard_map/all_to_all | solution.py:390
  149.3 0.1 reduce_sum.25
  149.5 14.9 %all_to_all.45 = bf16[8,21,2,128]{3,2,1,0:T(2,128)(2,1)S(1)} all-to-all(bf16[8,21,2,128]{3,2,1,0:T(2,128)(2,1)S(1)} %broadcast_in_dim.6), channel_id=1, replica_groups={{0,16,32,48,64,80,96,112},{8,24,40,56,72,88,104,120},{1,17,33,49,65,81,..., dimensions={0} | all-to-all | bytes 172032 | tf_op jit(solution)/shard_map/all_to_all | solution.py:390
  164.4 0.1 broadcast_in_dim.7
  164.5 11.0 %all_to_all.46 = bf16[8,336,128]{2,1,0:T(8,128)(2,1)S(1)} all-to-all(bf16[8,336,128]{2,1,0:T(8,128)(2,1)S(1)} %broadcast_in_dim.7), channel_id=1, replica_groups={{0,8,2,10,4,12,6,14},{16,24,18,26,20,28,22,30},{32,40,34,42,36,44,38,46..., dimensions={0} | all-to-all | bytes 1376256 | tf_op jit(solution)/shard_map/all_to_all | solution.py:390
  175.4 5.7 %collective-permute-start.3 = (bf16[4,672,128]{2,1,0:T(8,128)(2,1)S(1)}, bf16[4,672,128]{2,1,0:T(8,128)(2,1)S(1)}, u32[]{:S(2)}, u32[]{:S(2)}) collective-permute-start(bf16[4,672,128]{2,1,0:T(8,128)(2,1)S(1)} %bitcast.16), channel_id=1, source_target_pairs={{0,1},{1,0},{2,3},{3,2},{4,5},{5,4},{6,7},{7,6},{8,9},{9,8},{10,11... | collective-permute-start | bytes 2064392 | tf_op jit(solution)/shard_map/ppermute | solution.py:516
  181.1 1.8 collective-permute-done.3.other_ref
  182.9 0.9 copy-done.3
  183.7 4.0 %shard_map.165 = (f32[1024,128]{1,0:T(8,128)}, f32[64,256]{1,0:T(8,128)}, f32[256,1024]{1,0:T(8,128)}, f32[1024,256]{1,0:T(8,128)}, f32[1,256]{1,0:T(1,128)}, /*index=5*/f32[1,256]{1,0:T(1,128)}) custom-call(s32[1]{0:T(128)} %bitcast.core_ref, bf16[4,672,128]{2,1,0:T(8,128)(2,1)} %bitcast.17, bf16[4,672,128]{2,1,0:T(8,128)(2,1)} %copy-done.3), custom_call_target="tpu_custom_call" | custom-call | tf_op jit(solution)/shard_map/pallas_call | solution.py:379
  (11 shorter events, 0.1 us)
Async XLA Ops:
  58.7 5.0 %copy-start.1 = (bf16[8,8,2304]{2,1,0:T(8,128)(2,1)}, bf16[8,8,2304]{2,1,0:T(8,128)(2,1)S(1)}, u32[]{:S(2)}) copy-start(bf16[8,8,2304]{2,1,0:T(8,128)(2,1)S(1)} %all_to_all.41.rec_ref) | copy-start | bytes 884740
  58.8 5.0 %collective-permute-start = (bf16[8,8,1152]{2,1,0:T(8,128)(2,1)S(1)}, bf16[8,8,1152]{2,1,0:T(8,128)(2,1)S(1)}, u32[]{:S(2)}, u32[]{:S(2)}) collective-permute-start(bf16[8,8,1152]{2,1,0:T(8,128)(2,1)S(1)} %slice.8), channel_id=1, source_target_pairs={{0,8},{8,0},{16,24},{24,16},{32,40},{40,32},{48,56},{56,48},{64,72... | collective-permute-start | bytes 442376 | tf_op jit(solution)/shard_map/ppermute | solution.py:455
  63.7 0.7 copy-start.5
  73.0 4.2 %collective-permute-start.1 = (bf16[8,8,1024]{2,1,0:T(8,128)(2,1)}, bf16[8,8,1024]{2,1,0:T(8,128)(2,1)S(1)}, u32[]{:S(2)}, u32[]{:S(2)}) collective-permute-start(bf16[8,8,1024]{2,1,0:T(8,128)(2,1)} %get-tuple-element.33), channel_id=1, source_target_pairs={{0,8},{8,0},{16,24},{24,16},{32,40},{40,32},{48,56},{56,48},{64,72... | collective-permute-start | bytes 393224 | tf_op jit(solution)/shard_map/ppermute | solution.py:480
  90.5 17.3 %copy-start.2 = (bf16[8,8,2048]{2,1,0:T(8,128)(2,1)}, bf16[8,8,2048]{2,1,0:T(8,128)(2,1)S(1)}, u32[]{:S(2)}) copy-start(bf16[8,8,2048]{2,1,0:T(8,128)(2,1)S(1)} %all_to_all.42.left_ref) | copy-start | bytes 786436
  91.2 16.6 %all-to-all-start.3 = ((bf16[8,8,1024]{2,1,0:T(8,128)(2,1)}), bf16[8,8,1024]{2,1,0:T(8,128)(2,1)S(1)}, u32[]{:S(2)}, u32[]{:S(2)}) async-start(bf16[8,8,1024]{2,1,0:T(8,128)(2,1)} %slice.9), calls=%async_computation.3 | async-start | bytes 262144 | tf_op jit(solution)/shard_map/all_to_all | solution.py:390
  107.8 0.6 copy-start.4
  114.1 5.2 %collective-permute-start.2 = (bf16[4,672,128]{2,1,0:T(8,128)(2,1)}, bf16[4,672,128]{2,1,0:T(8,128)(2,1)S(1)}, u32[]{:S(2)}, u32[]{:S(2)}) collective-permute-start(bf16[4,672,128]{2,1,0:T(8,128)(2,1)} %get-tuple-element.46), channel_id=1, source_target_pairs={{0,1},{1,0},{2,3},{3,2},{4,5},{5,4},{6,7},{7,6},{8,9},{9,8},{10,11... | collective-permute-start | bytes 2064392 | tf_op jit(solution)/shard_map/ppermute | solution.py:506
  175.4 7.5 %copy-start = (bf16[8,336,128]{2,1,0:T(8,128)(2,1)}, bf16[8,336,128]{2,1,0:T(8,128)(2,1)S(1)}, u32[]{:S(2)}) copy-start(bf16[8,336,128]{2,1,0:T(8,128)(2,1)S(1)} %all_to_all.46) | copy-start | bytes 2064388
  175.4 7.4 %collective-permute-start.3 = (bf16[4,672,128]{2,1,0:T(8,128)(2,1)S(1)}, bf16[4,672,128]{2,1,0:T(8,128)(2,1)S(1)}, u32[]{:S(2)}, u32[]{:S(2)}) collective-permute-start(bf16[4,672,128]{2,1,0:T(8,128)(2,1)S(1)} %bitcast.16), channel_id=1, source_target_pairs={{0,1},{1,0},{2,3},{3,2},{4,5},{5,4},{6,7},{7,6},{8,9},{9,8},{10,11... | collective-permute-start | bytes 2064392 | tf_op jit(solution)/shard_map/ppermute | solution.py:516
  182.9 0.9 copy-start.3

commit v4 on v3

--- a/solution.py
+++ b/solution.py
@@ -57,34 +57,46 @@
     return jnp.sum(jnp.where(own, wide, 0.0), axis=1, keepdims=True)
 
 
+def fetch(pairs):
+    started = [pltpu.make_async_copy(*pair) for pair in pairs]
+    for copy in started:
+        copy.start()
+    return started
+
+
+def transition(x, scale_in, w_in_ref, scale_out, w_mid_ref, w_in_copy, w_mid_copy, with_slope):
+    hat_in, inv_in = layer_normalize(x)
+    normed_in = (hat_in * scale_in).astype(bf16)
+    w_in_copy.wait()
+    pre = plain(normed_in, w_in_ref[...])
+    share = 0.5 * (1.0 + lax.erf(pre * math.sqrt(0.5)))
+    hidden = (pre * share).astype(bf16)
+    slope = None
+    if with_slope:
+        slope = share + pre * (jnp.exp(-0.5 * pre * pre) * (1.0 / math.sqrt(2.0 * math.pi)))
+    w_mid_copy.wait()
+    mixed = x + plain(hidden, w_mid_ref[...])
+    hat_out, inv_out = layer_normalize(mixed)
+    normed_out = (hat_out * scale_out).astype(bf16)
+    return normed_in, hidden, slope, hat_in, inv_in, hat_out, inv_out, normed_out
+
+
 def forward_kernel(
-    x_ref, present_ref, residue_ref, scale_in_ref, w_in_ref, w_mid_ref, scale_out_ref, twin_ref,
-    keep_ref, right_ref, left_ref, normed_in_ref, hidden_ref, slope_ref, hat_in_ref, hat_out_ref,
-    normed_out_ref, spread_ref, left_rows, right_rows,
+    x_ref, present_ref, residue_ref, scale_in_ref, w_in_hbm, w_mid_hbm, scale_out_ref, twin_ref,
+    keep_ref, right_ref, left_ref, left_rows, right_rows, w_in_ref, w_mid_ref, sem_a, sem_b,
 ):
+    copy_in, copy_mid = fetch([(w_in_hbm, w_in_ref, sem_a), (w_mid_hbm, w_mid_ref, sem_b)])
     seqs, res = present_ref.shape
     rows = x_ref.shape[0]
     keep_ref[...] = jnp.zeros((seqs, lanes), f32)
     keep_ref[:, :res] = (present_ref[...] * residue_ref[...]).astype(f32)
     factor = twin_ref.shape[0] // 2
     group = lanes // factor
-    x = x_ref[...].astype(f32)
-    hat_in, inv_in = layer_normalize(x)
-    hat_in_ref[...] = hat_in
-    normed_in = (hat_in * scale_in_ref[...]).astype(bf16)
-    normed_in_ref[...] = normed_in
-    pre = plain(normed_in, w_in_ref[...])
-    share = 0.5 * (1.0 + lax.erf(pre * math.sqrt(0.5)))
-    hidden = (pre * share).astype(bf16)
-    hidden_ref[...] = hidden
-    slope_ref[...] = share + pre * (jnp.exp(-0.5 * pre * pre) * (1.0 / math.sqrt(2.0 * math.pi)))
-    mixed = x + plain(hidden, w_mid_ref[...])
-    hat_out, inv_out = layer_normalize(mixed)
-    hat_out_ref[...] = hat_out
+    normed_out = transition(
+        x_ref[...].astype(f32), scale_in_ref[...], w_in_ref, scale_out_ref[...], w_mid_ref, copy_in, copy_mid,
+        False,
+    )[-1]
     lane = lane_index((rows, lanes))
-    spread_ref[...] = jnp.where(lane == 0, inv_in, inv_out)
-    normed_out = (hat_out * scale_out_ref[...]).astype(bf16)
-    normed_out_ref[...] = normed_out
     keep = keep_ref[...]
     twin = twin_ref[...]
     projected = last_last(
@@ -118,18 +130,17 @@
 
 
 def pair_kernel(
-    parity_ref, rec_ref, other_ref, cot_ref, proj_ref, own_ref, send_ref, back_ref, grad_ref,
-    left_all, right_all, outer_all, adjoint_all, pulled_all, proj_rows, proj_all, other_all, sem,
+    parity_ref, rec_ref, other_ref, cot_hbm, proj_ref, back_ref, send_ref, grad_ref,
+    left_all, right_all, outer_all, adjoint_all, pulled_all, proj_rows, proj_all, other_all, cot_ref, sem, sem_b,
 ):
     shards, seqs, record = other_ref.shape
-    start = pltpu.make_async_copy(other_ref, other_all, sem)
-    start.start()
+    start, copy_cot = fetch([(other_ref, other_all, sem), (cot_hbm, cot_ref, sem_b)])
     blocks = 2
     even = parity_ref[0] == 0
     all_seqs = shards * seqs
     res = cot_ref.shape[0]
     cols = cot_ref.shape[1]
-    wide = back_ref.shape[2]
+    wide = send_ref.shape[2]
     factor = wide // res
     pairs = lanes // cols
     sets = factor // pairs
@@ -171,6 +182,7 @@
     count = first_first(keep_cols, keep_rows)[:cols]
     inverse = 1.0 / jnp.maximum(count, 1.0)
     nothing = jnp.zeros((cols, lanes), bf16)
+    copy_cot.wait()
     for i in range(res):
         scaled = (cot_ref[i].astype(f32) * inverse[:, i : i + 1]).astype(bf16)
         at = i * lanes
@@ -195,15 +207,15 @@
                 pulled_all[at : at + factor, n * lanes : (n + 1) * lanes] = pulled[
                     n * factor : (n + 1) * factor, i * lanes : (i + 1) * lanes
                 ].astype(bf16)
-    grad_ref[...] = plain(outer_all[...], adjoint_all[...])
+    grad_ref[...] = plain(outer_all[...], adjoint_all[...]).astype(bf16)
     grad_left = last_last(right_all[...], pulled_all[...])
     grad_right = plain(left_all[...], pulled_all[...])
 
-    def put(ref, t, values):
-        ref[:, :, t * lanes : (t + 1) * lanes] = values.reshape(shards, seqs, lanes).astype(bf16)
+    def put(ref, at, values):
+        ref[:, :, at : at + lanes] = values.reshape(shards, seqs, lanes).astype(bf16)
 
     for t in range(wide // lanes):
-        put(back_ref, t, grad_left[:, t * lanes : (t + 1) * lanes])
+        put(back_ref, wide + t * lanes, grad_left[:, t * lanes : (t + 1) * lanes])
         a = grad_right[:, 2 * t * lanes : (2 * t + 1) * lanes]
         b = grad_right[:, (2 * t + 1) * lanes : (2 * t + 2) * lanes]
         first = jnp.where(
@@ -212,8 +224,8 @@
         second = jnp.where(
             lane < 32, turn(a, 96), jnp.where(lane < 64, turn(a, 64), jnp.where(lane < 96, turn(b, 32), b))
         )
-        put(own_ref, t, jnp.where(even, first, second))
-        put(send_ref, t, jnp.where(even, second, first))
+        put(back_ref, t * lanes, jnp.where(even, first, second))
+        put(send_ref, t * lanes, jnp.where(even, second, first))
 
 
 def chunk_rows(rows, features, hidden, factor, pair_width, chunks):
@@ -230,12 +242,15 @@
 
 
 def backward_kernel(
-    core_ref, left_ref, right_ref, keep_ref, cot_ref, scale_in_ref, w_in_ref, w_mid_ref, scale_out_ref,
-    twin_ref, grad_ref, normed_in_ref, hidden_ref, slope_ref, hat_in_ref, hat_out_ref, normed_out_ref,
-    spread_ref, out_ref, own_ref, send_ref, left_rows, right_rows, chunks_ref, right_all, sem,
+    core_ref, left_hbm, right_hbm, keep_ref, x_ref, cot_ref, scale_in_ref, w_in_hbm, w_mid_hbm,
+    scale_out_ref, twin_ref, grad_hbm, out_ref, own_ref, send_ref,
+    left_rows, right_rows, chunks_ref, left_ref, right_all, w_in_ref, w_mid_ref, grad_ref,
+    sem_a, sem_b, sem_c, sem_d, sem_e,
 ):
-    start = pltpu.make_async_copy(right_ref, right_all, sem)
-    start.start()
+    copy_in, copy_mid, copy_left, copy_right, copy_grad = fetch([
+        (w_in_hbm, w_in_ref, sem_a), (w_mid_hbm, w_mid_ref, sem_b), (left_hbm, left_ref, sem_c),
+        (right_hbm, right_all, sem_d), (grad_hbm, grad_ref, sem_e),
+    ])
     seqs = keep_ref.shape[0]
     rows, features = cot_ref.shape
     res = rows // seqs
@@ -244,18 +259,23 @@
     per = lanes // res
     cols = own_ref.shape[0]
     chunks = 2 * cols
-    units = hidden_ref.shape[1]
+    units = w_in_ref.shape[1]
     pair_width = lanes
     starts = chunk_rows(rows, features, units, factor, pair_width, chunks)
     keep = keep_ref[...]
     lane_small = lane_index((seqs, lanes))
+    normed_in, hidden, slope, hat_in, inv_in, hat_out, inv_out, normed_out = transition(
+        x_ref[...].astype(f32), scale_in_ref[...], w_in_ref, scale_out_ref[...], w_mid_ref, copy_in, copy_mid,
+        True,
+    )
+    copy_left.wait()
     half = res * factor
     for t in range(res // group):
         tile = jnp.sum(left_ref[:, :, half + t * lanes : half + (t + 1) * lanes].astype(f32), axis=0)
         for m in range(group):
             piece = jnp.where(lane_small < factor, turn(tile, -m * factor), 0.0)
             left_rows[pl.ds(t * group + m, seqs, stride=res), :] = piece
-    start.wait()
+    copy_right.wait()
     for t in range(factor // per):
         tile = jnp.sum(right_all[:, :, t * lanes : (t + 1) * lanes].astype(f32), axis=0)
         for m in range(per):
@@ -274,27 +294,24 @@
     grad_proj = (left_rows[...] * keep_column(keep, seqs, res) + jnp.transpose(turned)).astype(bf16)
     twin = twin_ref[...]
     twin = jnp.concatenate([twin, jnp.zeros((lanes - 2 * factor, features), bf16)], axis=0)
-    operand_adjoint = first_first(grad_proj, normed_out_ref[...])
+    operand_adjoint = first_first(grad_proj, normed_out)
     rescaled = plain(grad_proj, twin)
-    hat_out = hat_out_ref[...]
     product_adjoint = jnp.sum(rescaled * hat_out, axis=0, keepdims=True)
-    inv_in = spread_ref[:, 0:1]
-    inv_out = spread_ref[:, 1:2]
     combined = cot_ref[...].astype(f32) + standardizer_adjoint(
         rescaled * scale_out_ref[...], hat_out, inv_out
     )
     mixed_half = combined.astype(bf16)
     grad_hidden = last_last(mixed_half, w_mid_ref[...])
-    grad_pre = (slope_ref[...] * grad_hidden).astype(bf16)
+    grad_pre = (slope * grad_hidden).astype(bf16)
     grad_in = last_last(grad_pre, w_in_ref[...])
-    hat_in = hat_in_ref[...]
     scale_adjoint = jnp.sum(grad_in * hat_in, axis=0, keepdims=True)
     out_ref[...] = (
         combined + standardizer_adjoint(grad_in * scale_in_ref[...], hat_in, inv_in)
     ).astype(bf16)
-    hidden_adjoint = first_first(hidden_ref[...], mixed_half)
-    expansion_adjoint = first_first(normed_in_ref[...], grad_pre)
+    hidden_adjoint = first_first(hidden, mixed_half)
+    expansion_adjoint = first_first(normed_in, grad_pre)
     split = features // lanes
+    copy_grad.wait()
 
     def put(k, at, values):
         chunks_ref[k // cols, k % cols, at : at + values.shape[0], :] = values.astype(bf16)
@@ -327,12 +344,9 @@
 
 
 def final_kernel(
-    core_ref, half_ref, other_ref, grad_ref, twin_ref, w_in_ref, w_mid_ref, scale_ref, product_ref,
-    other_all, sem,
+    core_ref, half_ref, other_ref, grad_hbm, twin_ref, w_in_hbm, w_mid_hbm, scale_ref, product_ref,
+    grad_ref, w_in_ref, w_mid_ref, sem_grad, sem_in, sem_mid,
 ):
-    start = pltpu.make_async_copy(other_ref, other_all, sem)
-    start.start()
-    start.wait()
     cols = half_ref.shape[0]
     chunks = 2 * cols
     features, units = w_in_ref.shape
@@ -342,46 +356,61 @@
     unit_step = units // chunks
     core = core_ref[0]
     height = factor * factor // 2 // chunks
+
+    def read(k, at, size):
+        return jnp.where(
+            core == k // cols,
+            half_ref[k % cols, at : at + size, :].astype(f32),
+            other_ref[k % cols, at : at + size, :].astype(f32),
+        )
+
+    leaving = []
     for k in range(chunks):
-        mine = core == k // cols
-
-        def read(at, size):
-            return jnp.where(
-                mine,
-                half_ref[k % cols, at : at + size, :].astype(f32),
-                other_all[k % cols, at : at + size, :].astype(f32),
-            )
-
-        w_in_ref[:, k * unit_step : (k + 1) * unit_step] = read(starts[0], features)
+        span = slice(k * unit_step, (k + 1) * unit_step)
+        w_in_ref[:, span] = read(k, starts[0], features)
+        leaving.append(pltpu.make_async_copy(w_in_ref.at[:, span], w_in_hbm.at[:, span], sem_in.at[k]))
+        leaving[-1].start()
         for m in range(split):
-            w_mid_ref[k * unit_step : (k + 1) * unit_step, m * lanes : (m + 1) * lanes] = read(
-                starts[1] + m * unit_step, unit_step
-            )
+            w_mid_ref[span, m * lanes : (m + 1) * lanes] = read(k, starts[1] + m * unit_step, unit_step)
+        leaving.append(pltpu.make_async_copy(w_mid_ref.at[span, :], w_mid_hbm.at[span, :], sem_mid.at[k]))
+        leaving[-1].start()
+    for k in range(chunks):
         for m in range(2):
-            block = read(starts[2] + m * height, height)
+            block = read(k, starts[2] + m * height, height)
             for n in range(height // factor):
                 q = 2 * (k * (height // factor) + n) + m
                 grad_ref[pl.ds(q, factor, stride=factor), :] = block[n * factor : (n + 1) * factor]
-        tall = 2 * factor // chunks
-        block = read(starts[3], starts[4] - starts[3])
+    leaving.append(pltpu.make_async_copy(grad_ref, grad_hbm, sem_grad))
+    leaving[-1].start()
+    tall = 2 * factor // chunks
+    for k in range(chunks):
+        block = read(k, starts[3], starts[4] - starts[3])
         for m in range(split):
             twin_ref[k * tall : (k + 1) * tall, m * lanes : (m + 1) * lanes] = block[m * tall : (m + 1) * tall]
-        if k == 0:
-            extra = read(starts[4], 8)
-            for n, ref in enumerate((scale_ref, product_ref)):
-                for m in range(split):
-                    ref[:, m * lanes : (m + 1) * lanes] = extra[n * split + m : n * split + m + 1]
-
-
-def call(kernel, outs, scratch, *args, scalars=0, loose=()):
+    extra = read(0, starts[4], 8)
+    for n, ref in enumerate((scale_ref, product_ref)):
+        for m in range(split):
+            ref[:, m * lanes : (m + 1) * lanes] = extra[n * split + m : n * split + m + 1]
+    for copy in leaving:
+        copy.wait()
+
+
+def call(kernel, outs, scratch, *args, scalars=0, loose=(), loose_outs=()):
     spaces = [pltpu.SMEM if n < scalars else pl.ANY if n in loose else pltpu.VMEM for n in range(len(args))]
     specs = [pl.BlockSpec(memory_space=space) for space in spaces]
     return pl.pallas_call(
         kernel,
         out_shape=[jax.ShapeDtypeStruct(s, d) for s, d in outs],
         in_specs=specs,
-        out_specs=[pl.BlockSpec(memory_space=pltpu.VMEM)] * len(outs),
-        scratch_shapes=[pltpu.SemaphoreType.DMA if s is None else pltpu.VMEM(*s) for s in scratch],
+        out_specs=[
+            pl.BlockSpec(memory_space=pl.ANY if n in loose_outs else pltpu.VMEM) for n in range(len(outs))
+        ],
+        scratch_shapes=[
+            pltpu.SemaphoreType.DMA if s is None
+            else pltpu.SemaphoreType.DMA(s) if isinstance(s[0], int)
+            else pltpu.VMEM(*s)
+            for s in scratch
+        ],
         interpret=INTERPRET,
     )(*args)
 
@@ -427,23 +456,24 @@
     scale_out = product_scale_vector.reshape(1, features)
     twin = twin_operand_matrix.T
     record = wide + lanes
-    (keep, right, left, normed_in, hidden, slope, hat_in, hat_out, normed_out, spread) = call(
+    keep, right, left = call(
         forward_kernel,
         [
             ((seqs, lanes), f32),
             ((row_devices // 2, seqs, record), bf16),
             ((shards, seqs, record), bf16),
-            ((rows, features), bf16),
-            ((rows, units), bf16),
-            ((rows, units), f32),
-            ((rows, features), f32),
-            ((rows, features), f32),
-            ((rows, features), bf16),
+        ],
+        [
             ((rows, lanes), f32),
-        ],
-        [((rows, lanes), f32), ((seqs * factor, lanes), f32)],
+            ((seqs * factor, lanes), f32),
+            ((features, units), bf16),
+            ((units, features), bf16),
+            None,
+            None,
+        ],
         x, homolog_existence, amino_existence.reshape(1, res), scale_in, expansion_matrix,
         contraction_matrix, scale_out, twin,
+        loose=(4, 5),
     )
     alike = [list(range(b, row_devices, 2)) for b in range(2)]
     swap_rows = [(i, i ^ 1) for i in range(row_devices)]
@@ -455,13 +485,12 @@
     other = lax.ppermute(records[:, :, :record], "row", swap_rows)
     pairs = lanes // col_res
     sets = factor // pairs
-    own, send, left, result_adjoint = call(
+    back, send, result_adjoint = call(
         pair_kernel,
         [
+            ((shards, seqs, 2 * wide), bf16),
             ((shards, seqs, wide), bf16),
-            ((shards, seqs, wide), bf16),
-            ((shards, seqs, wide), bf16),
-            ((sets * factor, pairs * lanes), f32),
+            ((sets * factor, pairs * lanes), bf16),
         ],
         [
             ((all_seqs, wide), bf16),
@@ -472,13 +501,15 @@
             ((factor * factor, lanes), f32),
             ((sets * factor, pairs * lanes), bf16),
             ((shards, seqs, record), bf16),
+            ((res, col_res, lanes), bf16),
+            None,
             None,
         ],
         parity, records, other, couple_delta_adjoint, couple_projection_matrix,
-        scalars=1, loose=(2,),
-    )
-    own = (own.astype(f32) + lax.ppermute(send, "row", swap_rows).astype(f32)).astype(bf16)
-    back = exchanged(jnp.concatenate([own, left], axis=2), ("col", "sub"))
+        scalars=1, loose=(2, 3),
+    )
+    paired = jnp.pad(lax.ppermute(send, "row", swap_rows), ((0, 0), (0, 0), (0, wide)))
+    back = exchanged((back.astype(f32) + paired.astype(f32)).astype(bf16), ("col", "sub"))
     right_back = exchanged(back[:, :, :wide], "row", alike)
     core = lax.axis_index("sub").reshape(1)
     starts = chunk_rows(rows, features, units, factor, pair_width, shards)
@@ -494,13 +525,20 @@
             ((rows, lanes), f32),
             ((seqs * factor, lanes), f32),
             ((cores, cols, lines, lanes), bf16),
+            ((shards, seqs, 2 * wide), bf16),
             ((shards, seqs, wide), bf16),
-            None,
-        ],
-        core, back, right_back, keep, feedforward_adjoint.reshape(rows, features), scale_in,
-        expansion_matrix, contraction_matrix, scale_out, twin, result_adjoint, normed_in, hidden, slope,
-        hat_in, hat_out, normed_out, spread,
-        scalars=1, loose=(2,),
+            ((features, units), bf16),
+            ((units, features), bf16),
+            ((sets * factor, pairs * lanes), bf16),
+            None,
+            None,
+            None,
+            None,
+            None,
+        ],
+        core, back, right_back, keep, x, feedforward_adjoint.reshape(rows, features), scale_in,
+        expansion_matrix, contraction_matrix, scale_out, twin, result_adjoint,
+        scalars=1, loose=(1, 2, 7, 8, 11),
     )
     swap = [(0, 1), (1, 0)]
     half = (own.astype(f32) + lax.ppermute(send, "sub", swap).astype(f32)).astype(bf16)
@@ -524,9 +562,16 @@
             ((1, features), f32),
             ((1, features), f32),
         ],
-        [((cols, lines, lanes), bf16), None],
+        [
+            ((factor * factor, pair_width), f32),
+            ((features, units), f32),
+            ((units, features), f32),
+            None,
+            (shards,),
+            (shards,),
+        ],
         core, half, other,
-        scalars=1, loose=(2,),
+        scalars=1, loose_outs=(0, 2, 3),
     )
     return (
         start_adjoint.reshape(seqs, res, features),

time: 189 us -> 188 us (level)
  no operation moved by 1% of the time
where the time goes in v4:
time: 188 us
  blocking collectives  120 us (64%)
  waiting for transfers between devices  25.5 us (14%)
  Pallas kernels  22.2 us (12%)
  starting transfers between devices  12.9 us (7%)
  other arithmetic  3.38 us (2%)
  local copies, waits for them, and re-layouts  3.03 us (2%)
    all_to_all x7, blocking collectives, exchanged(): lax.all_to_all(parts, axis, split_axis=0, concat_axis=0, axis_index_group...  120 us
    pallas_call x4, Pallas kernels, call(): pl.pallas_call(kernel, out_shape=[jax.ShapeDtypeStruct(s, d) for s, d in...  22.2 us
    all_to_all x1, waiting for transfers between devices, exchanged(): lax.all_to_all(parts, axis, split_axis=0, concat_axis=0, axis_index_group...  13 us
    ppermute x1, starting transfers between devices, per_device(): other = lax.ppermute(half, 'sub', swap)  5.68 us
    ppermute x1, waiting for transfers between devices, per_device(): other = lax.ppermute(records[:, :, :record], 'row', swap_rows)  4.8 us
    ppermute x1, waiting for transfers between devices, per_device(): lax.ppermute(send, 'row', swap_rows)  4 us
  transfers between devices with their start and end apart: 5, of which 5 were waited for; matrix products, arithmetic and copies ran while one was open for 0% of the time, Pallas kernels for 0%

profile of v4, /device:TPU:33, one launch (start us, length us, event | category | flops | bytes accessed | tf_op | source)
XLA Modules:
  0.0 187.6 jit_solution(2918846270955079155)
XLA Ops:
  0.6 4.0 %shard_map.162 = (f32[8,128]{1,0:T(8,128)}, bf16[8,8,1152]{2,1,0:T(8,128)(2,1)}, bf16[8,8,1152]{2,1,0:T(8,128)(2,1)}) custom-call(bf16[256,256]{1,0:T(8,128)(2,1)} %bitcast.19, s32[8,32]{1,0:T(8,128)} %present_ref.1, s32[1,32]{1,0:T(1,128)} %bitcast.30, f32[1,256]{1,0:T(1,128)} %bitcast.26, bf16[256,1024]{1,0:T(8,128)(2,1)} %w_in_hbm.3, ...), custom_call_target="tpu_custom_call" | custom-call | tf_op jit(solution)/shard_map/pallas_call | solution.py:401
  4.7 38.4 %all_to_all.40 = bf16[8,8,1152]{2,1,0:T(8,128)(2,1)S(1)} all-to-all(bf16[8,8,1152]{2,1,0:T(8,128)(2,1)} %get-tuple-element.22), channel_id=1, replica_groups={{0,16,32,48,64,80,96,112},{8,24,40,56,72,88,104,120},{1,17,33,49,65,81,..., dimensions={0} | all-to-all | bytes 294912 | tf_op jit(solution)/shard_map/all_to_all | solution.py:419
  43.1 0.9 pad_maximum_fusion
  44.1 15.2 %all_to_all.41.rec_ref = bf16[8,8,2304]{2,1,0:T(8,128)(2,1)S(1)} all-to-all(bf16[8,8,2304]{2,1,0:T(8,128)(2,1)S(1)} %pad_maximum_fusion), channel_id=1, replica_groups=mesh['groups'=2,'row'=16,'col'=4,'sub'=2] {'col','sub'}, dimensions={0} | all-to-all | bytes 589824 | tf_op jit(solution)/shard_map/all_to_all | solution.py:419
  59.2 0.1 collective-permute-start
  59.4 4.8 %collective-permute-done.other_ref = bf16[8,8,1152]{2,1,0:T(8,128)(2,1)S(1)} collective-permute-done((bf16[8,8,1152]{2,1,0:T(8,128)(2,1)S(1)}, bf16[8,8,1152]{2,1,0:T(8,128)(2,1)S(1)}, u32[]{:S(2)}, u32[]{:S(2)}) %collective-permute-start) | collective-permute-done | bytes 147488 | tf_op jit(solution)/shard_map/ppermute | solution.py:485
  64.2 0.0 copy-done.1
  64.2 0.7 copy-done.5
  64.9 8.5 %shard_map.163 = (bf16[8,8,2048]{2,1,0:T(8,128)(2,1)}, bf16[8,8,1024]{2,1,0:T(8,128)(2,1)}, bf16[512,256]{1,0:T(8,128)(2,1)}) custom-call(s32[1]{0:T(128)} %bitcast.1.parity_ref, bf16[8,8,2304]{2,1,0:T(8,128)(2,1)} %copy-done.1, bf16[8,8,1152]{2,1,0:T(8,128)(2,1)} %copy-done.5, bf16[32,64,128]{2,1,0:T(8,128)(2,1)} %cot_hbm.1, bf16[1024,128]{1,0:T(8,128)(2,1)} %proj_ref.1), custom_call_target="tpu_custom_call" | custom-call | tf_op jit(solution)/shard_map/pallas_call | solution.py:401
  73.3 0.1 collective-permute-start.1
  73.5 4.0 %collective-permute-done.1 = bf16[8,8,1024]{2,1,0:T(8,128)(2,1)S(1)} collective-permute-done((bf16[8,8,1024]{2,1,0:T(8,128)(2,1)}, bf16[8,8,1024]{2,1,0:T(8,128)(2,1)S(1)}, u32[]{:S(2)}, u32[]{:S(2)}) %collective-permute-start.1) | collective-permute-done | bytes 131104 | tf_op jit(solution)/shard_map/ppermute | solution.py:511
  77.5 1.0 add_convert_fusion.1
  78.5 11.5 %all_to_all.42.left_hbm = bf16[8,8,2048]{2,1,0:T(8,128)(2,1)S(1)} all-to-all(bf16[8,8,2048]{2,1,0:T(8,128)(2,1)S(1)} %add_convert_fusion.1), channel_id=1, replica_groups=mesh['groups'=2,'row'=16,'col'=4,'sub'=2] {'col','sub'}, dimensions={0} | all-to-all | bytes 524288 | tf_op jit(solution)/shard_map/all_to_all | solution.py:419
  90.0 0.7 slice.9
  90.7 3.6 %all-to-all-start.3 = ((bf16[8,8,1024]{2,1,0:T(8,128)(2,1)}), bf16[8,8,1024]{2,1,0:T(8,128)(2,1)S(1)}, u32[]{:S(2)}, u32[]{:S(2)}) async-start(bf16[8,8,1024]{2,1,0:T(8,128)(2,1)} %slice.9), calls=%async_computation.3 | async-start | bytes 262144 | tf_op jit(solution)/shard_map/all_to_all | solution.py:419
  94.3 13.0 %all-to-all-done.3.right_hbm = bf16[8,8,1024]{2,1,0:T(8,128)(2,1)S(1)} async-done(((bf16[8,8,1024]{2,1,0:T(8,128)(2,1)}), bf16[8,8,1024]{2,1,0:T(8,128)(2,1)S(1)}, u32[]{:S(2)}, u32[]{:S(2)}) %all-to-all-start.3) | async-done | bytes 131104 | tf_op jit(solution)/shard_map/all_to_all | solution.py:419
  107.3 0.6 copy-done.4
  107.9 6.0 %shard_map.164 = (bf16[256,256]{1,0:T(8,128)(2,1)}, bf16[4,672,128]{2,1,0:T(8,128)(2,1)}, bf16[4,672,128]{2,1,0:T(8,128)(2,1)}) custom-call(s32[1]{0:T(128)} %bitcast.core_ref, bf16[8,8,2048]{2,1,0:T(8,128)(2,1)} %copy-done.2, bf16[8,8,1024]{2,1,0:T(8,128)(2,1)} %copy-done.4, f32[8,128]{1,0:T(8,128)} %get-tuple-element.26.keep_ref, ...), custom_call_target="tpu_custom_call" | custom-call | tf_op jit(solution)/shard_map/pallas_call | solution.py:401
  114.0 3.4 %collective-permute-start.2 = (bf16[4,672,128]{2,1,0:T(8,128)(2,1)}, bf16[4,672,128]{2,1,0:T(8,128)(2,1)S(1)}, u32[]{:S(2)}, u32[]{:S(2)}) collective-permute-start(bf16[4,672,128]{2,1,0:T(8,128)(2,1)} %get-tuple-element.30), channel_id=1, source_target_pairs={{0,1},{1,0},{2,3},{3,2},{4,5},{5,4},{6,7},{7,6},{8,9},{9,8},{10,11... | collective-permute-start | bytes 2064392 | tf_op jit(solution)/shard_map/ppermute | solution.py:544
  117.3 2.0 %collective-permute-done.2 = bf16[4,672,128]{2,1,0:T(8,128)(2,1)S(1)} collective-permute-done((bf16[4,672,128]{2,1,0:T(8,128)(2,1)}, bf16[4,672,128]{2,1,0:T(8,128)(2,1)S(1)}, u32[]{:S(2)}, u32[]{:S(2)}) %collective-permute-start.2) | collective-permute-done | bytes 688160 | tf_op jit(solution)/shard_map/ppermute | solution.py:544
  119.3 1.3 add_convert_fusion
  120.6 13.8 %all_to_all.43 = bf16[8,336,128]{2,1,0:T(8,128)(2,1)S(1)} all-to-all(bf16[8,336,128]{2,1,0:T(8,128)(2,1)S(1)} %bitcast.18), channel_id=1, replica_groups={{0,8,2,10,4,12,6,14},{16,24,18,26,20,28,22,30},{32,40,34,42,36,44,38,46..., dimensions={0} | all-to-all | bytes 1376256 | tf_op jit(solution)/shard_map/all_to_all | solution.py:419
  134.4 0.1 reduce_sum.24
  134.5 15.0 %all_to_all.44 = bf16[8,21,2,128]{3,2,1,0:T(2,128)(2,1)S(1)} all-to-all(bf16[8,21,2,128]{3,2,1,0:T(2,128)(2,1)S(1)} %bitcast.22), channel_id=1, replica_groups={{0,16,32,48,64,80,96,112},{8,24,40,56,72,88,104,120},{1,17,33,49,65,81,..., dimensions={0} | all-to-all | bytes 172032 | tf_op jit(solution)/shard_map/all_to_all | solution.py:419
  149.4 0.1 reduce_sum.25
  149.6 14.9 %all_to_all.45 = bf16[8,21,2,128]{3,2,1,0:T(2,128)(2,1)S(1)} all-to-all(bf16[8,21,2,128]{3,2,1,0:T(2,128)(2,1)S(1)} %broadcast_in_dim.6), channel_id=1, replica_groups={{0,16,32,48,64,80,96,112},{8,24,40,56,72,88,104,120},{1,17,33,49,65,81,..., dimensions={0} | all-to-all | bytes 172032 | tf_op jit(solution)/shard_map/all_to_all | solution.py:419
  164.5 0.1 broadcast_in_dim.7
  164.6 11.0 %all_to_all.46 = bf16[8,336,128]{2,1,0:T(8,128)(2,1)S(1)} all-to-all(bf16[8,336,128]{2,1,0:T(8,128)(2,1)S(1)} %broadcast_in_dim.7), channel_id=1, replica_groups={{0,8,2,10,4,12,6,14},{16,24,18,26,20,28,22,30},{32,40,34,42,36,44,38,46..., dimensions={0} | all-to-all | bytes 1376256 | tf_op jit(solution)/shard_map/all_to_all | solution.py:419
  175.5 5.7 %collective-permute-start.3 = (bf16[4,672,128]{2,1,0:T(8,128)(2,1)S(1)}, bf16[4,672,128]{2,1,0:T(8,128)(2,1)S(1)}, u32[]{:S(2)}, u32[]{:S(2)}) collective-permute-start(bf16[4,672,128]{2,1,0:T(8,128)(2,1)S(1)} %bitcast.16), channel_id=1, source_target_pairs={{0,1},{1,0},{2,3},{3,2},{4,5},{5,4},{6,7},{7,6},{8,9},{9,8},{10,11... | collective-permute-start | bytes 2064392 | tf_op jit(solution)/shard_map/ppermute | solution.py:554
  181.2 1.8 collective-permute-done.3.other_ref
  183.0 0.9 copy-done.3
  183.8 3.6 %shard_map.165 = (f32[1024,128]{1,0:T(8,128)}, f32[64,256]{1,0:T(8,128)}, f32[256,1024]{1,0:T(8,128)}, f32[1024,256]{1,0:T(8,128)}, f32[1,256]{1,0:T(1,128)}, /*index=5*/f32[1,256]{1,0:T(1,128)}) custom-call(s32[1]{0:T(128)} %bitcast.core_ref, bf16[4,672,128]{2,1,0:T(8,128)(2,1)} %bitcast.17, bf16[4,672,128]{2,1,0:T(8,128)(2,1)} %copy-done.3), custom_call_target="tpu_custom_call" | custom-call | tf_op jit(solution)/shard_map/pallas_call | solution.py:401
  (10 shorter events, 0.1 us)
Async XLA Ops:
  59.2 5.0 %copy-start.1 = (bf16[8,8,2304]{2,1,0:T(8,128)(2,1)}, bf16[8,8,2304]{2,1,0:T(8,128)(2,1)S(1)}, u32[]{:S(2)}) copy-start(bf16[8,8,2304]{2,1,0:T(8,128)(2,1)S(1)} %all_to_all.41.rec_ref) | copy-start | bytes 884740
  59.2 5.0 %collective-permute-start = (bf16[8,8,1152]{2,1,0:T(8,128)(2,1)S(1)}, bf16[8,8,1152]{2,1,0:T(8,128)(2,1)S(1)}, u32[]{:S(2)}, u32[]{:S(2)}) collective-permute-start(bf16[8,8,1152]{2,1,0:T(8,128)(2,1)S(1)} %slice.8), channel_id=1, source_target_pairs={{0,8},{8,0},{16,24},{24,16},{32,40},{40,32},{48,56},{56,48},{64,72... | collective-permute-start | bytes 442376 | tf_op jit(solution)/shard_map/ppermute | solution.py:485
  64.2 0.7 copy-start.5
  73.3 4.2 %collective-permute-start.1 = (bf16[8,8,1024]{2,1,0:T(8,128)(2,1)}, bf16[8,8,1024]{2,1,0:T(8,128)(2,1)S(1)}, u32[]{:S(2)}, u32[]{:S(2)}) collective-permute-start(bf16[8,8,1024]{2,1,0:T(8,128)(2,1)} %get-tuple-element.25), channel_id=1, source_target_pairs={{0,8},{8,0},{16,24},{24,16},{32,40},{40,32},{48,56},{56,48},{64,72... | collective-permute-start | bytes 393224 | tf_op jit(solution)/shard_map/ppermute | solution.py:511
  90.0 17.3 %copy-start.2 = (bf16[8,8,2048]{2,1,0:T(8,128)(2,1)}, bf16[8,8,2048]{2,1,0:T(8,128)(2,1)S(1)}, u32[]{:S(2)}) copy-start(bf16[8,8,2048]{2,1,0:T(8,128)(2,1)S(1)} %all_to_all.42.left_hbm) | copy-start | bytes 786436
  90.7 16.6 %all-to-all-start.3 = ((bf16[8,8,1024]{2,1,0:T(8,128)(2,1)}), bf16[8,8,1024]{2,1,0:T(8,128)(2,1)S(1)}, u32[]{:S(2)}, u32[]{:S(2)}) async-start(bf16[8,8,1024]{2,1,0:T(8,128)(2,1)} %slice.9), calls=%async_computation.3 | async-start | bytes 262144 | tf_op jit(solution)/shard_map/all_to_all | solution.py:419
  107.3 0.7 copy-start.4
  114.0 5.3 %collective-permute-start.2 = (bf16[4,672,128]{2,1,0:T(8,128)(2,1)}, bf16[4,672,128]{2,1,0:T(8,128)(2,1)S(1)}, u32[]{:S(2)}, u32[]{:S(2)}) collective-permute-start(bf16[4,672,128]{2,1,0:T(8,128)(2,1)} %get-tuple-element.30), channel_id=1, source_target_pairs={{0,1},{1,0},{2,3},{3,2},{4,5},{5,4},{6,7},{7,6},{8,9},{9,8},{10,11... | collective-permute-start | bytes 2064392 | tf_op jit(solution)/shard_map/ppermute | solution.py:544
  175.5 7.5 %copy-start = (bf16[8,336,128]{2,1,0:T(8,128)(2,1)}, bf16[8,336,128]{2,1,0:T(8,128)(2,1)S(1)}, u32[]{:S(2)}) copy-start(bf16[8,336,128]{2,1,0:T(8,128)(2,1)S(1)} %all_to_all.46) | copy-start | bytes 2064388
  175.5 7.4 %collective-permute-start.3 = (bf16[4,672,128]{2,1,0:T(8,128)(2,1)S(1)}, bf16[4,672,128]{2,1,0:T(8,128)(2,1)S(1)}, u32[]{:S(2)}, u32[]{:S(2)}) collective-permute-start(bf16[4,672,128]{2,1,0:T(8,128)(2,1)S(1)} %bitcast.16), channel_id=1, source_target_pairs={{0,1},{1,0},{2,3},{3,2},{4,5},{5,4},{6,7},{7,6},{8,9},{9,8},{10,11... | collective-permute-start | bytes 2064392 | tf_op jit(solution)/shard_map/ppermute | solution.py:554
  183.0 0.9 copy-start.3

commit v5 on v4

--- a/solution.py
+++ b/solution.py
@@ -57,24 +57,15 @@
     return jnp.sum(jnp.where(own, wide, 0.0), axis=1, keepdims=True)
 
 
-def fetch(pairs):
-    started = [pltpu.make_async_copy(*pair) for pair in pairs]
-    for copy in started:
-        copy.start()
-    return started
-
-
-def transition(x, scale_in, w_in_ref, scale_out, w_mid_ref, w_in_copy, w_mid_copy, with_slope):
+def transition(x, scale_in, w_in_ref, scale_out, w_mid_ref, with_slope):
     hat_in, inv_in = layer_normalize(x)
     normed_in = (hat_in * scale_in).astype(bf16)
-    w_in_copy.wait()
     pre = plain(normed_in, w_in_ref[...])
     share = 0.5 * (1.0 + lax.erf(pre * math.sqrt(0.5)))
     hidden = (pre * share).astype(bf16)
     slope = None
     if with_slope:
         slope = share + pre * (jnp.exp(-0.5 * pre * pre) * (1.0 / math.sqrt(2.0 * math.pi)))
-    w_mid_copy.wait()
     mixed = x + plain(hidden, w_mid_ref[...])
     hat_out, inv_out = layer_normalize(mixed)
     normed_out = (hat_out * scale_out).astype(bf16)
@@ -82,10 +73,9 @@
 
 
 def forward_kernel(
-    x_ref, present_ref, residue_ref, scale_in_ref, w_in_hbm, w_mid_hbm, scale_out_ref, twin_ref,
-    keep_ref, right_ref, left_ref, left_rows, right_rows, w_in_ref, w_mid_ref, sem_a, sem_b,
+    x_ref, present_ref, residue_ref, scale_in_ref, w_in_ref, w_mid_ref, scale_out_ref, twin_ref,
+    keep_ref, right_ref, left_ref, left_rows, right_rows,
 ):
-    copy_in, copy_mid = fetch([(w_in_hbm, w_in_ref, sem_a), (w_mid_hbm, w_mid_ref, sem_b)])
     seqs, res = present_ref.shape
     rows = x_ref.shape[0]
     keep_ref[...] = jnp.zeros((seqs, lanes), f32)
@@ -93,8 +83,7 @@
     factor = twin_ref.shape[0] // 2
     group = lanes // factor
     normed_out = transition(
-        x_ref[...].astype(f32), scale_in_ref[...], w_in_ref, scale_out_ref[...], w_mid_ref, copy_in, copy_mid,
-        False,
+        x_ref[...].astype(f32), scale_in_ref[...], w_in_ref, scale_out_ref[...], w_mid_ref, False,
     )[-1]
     lane = lane_index((rows, lanes))
     keep = keep_ref[...]
@@ -130,11 +119,10 @@
 
 
 def pair_kernel(
-    parity_ref, rec_ref, other_ref, cot_hbm, proj_ref, back_ref, send_ref, grad_ref,
-    left_all, right_all, outer_all, adjoint_all, pulled_all, proj_rows, proj_all, other_all, cot_ref, sem, sem_b,
+    parity_ref, rec_ref, other_ref, cot_ref, proj_ref, back_ref, send_ref, grad_ref,
+    left_all, right_all, outer_all, adjoint_all, pulled_all, proj_rows, proj_all,
 ):
     shards, seqs, record = other_ref.shape
-    start, copy_cot = fetch([(other_ref, other_all, sem), (cot_hbm, cot_ref, sem_b)])
     blocks = 2
     even = parity_ref[0] == 0
     all_seqs = shards * seqs
@@ -153,7 +141,7 @@
 
     def right_tiles(t):
         own = rec_ref[:, :, t * lanes : (t + 1) * lanes].astype(f32).reshape(all_seqs, lanes)
-        other = other_all[:, :, t * lanes : (t + 1) * lanes].astype(f32).reshape(all_seqs, lanes)
+        other = other_ref[:, :, t * lanes : (t + 1) * lanes].astype(f32).reshape(all_seqs, lanes)
         return jnp.where(even, own, other), jnp.where(even, other, own)
 
     proj_rows[...] = proj_ref[...].astype(f32)
@@ -164,7 +152,6 @@
             ].astype(bf16)
     for t in range(wide // lanes):
         left_all[:, t * lanes : (t + 1) * lanes] = left_tile(t).astype(bf16)
-    start.wait()
     for t in range(wide // lanes):
         a, b = right_tiles(t)
         first = jnp.where(
@@ -182,7 +169,6 @@
     count = first_first(keep_cols, keep_rows)[:cols]
     inverse = 1.0 / jnp.maximum(count, 1.0)
     nothing = jnp.zeros((cols, lanes), bf16)
-    copy_cot.wait()
     for i in range(res):
         scaled = (cot_ref[i].astype(f32) * inverse[:, i : i + 1]).astype(bf16)
         at = i * lanes
@@ -242,15 +228,9 @@
 
 
 def backward_kernel(
-    core_ref, left_hbm, right_hbm, keep_ref, x_ref, cot_ref, scale_in_ref, w_in_hbm, w_mid_hbm,
-    scale_out_ref, twin_ref, grad_hbm, out_ref, own_ref, send_ref,
-    left_rows, right_rows, chunks_ref, left_ref, right_all, w_in_ref, w_mid_ref, grad_ref,
-    sem_a, sem_b, sem_c, sem_d, sem_e,
+    core_ref, left_ref, right_ref, keep_ref, x_ref, cot_ref, scale_in_ref, w_in_ref, w_mid_ref,
+    scale_out_ref, twin_ref, grad_ref, out_ref, own_ref, send_ref, left_rows, right_rows, chunks_ref,
 ):
-    copy_in, copy_mid, copy_left, copy_right, copy_grad = fetch([
-        (w_in_hbm, w_in_ref, sem_a), (w_mid_hbm, w_mid_ref, sem_b), (left_hbm, left_ref, sem_c),
-        (right_hbm, right_all, sem_d), (grad_hbm, grad_ref, sem_e),
-    ])
     seqs = keep_ref.shape[0]
     rows, features = cot_ref.shape
     res = rows // seqs
@@ -265,19 +245,16 @@
     keep = keep_ref[...]
     lane_small = lane_index((seqs, lanes))
     normed_in, hidden, slope, hat_in, inv_in, hat_out, inv_out, normed_out = transition(
-        x_ref[...].astype(f32), scale_in_ref[...], w_in_ref, scale_out_ref[...], w_mid_ref, copy_in, copy_mid,
-        True,
-    )
-    copy_left.wait()
+        x_ref[...].astype(f32), scale_in_ref[...], w_in_ref, scale_out_ref[...], w_mid_ref, True,
+    )
     half = res * factor
     for t in range(res // group):
         tile = jnp.sum(left_ref[:, :, half + t * lanes : half + (t + 1) * lanes].astype(f32), axis=0)
         for m in range(group):
             piece = jnp.where(lane_small < factor, turn(tile, -m * factor), 0.0)
             left_rows[pl.ds(t * group + m, seqs, stride=res), :] = piece
-    copy_right.wait()
     for t in range(factor // per):
-        tile = jnp.sum(right_all[:, :, t * lanes : (t + 1) * lanes].astype(f32), axis=0)
+        tile = jnp.sum(right_ref[:, :, t * lanes : (t + 1) * lanes].astype(f32), axis=0)
         for m in range(per):
             right_rows[pl.ds(t * per + m, seqs, stride=factor), :] = turn(tile, -m * res) * keep
     tiles = []
@@ -311,7 +288,6 @@
     hidden_adjoint = first_first(hidden, mixed_half)
     expansion_adjoint = first_first(normed_in, grad_pre)
     split = features // lanes
-    copy_grad.wait()
 
     def put(k, at, values):
         chunks_ref[k // cols, k % cols, at : at + values.shape[0], :] = values.astype(bf16)
@@ -344,8 +320,7 @@
 
 
 def final_kernel(
-    core_ref, half_ref, other_ref, grad_hbm, twin_ref, w_in_hbm, w_mid_hbm, scale_ref, product_ref,
-    grad_ref, w_in_ref, w_mid_ref, sem_grad, sem_in, sem_mid,
+    core_ref, half_ref, other_ref, grad_ref, twin_ref, w_in_ref, w_mid_ref, scale_ref, product_ref
 ):
     cols = half_ref.shape[0]
     chunks = 2 * cols
@@ -364,24 +339,17 @@
             other_ref[k % cols, at : at + size, :].astype(f32),
         )
 
-    leaving = []
     for k in range(chunks):
         span = slice(k * unit_step, (k + 1) * unit_step)
         w_in_ref[:, span] = read(k, starts[0], features)
-        leaving.append(pltpu.make_async_copy(w_in_ref.at[:, span], w_in_hbm.at[:, span], sem_in.at[k]))
-        leaving[-1].start()
         for m in range(split):
             w_mid_ref[span, m * lanes : (m + 1) * lanes] = read(k, starts[1] + m * unit_step, unit_step)
-        leaving.append(pltpu.make_async_copy(w_mid_ref.at[span, :], w_mid_hbm.at[span, :], sem_mid.at[k]))
-        leaving[-1].start()
     for k in range(chunks):
         for m in range(2):
             block = read(k, starts[2] + m * height, height)
             for n in range(height // factor):
                 q = 2 * (k * (height // factor) + n) + m
                 grad_ref[pl.ds(q, factor, stride=factor), :] = block[n * factor : (n + 1) * factor]
-    leaving.append(pltpu.make_async_copy(grad_ref, grad_hbm, sem_grad))
-    leaving[-1].start()
     tall = 2 * factor // chunks
     for k in range(chunks):
         block = read(k, starts[3], starts[4] - starts[3])
@@ -391,26 +359,17 @@
     for n, ref in enumerate((scale_ref, product_ref)):
         for m in range(split):
             ref[:, m * lanes : (m + 1) * lanes] = extra[n * split + m : n * split + m + 1]
-    for copy in leaving:
-        copy.wait()
-
-
-def call(kernel, outs, scratch, *args, scalars=0, loose=(), loose_outs=()):
-    spaces = [pltpu.SMEM if n < scalars else pl.ANY if n in loose else pltpu.VMEM for n in range(len(args))]
-    specs = [pl.BlockSpec(memory_space=space) for space in spaces]
+
+
+def call(kernel, outs, scratch, *args, scalars=0):
+    specs = [pl.BlockSpec(memory_space=pltpu.SMEM)] * scalars
+    specs += [pl.BlockSpec(memory_space=pltpu.VMEM)] * (len(args) - scalars)
     return pl.pallas_call(
         kernel,
         out_shape=[jax.ShapeDtypeStruct(s, d) for s, d in outs],
         in_specs=specs,
-        out_specs=[
-            pl.BlockSpec(memory_space=pl.ANY if n in loose_outs else pltpu.VMEM) for n in range(len(outs))
-        ],
-        scratch_shapes=[
-            pltpu.SemaphoreType.DMA if s is None
-            else pltpu.SemaphoreType.DMA(s) if isinstance(s[0], int)
-            else pltpu.VMEM(*s)
-            for s in scratch
-        ],
+        out_specs=[pl.BlockSpec(memory_space=pltpu.VMEM)] * len(outs),
+        scratch_shapes=[pltpu.VMEM(s, d) for s, d in scratch],
         interpret=INTERPRET,
     )(*args)
 
@@ -466,14 +425,9 @@
         [
             ((rows, lanes), f32),
             ((seqs * factor, lanes), f32),
-            ((features, units), bf16),
-            ((units, features), bf16),
-            None,
-            None,
         ],
         x, homolog_existence, amino_existence.reshape(1, res), scale_in, expansion_matrix,
         contraction_matrix, scale_out, twin,
-        loose=(4, 5),
     )
     alike = [list(range(b, row_devices, 2)) for b in range(2)]
     swap_rows = [(i, i ^ 1) for i in range(row_devices)]
@@ -500,13 +454,9 @@
             ((res * factor, sets * lanes), bf16),
             ((factor * factor, lanes), f32),
             ((sets * factor, pairs * lanes), bf16),
-            ((shards, seqs, record), bf16),
-            ((res, col_res, lanes), bf16),
-            None,
-            None,
         ],
         parity, records, other, couple_delta_adjoint, couple_projection_matrix,
-        scalars=1, loose=(2, 3),
+        scalars=1,
     )
     paired = jnp.pad(lax.ppermute(send, "row", swap_rows), ((0, 0), (0, 0), (0, wide)))
     back = exchanged((back.astype(f32) + paired.astype(f32)).astype(bf16), ("col", "sub"))
@@ -525,20 +475,10 @@
             ((rows, lanes), f32),
             ((seqs * factor, lanes), f32),
             ((cores, cols, lines, lanes), bf16),
-            ((shards, seqs, 2 * wide), bf16),
-            ((shards, seqs, wide), bf16),
-            ((features, units), bf16),
-            ((units, features), bf16),
-            ((sets * factor, pairs * lanes), bf16),
-            None,
-            None,
-            None,
-            None,
-            None,
         ],
         core, back, right_back, keep, x, feedforward_adjoint.reshape(rows, features), scale_in,
         expansion_matrix, contraction_matrix, scale_out, twin, result_adjoint,
-        scalars=1, loose=(1, 2, 7, 8, 11),
+        scalars=1,
     )
     swap = [(0, 1), (1, 0)]
     half = (own.astype(f32) + lax.ppermute(send, "sub", swap).astype(f32)).astype(bf16)
@@ -562,16 +502,9 @@
             ((1, features), f32),
             ((1, features), f32),
         ],
-        [
-            ((factor * factor, pair_width), f32),
-            ((features, units), f32),
-            ((units, features), f32),
-            None,
-            (shards,),
-            (shards,),
-        ],
+        [],
         core, half, other,
-        scalars=1, loose_outs=(0, 2, 3),
+        scalars=1,
     )
     return (
         start_adjoint.reshape(seqs, res, features),

time: 188 us -> 185 us (0.984)
  Pallas kernels: 22.2 us -> 19.5 us
    pallas_call x4, Pallas kernels: 22.2 us -> 19.5 us  [call(): pl.pallas_call(kernel, out_shape=[jax.ShapeDtypeStruct(s, d) for s, d in...]
where the time goes in v5:
time: 185 us; the launch traced here: 184 us
  blocking collectives  120 us (65%)
  waiting for transfers between devices  25.6 us (14%)
  Pallas kernels  19.5 us (11%)
  starting transfers between devices  12.5 us (7%)
  other arithmetic  3.38 us (2%)
  local copies, waits for them, and re-layouts  3.03 us (2%)
    all_to_all x7, blocking collectives, exchanged(): lax.all_to_all(parts, axis, split_axis=0, concat_axis=0, axis_index_group...  120 us
    pallas_call x4, Pallas kernels, call(): pl.pallas_call(kernel, out_shape=[jax.ShapeDtypeStruct(s, d) for s, d in...  19.5 us
    all_to_all x1, waiting for transfers between devices, exchanged(): lax.all_to_all(parts, axis, split_axis=0, concat_axis=0, axis_index_group...  13 us
    ppermute x1, starting transfers between devices, per_device(): other = lax.ppermute(half, 'sub', swap)  5.68 us
    ppermute x1, waiting for transfers between devices, per_device(): other = lax.ppermute(records[:, :, :record], 'row', swap_rows)  4.8 us
    ppermute x1, waiting for transfers between devices, per_device(): lax.ppermute(send, 'row', swap_rows)  4.01 us
  transfers between devices with their start and end apart: 5, of which 5 were waited for; matrix products, arithmetic and copies ran while one was open for 0% of the time, Pallas kernels for 0%

profile of v5, /device:TPU:33, one launch (start us, length us, event | category | flops | bytes accessed | tf_op | source)
XLA Modules:
  0.0 184.4 jit_solution(410584948072811583)
XLA Ops:
  0.6 3.3 %shard_map.162 = (f32[8,128]{1,0:T(8,128)}, bf16[8,8,1152]{2,1,0:T(8,128)(2,1)}, bf16[8,8,1152]{2,1,0:T(8,128)(2,1)}) custom-call(bf16[256,256]{1,0:T(8,128)(2,1)} %bitcast.19, s32[8,32]{1,0:T(8,128)} %present_ref.1, s32[1,32]{1,0:T(1,128)} %bitcast.30, f32[1,256]{1,0:T(1,128)} %bitcast.26, bf16[256,1024]{1,0:T(8,128)(2,1)} %w_in_ref.3, ...), custom_call_target="tpu_custom_call" | custom-call | tf_op jit(solution)/shard_map/pallas_call | solution.py:367
  3.9 38.4 %all_to_all.40 = bf16[8,8,1152]{2,1,0:T(8,128)(2,1)S(1)} all-to-all(bf16[8,8,1152]{2,1,0:T(8,128)(2,1)} %get-tuple-element.22), channel_id=1, replica_groups={{0,16,32,48,64,80,96,112},{8,24,40,56,72,88,104,120},{1,17,33,49,65,81,..., dimensions={0} | all-to-all | bytes 294912 | tf_op jit(solution)/shard_map/all_to_all | solution.py:378
  42.4 0.9 pad_maximum_fusion
  43.3 15.2 %all_to_all.41.rec_ref = bf16[8,8,2304]{2,1,0:T(8,128)(2,1)S(1)} all-to-all(bf16[8,8,2304]{2,1,0:T(8,128)(2,1)S(1)} %pad_maximum_fusion), channel_id=1, replica_groups=mesh['groups'=2,'row'=16,'col'=4,'sub'=2] {'col','sub'}, dimensions={0} | all-to-all | bytes 589824 | tf_op jit(solution)/shard_map/all_to_all | solution.py:378
  58.5 0.1 collective-permute-start
  58.6 4.8 %collective-permute-done.other_ref = bf16[8,8,1152]{2,1,0:T(8,128)(2,1)S(1)} collective-permute-done((bf16[8,8,1152]{2,1,0:T(8,128)(2,1)S(1)}, bf16[8,8,1152]{2,1,0:T(8,128)(2,1)S(1)}, u32[]{:S(2)}, u32[]{:S(2)}) %collective-permute-start) | collective-permute-done | bytes 147488 | tf_op jit(solution)/shard_map/ppermute | solution.py:439
  63.4 0.7 copy-done.5
  64.1 8.5 %shard_map.163 = (bf16[8,8,2048]{2,1,0:T(8,128)(2,1)}, bf16[8,8,1024]{2,1,0:T(8,128)(2,1)}, bf16[512,256]{1,0:T(8,128)(2,1)}) custom-call(s32[1]{0:T(128)} %bitcast.1.parity_ref, bf16[8,8,2304]{2,1,0:T(8,128)(2,1)} %copy-done.1, bf16[8,8,1152]{2,1,0:T(8,128)(2,1)} %copy-done.5, bf16[32,64,128]{2,1,0:T(8,128)(2,1)} %cot_ref.1, bf16[1024,128]{1,0:T(8,128)(2,1)} %proj_ref.1), custom_call_target="tpu_custom_call" | custom-call | tf_op jit(solution)/shard_map/pallas_call | solution.py:367
  72.6 0.0 collective-permute-start.1
  72.6 4.0 %collective-permute-done.1 = bf16[8,8,1024]{2,1,0:T(8,128)(2,1)S(1)} collective-permute-done((bf16[8,8,1024]{2,1,0:T(8,128)(2,1)}, bf16[8,8,1024]{2,1,0:T(8,128)(2,1)S(1)}, u32[]{:S(2)}, u32[]{:S(2)}) %collective-permute-start.1) | collective-permute-done | bytes 131104 | tf_op jit(solution)/shard_map/ppermute | solution.py:461
  76.6 1.0 add_convert_fusion.1
  77.6 11.5 %all_to_all.42.left_ref = bf16[8,8,2048]{2,1,0:T(8,128)(2,1)S(1)} all-to-all(bf16[8,8,2048]{2,1,0:T(8,128)(2,1)S(1)} %add_convert_fusion.1), channel_id=1, replica_groups=mesh['groups'=2,'row'=16,'col'=4,'sub'=2] {'col','sub'}, dimensions={0} | all-to-all | bytes 524288 | tf_op jit(solution)/shard_map/all_to_all | solution.py:378
  89.1 0.7 slice.9
  89.8 3.6 %all-to-all-start.3 = ((bf16[8,8,1024]{2,1,0:T(8,128)(2,1)}), bf16[8,8,1024]{2,1,0:T(8,128)(2,1)S(1)}, u32[]{:S(2)}, u32[]{:S(2)}) async-start(bf16[8,8,1024]{2,1,0:T(8,128)(2,1)} %slice.9), calls=%async_computation.3 | async-start | bytes 262144 | tf_op jit(solution)/shard_map/all_to_all | solution.py:378
  93.4 13.0 %all-to-all-done.3.right_ref = bf16[8,8,1024]{2,1,0:T(8,128)(2,1)S(1)} async-done(((bf16[8,8,1024]{2,1,0:T(8,128)(2,1)}), bf16[8,8,1024]{2,1,0:T(8,128)(2,1)S(1)}, u32[]{:S(2)}, u32[]{:S(2)}) %all-to-all-start.3) | async-done | bytes 131104 | tf_op jit(solution)/shard_map/all_to_all | solution.py:378
  106.4 0.0 copy-done.2
  106.4 0.6 copy-done.4
  107.1 4.8 %shard_map.164 = (bf16[256,256]{1,0:T(8,128)(2,1)}, bf16[4,672,128]{2,1,0:T(8,128)(2,1)}, bf16[4,672,128]{2,1,0:T(8,128)(2,1)}) custom-call(s32[1]{0:T(128)} %bitcast.core_ref, bf16[8,8,2048]{2,1,0:T(8,128)(2,1)} %copy-done.2, bf16[8,8,1024]{2,1,0:T(8,128)(2,1)} %copy-done.4, f32[8,128]{1,0:T(8,128)} %get-tuple-element.26.keep_ref, ...), custom_call_target="tpu_custom_call" | custom-call | tf_op jit(solution)/shard_map/pallas_call | solution.py:367
  111.9 3.0 %collective-permute-start.2 = (bf16[4,672,128]{2,1,0:T(8,128)(2,1)}, bf16[4,672,128]{2,1,0:T(8,128)(2,1)S(1)}, u32[]{:S(2)}, u32[]{:S(2)}) collective-permute-start(bf16[4,672,128]{2,1,0:T(8,128)(2,1)} %get-tuple-element.30), channel_id=1, source_target_pairs={{0,1},{1,0},{2,3},{3,2},{4,5},{5,4},{6,7},{7,6},{8,9},{9,8},{10,11... | collective-permute-start | bytes 2064392 | tf_op jit(solution)/shard_map/ppermute | solution.py:484
  114.9 2.0 %collective-permute-done.2 = bf16[4,672,128]{2,1,0:T(8,128)(2,1)S(1)} collective-permute-done((bf16[4,672,128]{2,1,0:T(8,128)(2,1)}, bf16[4,672,128]{2,1,0:T(8,128)(2,1)S(1)}, u32[]{:S(2)}, u32[]{:S(2)}) %collective-permute-start.2) | collective-permute-done | bytes 688160 | tf_op jit(solution)/shard_map/ppermute | solution.py:484
  116.9 1.3 add_convert_fusion
  118.2 13.8 %all_to_all.43 = bf16[8,336,128]{2,1,0:T(8,128)(2,1)S(1)} all-to-all(bf16[8,336,128]{2,1,0:T(8,128)(2,1)S(1)} %bitcast.18), channel_id=1, replica_groups={{0,8,2,10,4,12,6,14},{16,24,18,26,20,28,22,30},{32,40,34,42,36,44,38,46..., dimensions={0} | all-to-all | bytes 1376256 | tf_op jit(solution)/shard_map/all_to_all | solution.py:378
  132.0 0.1 reduce_sum.24
  132.1 15.0 %all_to_all.44 = bf16[8,21,2,128]{3,2,1,0:T(2,128)(2,1)S(1)} all-to-all(bf16[8,21,2,128]{3,2,1,0:T(2,128)(2,1)S(1)} %bitcast.22), channel_id=1, replica_groups={{0,16,32,48,64,80,96,112},{8,24,40,56,72,88,104,120},{1,17,33,49,65,81,..., dimensions={0} | all-to-all | bytes 172032 | tf_op jit(solution)/shard_map/all_to_all | solution.py:378
  147.0 0.1 reduce_sum.25
  147.2 14.9 %all_to_all.45 = bf16[8,21,2,128]{3,2,1,0:T(2,128)(2,1)S(1)} all-to-all(bf16[8,21,2,128]{3,2,1,0:T(2,128)(2,1)S(1)} %broadcast_in_dim.6), channel_id=1, replica_groups={{0,16,32,48,64,80,96,112},{8,24,40,56,72,88,104,120},{1,17,33,49,65,81,..., dimensions={0} | all-to-all | bytes 172032 | tf_op jit(solution)/shard_map/all_to_all | solution.py:378
  162.1 0.1 broadcast_in_dim.7
  162.2 11.0 %all_to_all.46 = bf16[8,336,128]{2,1,0:T(8,128)(2,1)S(1)} all-to-all(bf16[8,336,128]{2,1,0:T(8,128)(2,1)S(1)} %broadcast_in_dim.7), channel_id=1, replica_groups={{0,8,2,10,4,12,6,14},{16,24,18,26,20,28,22,30},{32,40,34,42,36,44,38,46..., dimensions={0} | all-to-all | bytes 1376256 | tf_op jit(solution)/shard_map/all_to_all | solution.py:378
  173.1 5.7 %collective-permute-start.3 = (bf16[4,672,128]{2,1,0:T(8,128)(2,1)S(1)}, bf16[4,672,128]{2,1,0:T(8,128)(2,1)S(1)}, u32[]{:S(2)}, u32[]{:S(2)}) collective-permute-start(bf16[4,672,128]{2,1,0:T(8,128)(2,1)S(1)} %bitcast.16), channel_id=1, source_target_pairs={{0,1},{1,0},{2,3},{3,2},{4,5},{5,4},{6,7},{7,6},{8,9},{9,8},{10,11... | collective-permute-start | bytes 2064392 | tf_op jit(solution)/shard_map/ppermute | solution.py:494
  178.8 1.8 collective-permute-done.3.other_ref
  180.6 0.9 copy-done.3
  181.4 2.9 %shard_map.165 = (f32[1024,128]{1,0:T(8,128)}, f32[64,256]{1,0:T(8,128)}, f32[256,1024]{1,0:T(8,128)}, f32[1024,256]{1,0:T(8,128)}, f32[1,256]{1,0:T(1,128)}, /*index=5*/f32[1,256]{1,0:T(1,128)}) custom-call(s32[1]{0:T(128)} %bitcast.core_ref, bf16[4,672,128]{2,1,0:T(8,128)(2,1)} %bitcast.17, bf16[4,672,128]{2,1,0:T(8,128)(2,1)} %copy-done.3), custom_call_target="tpu_custom_call" | custom-call | tf_op jit(solution)/shard_map/pallas_call | solution.py:367
  (10 shorter events, 0.1 us)
Async XLA Ops:
  58.5 5.0 %copy-start.1 = (bf16[8,8,2304]{2,1,0:T(8,128)(2,1)}, bf16[8,8,2304]{2,1,0:T(8,128)(2,1)S(1)}, u32[]{:S(2)}) copy-start(bf16[8,8,2304]{2,1,0:T(8,128)(2,1)S(1)} %all_to_all.41.rec_ref) | copy-start | bytes 884740
  58.5 5.0 %collective-permute-start = (bf16[8,8,1152]{2,1,0:T(8,128)(2,1)S(1)}, bf16[8,8,1152]{2,1,0:T(8,128)(2,1)S(1)}, u32[]{:S(2)}, u32[]{:S(2)}) collective-permute-start(bf16[8,8,1152]{2,1,0:T(8,128)(2,1)S(1)} %slice.8), channel_id=1, source_target_pairs={{0,8},{8,0},{16,24},{24,16},{32,40},{40,32},{48,56},{56,48},{64,72... | collective-permute-start | bytes 442376 | tf_op jit(solution)/shard_map/ppermute | solution.py:439
  63.4 0.7 copy-start.5
  72.6 4.0 %collective-permute-start.1 = (bf16[8,8,1024]{2,1,0:T(8,128)(2,1)}, bf16[8,8,1024]{2,1,0:T(8,128)(2,1)S(1)}, u32[]{:S(2)}, u32[]{:S(2)}) collective-permute-start(bf16[8,8,1024]{2,1,0:T(8,128)(2,1)} %get-tuple-element.25), channel_id=1, source_target_pairs={{0,8},{8,0},{16,24},{24,16},{32,40},{40,32},{48,56},{56,48},{64,72... | collective-permute-start | bytes 393224 | tf_op jit(solution)/shard_map/ppermute | solution.py:461
  89.1 17.3 %copy-start.2 = (bf16[8,8,2048]{2,1,0:T(8,128)(2,1)}, bf16[8,8,2048]{2,1,0:T(8,128)(2,1)S(1)}, u32[]{:S(2)}) copy-start(bf16[8,8,2048]{2,1,0:T(8,128)(2,1)S(1)} %all_to_all.42.left_ref) | copy-start | bytes 786436
  89.8 16.6 %all-to-all-start.3 = ((bf16[8,8,1024]{2,1,0:T(8,128)(2,1)}), bf16[8,8,1024]{2,1,0:T(8,128)(2,1)S(1)}, u32[]{:S(2)}, u32[]{:S(2)}) async-start(bf16[8,8,1024]{2,1,0:T(8,128)(2,1)} %slice.9), calls=%async_computation.3 | async-start | bytes 262144 | tf_op jit(solution)/shard_map/all_to_all | solution.py:378
  106.4 0.7 copy-start.4
  111.9 5.0 %collective-permute-start.2 = (bf16[4,672,128]{2,1,0:T(8,128)(2,1)}, bf16[4,672,128]{2,1,0:T(8,128)(2,1)S(1)}, u32[]{:S(2)}, u32[]{:S(2)}) collective-permute-start(bf16[4,672,128]{2,1,0:T(8,128)(2,1)} %get-tuple-element.30), channel_id=1, source_target_pairs={{0,1},{1,0},{2,3},{3,2},{4,5},{5,4},{6,7},{7,6},{8,9},{9,8},{10,11... | collective-permute-start | bytes 2064392 | tf_op jit(solution)/shard_map/ppermute | solution.py:484
  173.1 7.5 %copy-start = (bf16[8,336,128]{2,1,0:T(8,128)(2,1)}, bf16[8,336,128]{2,1,0:T(8,128)(2,1)S(1)}, u32[]{:S(2)}) copy-start(bf16[8,336,128]{2,1,0:T(8,128)(2,1)S(1)} %all_to_all.46) | copy-start | bytes 2064388
  173.1 7.4 %collective-permute-start.3 = (bf16[4,672,128]{2,1,0:T(8,128)(2,1)S(1)}, bf16[4,672,128]{2,1,0:T(8,128)(2,1)S(1)}, u32[]{:S(2)}, u32[]{:S(2)}) collective-permute-start(bf16[4,672,128]{2,1,0:T(8,128)(2,1)S(1)} %bitcast.16), channel_id=1, source_target_pairs={{0,1},{1,0},{2,3},{3,2},{4,5},{5,4},{6,7},{7,6},{8,9},{9,8},{10,11... | collective-permute-start | bytes 2064392 | tf_op jit(solution)/shard_map/ppermute | solution.py:494
  180.6 0.9 copy-start.3

commit v6 on v5

--- a/solution.py
+++ b/solution.py
@@ -437,6 +437,8 @@
         jnp.concatenate([right, left], axis=2), ("col", "sub")
     )
     other = lax.ppermute(records[:, :, :record], "row", swap_rows)
+    core = lax.axis_index("sub").reshape(1)
+    other, parity, core = lax.optimization_barrier((other, parity, core))
     pairs = lanes // col_res
     sets = factor // pairs
     back, send, result_adjoint = call(
@@ -461,7 +463,6 @@
     paired = jnp.pad(lax.ppermute(send, "row", swap_rows), ((0, 0), (0, 0), (0, wide)))
     back = exchanged((back.astype(f32) + paired.astype(f32)).astype(bf16), ("col", "sub"))
     right_back = exchanged(back[:, :, :wide], "row", alike)
-    core = lax.axis_index("sub").reshape(1)
     starts = chunk_rows(rows, features, units, factor, pair_width, shards)
     lines = -(-(starts[4] + 8) // (2 * row_devices)) * 2 * row_devices
     start_adjoint, own, send = call(

time: 185 us -> 183 us (0.989)
  blocking collectives: 120 us -> 136 us
  waiting for transfers between devices: 25.6 us -> 12.6 us
  starting transfers between devices: 12.5 us -> 8.85 us
    all_to_all x7 -> x8, blocking collectives: 120 us -> 136 us  [exchanged(): lax.all_to_all(parts, axis, split_axis=0, concat_axis=0, axis_index_group...]
    all_to_all x1 -> x0, waiting for transfers between devices: 13 us -> none  [exchanged(): lax.all_to_all(parts, axis, split_axis=0, concat_axis=0, axis_index_group...]
    all_to_all x1 -> x0, starting transfers between devices: 3.58 us -> none  [exchanged(): lax.all_to_all(parts, axis, split_axis=0, concat_axis=0, axis_index_group...]
  transfers between devices with their start and end apart: 5 -> 4, of which waited for: 5 -> 4; matrix products, arithmetic and copies ran while one was open for 0% -> 0% of each run, Pallas kernels for 0% -> 0%
where the time goes in v6:
time: 183 us
  blocking collectives  136 us (74%)
  Pallas kernels  19.5 us (11%)
  waiting for transfers between devices  12.6 us (7%)
  starting transfers between devices  8.85 us (5%)
  other arithmetic  3.38 us (2%)
    all_to_all x8, blocking collectives, exchanged(): lax.all_to_all(parts, axis, split_axis=0, concat_axis=0, axis_index_group...  136 us
    pallas_call x4, Pallas kernels, call(): pl.pallas_call(kernel, out_shape=[jax.ShapeDtypeStruct(s, d) for s, d in...  19.5 us
    ppermute x1, starting transfers between devices, per_device(): other = lax.ppermute(half, 'sub', swap)  5.68 us
    ppermute x1, waiting for transfers between devices, per_device(): other = lax.ppermute(records[:, :, :record], 'row', swap_rows)  4.8 us
    ppermute x1, waiting for transfers between devices, per_device(): lax.ppermute(send, 'row', swap_rows)  4.01 us
  transfers between devices with their start and end apart: 4, of which 4 were waited for; matrix products, arithmetic and copies ran while one was open for 0% of the time, Pallas kernels for 0%

profile of v6, /device:TPU:33, one launch (start us, length us, event | category | flops | bytes accessed | tf_op | source)
XLA Modules:
  0.0 182.8 jit_solution(5539211432799545257)
XLA Ops:
  0.6 3.3 %shard_map.162 = (f32[8,128]{1,0:T(8,128)}, bf16[8,8,1152]{2,1,0:T(8,128)(2,1)}, bf16[8,8,1152]{2,1,0:T(8,128)(2,1)}) custom-call(bf16[256,256]{1,0:T(8,128)(2,1)} %bitcast.19, s32[8,32]{1,0:T(8,128)} %present_ref.1, s32[1,32]{1,0:T(1,128)} %bitcast.30, f32[1,256]{1,0:T(1,128)} %bitcast.26, bf16[256,1024]{1,0:T(8,128)(2,1)} %w_in_ref.3, ...), custom_call_target="tpu_custom_call" | custom-call | tf_op jit(solution)/shard_map/pallas_call | solution.py:367
  3.9 38.4 %all_to_all.40 = bf16[8,8,1152]{2,1,0:T(8,128)(2,1)S(1)} all-to-all(bf16[8,8,1152]{2,1,0:T(8,128)(2,1)} %get-tuple-element.25), channel_id=1, replica_groups={{0,16,32,48,64,80,96,112},{8,24,40,56,72,88,104,120},{1,17,33,49,65,81,..., dimensions={0} | all-to-all | bytes 294912 | tf_op jit(solution)/shard_map/all_to_all | solution.py:378
  42.4 0.9 pad_maximum_fusion
  43.3 15.2 %all_to_all.41.rec_ref = bf16[8,8,2304]{2,1,0:T(8,128)(2,1)S(1)} all-to-all(bf16[8,8,2304]{2,1,0:T(8,128)(2,1)S(1)} %pad_maximum_fusion), channel_id=1, replica_groups=mesh['groups'=2,'row'=16,'col'=4,'sub'=2] {'col','sub'}, dimensions={0} | all-to-all | bytes 589824 | tf_op jit(solution)/shard_map/all_to_all | solution.py:378
  58.5 0.1 collective-permute-start
  58.6 4.8 %collective-permute-done.other_ref = bf16[8,8,1152]{2,1,0:T(8,128)(2,1)S(1)} collective-permute-done((bf16[8,8,1152]{2,1,0:T(8,128)(2,1)S(1)}, bf16[8,8,1152]{2,1,0:T(8,128)(2,1)S(1)}, u32[]{:S(2)}, u32[]{:S(2)}) %collective-permute-start) | collective-permute-done | bytes 147488 | tf_op jit(solution)/shard_map/ppermute | solution.py:439
  63.4 0.0 copy-start.4
  63.4 0.0 copy-done.1
  63.4 0.7 copy-done.4
  64.1 8.5 %shard_map.163 = (bf16[8,8,2048]{2,1,0:T(8,128)(2,1)}, bf16[8,8,1024]{2,1,0:T(8,128)(2,1)}, bf16[512,256]{1,0:T(8,128)(2,1)}) custom-call(s32[1]{0:T(128)} %bitcast.5.parity_ref, bf16[8,8,2304]{2,1,0:T(8,128)(2,1)} %copy-done.1, bf16[8,8,1152]{2,1,0:T(8,128)(2,1)} %copy-done.4, bf16[32,64,128]{2,1,0:T(8,128)(2,1)} %cot_ref.1, bf16[1024,128]{1,0:T(8,128)(2,1)} %proj_ref.1), custom_call_target="tpu_custom_call" | custom-call | tf_op jit(solution)/shard_map/pallas_call | solution.py:367
  72.6 0.0 collective-permute-start.1
  72.6 4.0 %collective-permute-done.1 = bf16[8,8,1024]{2,1,0:T(8,128)(2,1)S(1)} collective-permute-done((bf16[8,8,1024]{2,1,0:T(8,128)(2,1)}, bf16[8,8,1024]{2,1,0:T(8,128)(2,1)S(1)}, u32[]{:S(2)}, u32[]{:S(2)}) %collective-permute-start.1) | collective-permute-done | bytes 131104 | tf_op jit(solution)/shard_map/ppermute | solution.py:463
  76.6 1.0 add_convert_fusion.1
  77.6 11.5 %all_to_all.42.left_ref = bf16[8,8,2048]{2,1,0:T(8,128)(2,1)S(1)} all-to-all(bf16[8,8,2048]{2,1,0:T(8,128)(2,1)S(1)} %add_convert_fusion.1), channel_id=1, replica_groups=mesh['groups'=2,'row'=16,'col'=4,'sub'=2] {'col','sub'}, dimensions={0} | all-to-all | bytes 524288 | tf_op jit(solution)/shard_map/all_to_all | solution.py:378
  89.1 16.4 %all_to_all.43.right_ref = bf16[8,8,1024]{2,1,0:T(8,128)(2,1)} all-to-all(bf16[8,8,1024]{2,1,0:T(8,128)(2,1)S(1)} %slice.9), channel_id=1, replica_groups={{0,16,32,48,64,80,96,112},{8,24,40,56,72,88,104,120},{1,17,33,49,65,81,..., dimensions={0} | all-to-all | bytes 262144 | tf_op jit(solution)/shard_map/all_to_all | solution.py:378
  105.5 0.0 copy-done.2
  105.5 4.8 %shard_map.164 = (bf16[256,256]{1,0:T(8,128)(2,1)}, bf16[4,672,128]{2,1,0:T(8,128)(2,1)}, bf16[4,672,128]{2,1,0:T(8,128)(2,1)}) custom-call(s32[1]{0:T(128)} %bitcast.6.core_ref, bf16[8,8,2048]{2,1,0:T(8,128)(2,1)} %copy-done.2, bf16[8,8,1024]{2,1,0:T(8,128)(2,1)} %all_to_all.43.right_ref, f32[8,128]{1,0:T(8,128)} %get-tuple-element.32.keep_ref, ...), custom_call_target="tpu_custom_call" | custom-call | tf_op jit(solution)/shard_map/pallas_call | solution.py:367
  110.3 3.0 %collective-permute-start.2 = (bf16[4,672,128]{2,1,0:T(8,128)(2,1)}, bf16[4,672,128]{2,1,0:T(8,128)(2,1)S(1)}, u32[]{:S(2)}, u32[]{:S(2)}) collective-permute-start(bf16[4,672,128]{2,1,0:T(8,128)(2,1)} %get-tuple-element.36), channel_id=1, source_target_pairs={{0,1},{1,0},{2,3},{3,2},{4,5},{5,4},{6,7},{7,6},{8,9},{9,8},{10,11... | collective-permute-start | bytes 2064392 | tf_op jit(solution)/shard_map/ppermute | solution.py:485
  113.3 2.0 %collective-permute-done.2 = bf16[4,672,128]{2,1,0:T(8,128)(2,1)S(1)} collective-permute-done((bf16[4,672,128]{2,1,0:T(8,128)(2,1)}, bf16[4,672,128]{2,1,0:T(8,128)(2,1)S(1)}, u32[]{:S(2)}, u32[]{:S(2)}) %collective-permute-start.2) | collective-permute-done | bytes 688160 | tf_op jit(solution)/shard_map/ppermute | solution.py:485
  115.3 1.3 add_convert_fusion
  116.6 13.8 %all_to_all.44 = bf16[8,336,128]{2,1,0:T(8,128)(2,1)S(1)} all-to-all(bf16[8,336,128]{2,1,0:T(8,128)(2,1)S(1)} %bitcast.18), channel_id=1, replica_groups={{0,8,2,10,4,12,6,14},{16,24,18,26,20,28,22,30},{32,40,34,42,36,44,38,46..., dimensions={0} | all-to-all | bytes 1376256 | tf_op jit(solution)/shard_map/all_to_all | solution.py:378
  130.4 0.1 reduce_sum.24
  130.5 15.0 %all_to_all.45 = bf16[8,21,2,128]{3,2,1,0:T(2,128)(2,1)S(1)} all-to-all(bf16[8,21,2,128]{3,2,1,0:T(2,128)(2,1)S(1)} %bitcast.22), channel_id=1, replica_groups={{0,16,32,48,64,80,96,112},{8,24,40,56,72,88,104,120},{1,17,33,49,65,81,..., dimensions={0} | all-to-all | bytes 172032 | tf_op jit(solution)/shard_map/all_to_all | solution.py:378
  145.5 0.1 reduce_sum.25
  145.6 14.9 %all_to_all.46 = bf16[8,21,2,128]{3,2,1,0:T(2,128)(2,1)S(1)} all-to-all(bf16[8,21,2,128]{3,2,1,0:T(2,128)(2,1)S(1)} %broadcast_in_dim.6), channel_id=1, replica_groups={{0,16,32,48,64,80,96,112},{8,24,40,56,72,88,104,120},{1,17,33,49,65,81,..., dimensions={0} | all-to-all | bytes 172032 | tf_op jit(solution)/shard_map/all_to_all | solution.py:378
  160.5 0.1 broadcast_in_dim.7
  160.6 11.0 %all_to_all.47 = bf16[8,336,128]{2,1,0:T(8,128)(2,1)S(1)} all-to-all(bf16[8,336,128]{2,1,0:T(8,128)(2,1)S(1)} %broadcast_in_dim.7), channel_id=1, replica_groups={{0,8,2,10,4,12,6,14},{16,24,18,26,20,28,22,30},{32,40,34,42,36,44,38,46..., dimensions={0} | all-to-all | bytes 1376256 | tf_op jit(solution)/shard_map/all_to_all | solution.py:378
  171.6 5.7 %collective-permute-start.3 = (bf16[4,672,128]{2,1,0:T(8,128)(2,1)S(1)}, bf16[4,672,128]{2,1,0:T(8,128)(2,1)S(1)}, u32[]{:S(2)}, u32[]{:S(2)}) collective-permute-start(bf16[4,672,128]{2,1,0:T(8,128)(2,1)S(1)} %bitcast.16), channel_id=1, source_target_pairs={{0,1},{1,0},{2,3},{3,2},{4,5},{5,4},{6,7},{7,6},{8,9},{9,8},{10,11... | collective-permute-start | bytes 2064392 | tf_op jit(solution)/shard_map/ppermute | solution.py:495
  177.2 1.8 collective-permute-done.3.other_ref
  179.0 0.0 copy-done
  179.0 0.9 copy-done.3
  179.9 2.9 %shard_map.165 = (f32[1024,128]{1,0:T(8,128)}, f32[64,256]{1,0:T(8,128)}, f32[256,1024]{1,0:T(8,128)}, f32[1024,256]{1,0:T(8,128)}, f32[1,256]{1,0:T(1,128)}, /*index=5*/f32[1,256]{1,0:T(1,128)}) custom-call(s32[1]{0:T(128)} %bitcast.6.core_ref, bf16[4,672,128]{2,1,0:T(8,128)(2,1)} %bitcast.17, bf16[4,672,128]{2,1,0:T(8,128)(2,1)} %copy-done.3), custom_call_target="tpu_custom_call" | custom-call | tf_op jit(solution)/shard_map/pallas_call | solution.py:367
  (7 shorter events, 0.1 us)
Async XLA Ops:
  58.5 5.0 %copy-start.1 = (bf16[8,8,2304]{2,1,0:T(8,128)(2,1)}, bf16[8,8,2304]{2,1,0:T(8,128)(2,1)S(1)}, u32[]{:S(2)}) copy-start(bf16[8,8,2304]{2,1,0:T(8,128)(2,1)S(1)} %all_to_all.41.rec_ref) | copy-start | bytes 884740
  58.5 5.0 %collective-permute-start = (bf16[8,8,1152]{2,1,0:T(8,128)(2,1)S(1)}, bf16[8,8,1152]{2,1,0:T(8,128)(2,1)S(1)}, u32[]{:S(2)}, u32[]{:S(2)}) collective-permute-start(bf16[8,8,1152]{2,1,0:T(8,128)(2,1)S(1)} %slice.8), channel_id=1, source_target_pairs={{0,8},{8,0},{16,24},{24,16},{32,40},{40,32},{48,56},{56,48},{64,72... | collective-permute-start | bytes 442376 | tf_op jit(solution)/shard_map/ppermute | solution.py:439
  63.4 0.7 copy-start.4
  72.6 4.0 %collective-permute-start.1 = (bf16[8,8,1024]{2,1,0:T(8,128)(2,1)}, bf16[8,8,1024]{2,1,0:T(8,128)(2,1)S(1)}, u32[]{:S(2)}, u32[]{:S(2)}) collective-permute-start(bf16[8,8,1024]{2,1,0:T(8,128)(2,1)} %get-tuple-element.31), channel_id=1, source_target_pairs={{0,8},{8,0},{16,24},{24,16},{32,40},{40,32},{48,56},{56,48},{64,72... | collective-permute-start | bytes 393224 | tf_op jit(solution)/shard_map/ppermute | solution.py:463
  89.1 16.4 %copy-start.2 = (bf16[8,8,2048]{2,1,0:T(8,128)(2,1)}, bf16[8,8,2048]{2,1,0:T(8,128)(2,1)S(1)}, u32[]{:S(2)}) copy-start(bf16[8,8,2048]{2,1,0:T(8,128)(2,1)S(1)} %all_to_all.42.left_ref) | copy-start | bytes 786436
  110.3 5.0 %collective-permute-start.2 = (bf16[4,672,128]{2,1,0:T(8,128)(2,1)}, bf16[4,672,128]{2,1,0:T(8,128)(2,1)S(1)}, u32[]{:S(2)}, u32[]{:S(2)}) collective-permute-start(bf16[4,672,128]{2,1,0:T(8,128)(2,1)} %get-tuple-element.36), channel_id=1, source_target_pairs={{0,1},{1,0},{2,3},{3,2},{4,5},{5,4},{6,7},{7,6},{8,9},{9,8},{10,11... | collective-permute-start | bytes 2064392 | tf_op jit(solution)/shard_map/ppermute | solution.py:485
  171.5 7.5 %copy-start = (bf16[8,336,128]{2,1,0:T(8,128)(2,1)}, bf16[8,336,128]{2,1,0:T(8,128)(2,1)S(1)}, u32[]{:S(2)}) copy-start(bf16[8,336,128]{2,1,0:T(8,128)(2,1)S(1)} %all_to_all.47) | copy-start | bytes 2064388
  171.6 7.4 %collective-permute-start.3 = (bf16[4,672,128]{2,1,0:T(8,128)(2,1)S(1)}, bf16[4,672,128]{2,1,0:T(8,128)(2,1)S(1)}, u32[]{:S(2)}, u32[]{:S(2)}) collective-permute-start(bf16[4,672,128]{2,1,0:T(8,128)(2,1)S(1)} %bitcast.16), channel_id=1, source_target_pairs={{0,1},{1,0},{2,3},{3,2},{4,5},{5,4},{6,7},{7,6},{8,9},{9,8},{10,11... | collective-permute-start | bytes 2064392 | tf_op jit(solution)/shard_map/ppermute | solution.py:495
  179.0 0.9 copy-start.3
